TPU v7x, 256 devices: a whole 4x4x8 slice. The times are simulated.
256 devices in a mesh: gx: 4 (over x), gy: 4 (over y), gz: 16 (over z, core).
Axes of the slice: x: 4, y: 4, z: 8, core: 2. Of those that a mesh axis runs over, the one named last changes fastest.
Arguments:
- snapshots: bfloat16 [64, 3, 32, 128, 512], P(None, None, 'gy', 'gz', 'gx'), may hold values from -6 to 6
- modes: bfloat16 [128, 3, 32, 128, 512], P(None, None, 'gy', 'gz', 'gx'), may hold values from -0.0024414062 to 0.0024414062
Outputs:
- reduced_snapshots: float32 [128, 64], replicated
- reduced_features: float32 [128, 64], replicated
- gram_snap: float32 [128, 128], replicated
- gram_feature: float32 [128, 128], replicated
- gram_quad: float32 [64, 64], replicated
All inputs are finite; a program needn't handle non-finite values.
Results may differ from a plain program's by a relative error of at most 0.0029.
Values may be sent and summed in bfloat16 or wider, within the bound.
No kernel may reach another device: no remote copies, remote signals or barrier semaphores. Data moves between devices by JAX's collectives and lax.ppermute only.
A program may use at most 128 MiB of HBM per device.

v0:
```python
import jax
import jax.numpy as jnp
from jax import lax
from jax.sharding import Mesh
from jax.sharding import PartitionSpec as P

GZ = ("gz_0", "gz_1")


viscosity = 0.1


def padded_2(cells, sides, width, closed):
    for axis, dim in sides:
        count = lax.axis_size(axis)
        ends = count if closed else count - 1
        head = lax.slice_in_dim(cells, 0, width, axis=dim)
        tail = lax.slice_in_dim(cells, cells.shape[dim] - width, cells.shape[dim], axis=dim)
        cells = jnp.concatenate(
            [
                lax.ppermute(tail, axis, [(i, (i + 1) % count) for i in range(ends)]),
                cells,
                lax.ppermute(head, axis, [((i + 1) % count, i) for i in range(ends)]),
            ],
            axis=dim,
        )
    return cells


def sent_to_all(shard, axis):
    length = lax.axis_size(axis)
    return lax.all_to_all(
        jnp.broadcast_to(shard[None], (length, *shard.shape)), axis, 0, 0, tiled=True
    )


def taken_together(shard, axis):
    everything = sent_to_all(shard, axis)
    return jnp.sum(everything, axis=0)


def by_axis(shard, axes):
    far, near = axes
    nearer = taken_together(shard, near)
    return taken_together(nearer, far)


def stencil_terms(padded, direction, extent):
    pieces = [
        lax.slice_in_dim(padded, offset, offset + extent, axis=direction).astype(jnp.float32)
        for offset in range(5)
    ]
    gradient = (8.0 * (pieces[3] - pieces[1]) - (pieces[4] - pieces[0])) / 12.0
    curvature = (16.0 * (pieces[3] + pieces[1]) - (pieces[4] + pieces[0]) - 30.0 * pieces[2]) / 12.0
    return (gradient, curvature)


def feature_field(velocity, padded_list):
    advect = jnp.zeros(velocity.shape, jnp.float32)
    laplace = jnp.zeros(velocity.shape, jnp.float32)
    for padded, direction, component in padded_list:
        gradient, curvature = stencil_terms(padded, direction, velocity.shape[direction])
        advect = advect + velocity[:, component : component + 1] * gradient
        laplace = laplace + curvature
    return (viscosity * laplace - advect).astype(jnp.bfloat16)


def project(modes_flat, data_flat):
    return lax.dot_general(
        modes_flat, data_flat, (((1,), (1,)), ((), ())), preferred_element_type=jnp.float32
    )


def local_features(snapshots):
    padded_stream = padded_2(snapshots, (("gx", 4),), 2, True)
    padded_span = padded_2(snapshots, ((GZ, 3),), 2, True)
    padded_wall = padded_2(snapshots, (("gy", 2),), 2, False)
    velocity = snapshots.astype(jnp.float32)
    listed = ((padded_stream, 4, 0), (padded_wall, 2, 1), (padded_span, 3, 2))
    return feature_field(velocity, listed)


def shards(snapshots, modes):
    snap_count = snapshots.shape[0]
    mode_count = modes.shape[0]
    modes_flat = modes.reshape(mode_count, -1)
    snap_flat = snapshots.reshape(snap_count, -1)
    features = local_features(snapshots)
    feature_flat = features.reshape(snap_count, -1)
    stacked = jnp.concatenate([snap_flat, feature_flat], axis=0)
    combined = by_axis(project(modes_flat, stacked), (("gx", "gy"), ("gz_0", "gz_1")))
    reduced_snapshots = combined[:, :snap_count]
    reduced_features = combined[:, snap_count:]
    high = lax.Precision.HIGHEST
    gram_snap = (
        jnp.dot(
            reduced_snapshots,
            reduced_snapshots.T,
            precision=high,
            preferred_element_type=jnp.float32,
        )
        / snap_count
    )
    gram_feature = (
        jnp.dot(
            reduced_features,
            reduced_snapshots.T,
            precision=high,
            preferred_element_type=jnp.float32,
        )
        / snap_count
    )
    products = (
        jnp.dot(
            reduced_snapshots.T,
            reduced_snapshots,
            precision=high,
            preferred_element_type=jnp.float32,
        )
        / mode_count
    )
    gram_quad = products * products
    return (reduced_snapshots, reduced_features, gram_snap, gram_feature, gram_quad)


def solution(mesh):
    finer = Mesh(
        mesh.devices.reshape(mesh.shape["gx"], mesh.shape["gy"], 8, 2), ("gx", "gy", "gz_0", "gz_1")
    )
    placed = (P(None, None, "gy", GZ, "gx"), P(None, None, "gy", GZ, "gx"))
    return jax.shard_map(
        shards, mesh=finer, in_specs=placed, out_specs=(P(), P(), P(), P(), P()), check_vma=False
    )
```

profile of v0, /device:TPU:1, one launch (start us, length us, event | category | flops | bytes accessed | tf_op | source)
XLA Modules:
  0.0 161.7 jit_solution(7676061461131518729)
XLA Ops:
  0.6 0.0 copy-start
  0.6 3.0 %fusion.49 = (bf16[64,3,2,8,128]{4,3,2,1,0:T(8,128)(2,1)}, bf16[64,3,2,8,128]{4,3,2,1,0:T(8,128)(2,1)}) fusion(bf16[64,3,8,8,128]{4,3,2,1,0:T(8,128)(2,1)} %param.2), kind=kLoop, calls=%fused_computation.80 | loop fusion | bytes 3145728 | tf_op jit(solution)/shard_map/slice | solution.py:17
  3.6 4.9 %collective-permute-start.3 = (bf16[64,3,2,8,128]{4,3,2,1,0:T(8,128)(2,1)}, bf16[64,3,2,8,128]{4,3,2,1,0:T(8,128)(2,1)}, u32[]{:S(2)}, u32[]{:S(2)}) collective-permute-start(bf16[64,3,2,8,128]{4,3,2,1,0:T(8,128)(2,1)} %get-tuple-element.18), channel_id=1, source_target_pairs={{0,16},{16,32},{32,48},{1,17},{17,33},{33,49},{2,18},{18,34},{34,5... | collective-permute-start | bytes 2359304 | tf_op jit(solution)/shard_map/ppermute | solution.py:21
  8.5 0.0 copy-done
  8.5 4.3 %fusion.51 = (bf16[64,3,8,8,2]{4,3,2,1,0:T(8,128)(2,1)}, bf16[64,3,8,8,2]{4,3,2,1,0:T(8,128)(2,1)}) fusion(bf16[64,3,8,8,128]{4,3,2,1,0:T(8,128)(2,1)S(1)} %copy-done), kind=kLoop, calls=%fused_computation.82 | loop fusion | bytes 196608 | tf_op jit(solution)/shard_map/slice | solution.py:17
  12.8 4.8 %copy.28 = bf16[64,3,8,8,2]{0,3,4,2,1:T(8,128)(2,1)S(1)} copy(bf16[64,3,8,8,2]{4,3,2,1,0:T(8,128)(2,1)} %get-tuple-element.21) | data formatting | bytes 98304
  17.7 2.5 %collective-permute-start = (bf16[64,3,8,8,2]{0,3,4,2,1:T(8,128)(2,1)S(1)}, bf16[64,3,8,8,2]{0,3,4,2,1:T(8,128)(2,1)S(1)}, u32[]{:S(2)}, u32[]{:S(2)}) collective-permute-start(bf16[64,3,8,8,2]{0,3,4,2,1:T(8,128)(2,1)S(1)} %copy.28), channel_id=1, source_target_pairs={{64,0},{128,64},{192,128},{0,192},{65,1},{129,65},{193,129},{1,193... | collective-permute-start | bytes 147464 | tf_op jit(solution)/shard_map/ppermute | solution.py:23
  20.2 4.8 %copy.29 = bf16[64,3,8,8,2]{0,3,4,2,1:T(8,128)(2,1)S(1)} copy(bf16[64,3,8,8,2]{4,3,2,1,0:T(8,128)(2,1)} %get-tuple-element.22) | data formatting | bytes 98304
  25.1 0.1 collective-permute-start.1
  25.1 1.1 fusion.50
  26.2 1.0 copy.30
  27.2 1.2 collective-permute-start.4
  28.5 1.3 collective-permute-start.2
  29.7 1.0 copy.31
  30.7 3.8 %copy.45 = bf16[8,8,192,128]{3,1,2,0:T(8,128)(2,1)} copy(bf16[8,8,192,128]{3,2,1,0:T(8,128)(2,1)S(1)} %bitcast.25) | data formatting | bytes 6291456
  34.6 0.0 collective-permute-done
  34.6 1.5 collective-permute-start.5
  36.1 6.0 %copy.18 = bf16[64,3,8,8,2]{4,3,2,1,0:T(8,128)(2,1)} copy(bf16[64,3,8,8,2]{0,3,4,2,1:T(8,128)(2,1)S(1)} %collective-permute-done) | data formatting | bytes 98304 | tf_op jit(solution)/shard_map/ppermute | solution.py:23
  42.1 0.0 collective-permute-done.1
  42.1 6.0 %copy.20 = bf16[64,3,8,8,2]{4,3,2,1,0:T(8,128)(2,1)} copy(bf16[64,3,8,8,2]{0,3,4,2,1:T(8,128)(2,1)S(1)} %collective-permute-done.1) | data formatting | bytes 98304 | tf_op jit(solution)/shard_map/ppermute | solution.py:21
  48.1 0.0 collective-permute-done.3
  48.1 1.3 constant_dynamic-update-slice_fusion.3
  49.4 4.3 %fusion.48 = (f32[64,3,8,8,128]{4,3,2,1,0:T(8,128)S(1)}, bf16[64,3,10,8,128]{4,3,2,1,0:T(8,128)(2,1)S(1)}, bf16[64,3,10,8,128]{4,3,2,1,0:T(8,128)(2,1)S(1)}, bf16[64,3,8,10,128]{4,3,2,1,0:T(8,128)(2,1)}) fusion(bf16[64,3,8,8,128]{4,3,2,1,0:T(8,128)(2,1)S(1)} %copy-done, bf16[64,3,10,8,128]{4,3,2,1,0:T(8,128)(2,1)S(1)} %constant_dynamic-update-slice_fusion.3), kind=kLoop, calls=%fused_computation.79 | loop fusion | flops 1572862 | bytes 18874368 | tf_op jit(solution)/shard_map/convert_element_type | solution.py:50
  53.7 0.0 collective-permute-done.5
  53.7 2.8 %copy.24 = bf16[64,3,8,2,128]{4,3,2,1,0:T(2,128)(2,1)} copy(bf16[64,3,8,2,128]{4,2,3,1,0:T(8,128)(2,1)} %collective-permute-done.5) | data formatting | bytes 1572864 | tf_op jit(solution)/shard_map/ppermute | solution.py:21
  56.5 0.0 collective-permute-done.4
  56.5 2.9 %copy_dynamic-update-slice_fusion = bf16[64,3,8,10,128]{4,3,2,1,0:T(8,128)(2,1)} fusion(bf16[64,3,8,10,128]{4,3,2,1,0:T(8,128)(2,1)} %get-tuple-element.16, bf16[64,3,8,2,128]{4,2,3,1,0:T(8,128)(2,1)} %collective-permute-done.4), kind=kLoop, calls=%fused_computation.68 | loop fusion | bytes 1572864 | tf_op jit(solution)/shard_map/concatenate | solution.py:19
  59.4 2.8 %fusion.36 = (f32[64,8,8,128]{3,2,1,0:T(8,128)}, f32[64,8,8,128]{3,2,1,0:T(8,128)}, f32[64,8,8,128]{3,2,1,0:T(8,128)}) fusion(f32[64,3,8,8,128]{4,3,2,1,0:T(8,128)S(1)} %get-tuple-element.13), kind=kLoop, calls=%fused_computation.62 | loop fusion | flops 1572864 | bytes 12582912 | tf_op jit(solution)/shard_map/mul | solution.py:63
  62.3 0.0 collective-permute-done.2
  62.3 1.3 constant_dynamic-update-slice_fusion
  63.5 22.9 %fusion.7 = bf16[64,3,8,8,128]{4,3,2,1,0:T(8,128)(2,1)S(1)} fusion(bf16[64,3,8,2,128]{4,3,2,1,0:T(2,128)(2,1)} %copy.24, bf16[64,3,8,8,128]{4,3,2,1,0:T(8,128)(2,1)S(1)} %copy-done, bf16[64,3,8,8,2]{4,3,2,1,0:T(8,128)(2,1)} %copy.20, bf16[64,3,8,8,2]{4,3,2,1,0:T(8,128)(2,1)} %copy.18, bf16[64,3,8,10,128]{4,3,2,1,0:T(8,128)(2,1)} %copy_dynamic-update-slice_fusion, ...), kind=kLoop, calls=%fused_computation.19 | loop fusion | flops 108527616 | bytes 32342016 | tf_op jit(solution)/shard_map/convert_element_type | solution.py:65
  86.5 0.0 copy-start.1
  86.5 2.0 %copy.44 = bf16[8,8,192,128]{3,1,2,0:T(8,128)(2,1)S(1)} copy(bf16[8,8,192,128]{3,2,1,0:T(8,128)(2,1)S(1)} %bitcast.26) | data formatting | bytes 6291456
  88.5 0.0 copy-done.1
  88.5 8.1 %fusion.37 = f32[128,128]{0,1:T(8,128)S(1)} fusion(bf16[16,8,192,128]{3,2,1,0:T(8,128)(2,1)} %bitcast.29, bf16[64,24576]{1,0:T(8,128)(2,1)S(1)} %bitcast.28, bf16[64,24576]{1,0:T(8,128)(2,1)S(1)} %bitcast.27), kind=kOutput, calls=%fused_computation.63 | convolution fusion | flops 817889280 | bytes 12648448 | tf_op jit(solution)/shard_map/dot_general | solution.py:69
  96.6 0.1 copy.25
  96.7 0.1 broadcast_in_dim.4
  96.8 35.9 %all_to_all.10 = f32[16,128,128]{2,1,0:T(8,128)S(1)} all-to-all(f32[16,128,128]{2,1,0:T(8,128)S(1)} %broadcast_in_dim.4), channel_id=1, replica_groups=mesh['gx'=4,'gy'=4,'gz_0'=8,'gz_1'=2] {'gz_0','gz_1'}, dimensions={0} | all-to-all | bytes 2097152 | tf_op jit(solution)/shard_map/all_to_all | solution.py:32
  132.7 0.1 reduce_sum.18
  132.8 0.1 broadcast_in_dim.5
  132.9 24.6 %all_to_all.11 = f32[16,128,128]{2,1,0:T(8,128)S(1)} all-to-all(f32[16,128,128]{2,1,0:T(8,128)S(1)} %broadcast_in_dim.5), channel_id=1, replica_groups=mesh['gx'=4,'gy'=4,'gz_0'=8,'gz_1'=2] {'gx','gy'}, dimensions={0} | all-to-all | bytes 2097152 | tf_op jit(solution)/shard_map/all_to_all | solution.py:32
  157.5 0.1 reduce_sum.19
  157.5 0.1 fusion.52
  157.6 0.9 convolution_multiply_fusion
  158.6 0.9 convolution_multiply_fusion.1
  159.5 0.9 fusion.42
  160.4 0.7 copy.26
  161.1 0.7 copy.27
Async XLA Ops:
  0.6 7.9 %copy-start = (bf16[64,3,8,8,128]{4,3,2,1,0:T(8,128)(2,1)S(1)}, bf16[64,3,8,8,128]{4,3,2,1,0:T(8,128)(2,1)}, u32[]{:S(2)}) copy-start(bf16[64,3,8,8,128]{4,3,2,1,0:T(8,128)(2,1)} %param.2) | copy-start | bytes 9437188
  3.6 44.5 %collective-permute-start.3 = (bf16[64,3,2,8,128]{4,3,2,1,0:T(8,128)(2,1)}, bf16[64,3,2,8,128]{4,3,2,1,0:T(8,128)(2,1)}, u32[]{:S(2)}, u32[]{:S(2)}) collective-permute-start(bf16[64,3,2,8,128]{4,3,2,1,0:T(8,128)(2,1)} %get-tuple-element.18), channel_id=1, source_target_pairs={{0,16},{16,32},{32,48},{1,17},{17,33},{33,49},{2,18},{18,34},{34,5... | collective-permute-start | bytes 2359304 | tf_op jit(solution)/shard_map/ppermute | solution.py:21
  17.7 16.9 %collective-permute-start = (bf16[64,3,8,8,2]{0,3,4,2,1:T(8,128)(2,1)S(1)}, bf16[64,3,8,8,2]{0,3,4,2,1:T(8,128)(2,1)S(1)}, u32[]{:S(2)}, u32[]{:S(2)}) collective-permute-start(bf16[64,3,8,8,2]{0,3,4,2,1:T(8,128)(2,1)S(1)} %copy.28), channel_id=1, source_target_pairs={{64,0},{128,64},{192,128},{0,192},{65,1},{129,65},{193,129},{1,193... | collective-permute-start | bytes 147464 | tf_op jit(solution)/shard_map/ppermute | solution.py:23
  25.1 17.0 %collective-permute-start.1 = (bf16[64,3,8,8,2]{0,3,4,2,1:T(8,128)(2,1)S(1)}, bf16[64,3,8,8,2]{0,3,4,2,1:T(8,128)(2,1)S(1)}, u32[]{:S(2)}, u32[]{:S(2)}) collective-permute-start(bf16[64,3,8,8,2]{0,3,4,2,1:T(8,128)(2,1)S(1)} %copy.29), channel_id=1, source_target_pairs={{0,64},{64,128},{128,192},{192,0},{1,65},{65,129},{129,193},{193,1... | collective-permute-start | bytes 147464 | tf_op jit(solution)/shard_map/ppermute | solution.py:21
  27.2 29.3 %collective-permute-start.4 = (bf16[64,3,8,2,128]{4,2,3,1,0:T(8,128)(2,1)}, bf16[64,3,8,2,128]{4,2,3,1,0:T(8,128)(2,1)}, u32[]{:S(2)}, u32[]{:S(2)}) collective-permute-start(bf16[64,3,8,2,128]{4,2,3,1,0:T(8,128)(2,1)} %copy.30), channel_id=1, source_target_pairs={{1,0},{2,1},{3,2},{4,3},{5,4},{6,5},{7,6},{8,7},{9,8},{10,9},{11,1... | collective-permute-start | bytes 2359304 | tf_op jit(solution)/shard_map/ppermute | solution.py:23
  28.5 33.8 %collective-permute-start.2 = (bf16[64,3,2,8,128]{4,3,2,1,0:T(8,128)(2,1)}, bf16[64,3,2,8,128]{4,3,2,1,0:T(8,128)(2,1)}, u32[]{:S(2)}, u32[]{:S(2)}) collective-permute-start(bf16[64,3,2,8,128]{4,3,2,1,0:T(8,128)(2,1)} %get-tuple-element.17), channel_id=1, source_target_pairs={{16,0},{32,16},{48,32},{17,1},{33,17},{49,33},{18,2},{34,18},{50,3... | collective-permute-start | bytes 2359304 | tf_op jit(solution)/shard_map/ppermute | solution.py:23
  34.6 19.1 %collective-permute-start.5 = (bf16[64,3,8,2,128]{4,2,3,1,0:T(8,128)(2,1)}, bf16[64,3,8,2,128]{4,2,3,1,0:T(8,128)(2,1)}, u32[]{:S(2)}, u32[]{:S(2)}) collective-permute-start(bf16[64,3,8,2,128]{4,2,3,1,0:T(8,128)(2,1)} %copy.31), channel_id=1, source_target_pairs={{0,1},{1,2},{2,3},{3,4},{4,5},{5,6},{6,7},{7,8},{8,9},{9,10},{10,1... | collective-permute-start | bytes 2359304 | tf_op jit(solution)/shard_map/ppermute | solution.py:21
  86.5 2.1 %copy-start.1 = (bf16[8,8,192,128]{3,1,2,0:T(8,128)(2,1)S(1)}, bf16[8,8,192,128]{3,1,2,0:T(8,128)(2,1)}, u32[]{:S(2)}) copy-start(bf16[8,8,192,128]{3,1,2,0:T(8,128)(2,1)} %copy.45) | copy-start | bytes 9437188
where the time goes:
time: 162 us
  blocking collectives  60.5 us (37%)
  local copies, waits for them, and re-layouts  47.9 us (30%)
  other arithmetic  30.2 us (19%)
  starting transfers between devices  11.5 us (7%)
  matrix products  10.8 us (7%)
    all_to_all x2, blocking collectives, sent_to_all(): lax.all_to_all(jnp.broadcast_to(shard[None], (length, *shard.shape)), axi...  60.5 us
    convert_element_type x1, other arithmetic, feature_field(): return (viscosity * laplace - advect).astype(jnp.bfloat16)  22.9 us
    unnamed x13, local copies, waits for them, and re-layouts  20.2 us
    ppermute x2, local copies, waits for them, and re-layouts, padded_2(): lax.ppermute(tail, axis, [(i, (i + 1) % count) for i in range(ends)])  8.81 us
    slice x3, local copies, waits for them, and re-layouts, padded_2(): head = lax.slice_in_dim(cells, 0, width, axis=dim)  8.36 us
    dot_general x1, matrix products, project(): lax.dot_general(modes_flat, data_flat, (((1,), (1,)), ((), ())), preferre...  8.07 us
    ppermute x3, starting transfers between devices, padded_2(): lax.ppermute(tail, axis, [(i, (i + 1) % count) for i in range(ends)])  6.49 us
    ppermute x1, local copies, waits for them, and re-layouts, padded_2(): lax.ppermute(head, axis, [((i + 1) % count, i) for i in range(ends)])  5.98 us
  transfers between devices with their start and end apart: 6, of which 0 were waited for; matrix products, arithmetic and copies ran while one was open for 29% of the time, Pallas kernels for 0%

commit v1 on v0

v1 whole, which is shorter than its diff:
```python
import functools

import jax
import jax.numpy as jnp
import numpy as np
from jax import lax
from jax.experimental import pallas as pl
from jax.experimental.pallas import tpu as pltpu
from jax.sharding import Mesh
from jax.sharding import PartitionSpec as P


GZ = ("gz_0", "gz_1")
BF16 = jnp.bfloat16
F32 = jnp.float32
VISCOSITY = 0.1
HIGH = lax.Precision.HIGHEST
NT = (((1,), (1,)), ((), ()))
TN = (((0,), (0,)), ((), ()))

GRAD = {-2: 1.0, -1: -8.0, 1: 8.0, 2: -1.0}
CURV = {-2: -1.0, -1: 16.0, 0: -30.0, 1: 16.0, 2: -1.0}


def plane_operator():
    op = np.zeros((192, 128), np.float32)

    def column(y, z):
        if y < 0:
            return 64 + (y + 2) * 8 + z
        if y > 7:
            return 80 + (y - 8) * 8 + z
        if z < 0:
            return 96 + y * 2 + z + 2
        if z > 7:
            return 112 + y * 2 + z - 8
        return y * 8 + z

    for y in range(8):
        for z in range(8):
            row = y * 8 + z
            for k, value in CURV.items():
                op[row, column(y + k, z)] += value
                op[row, column(y, z + k)] += value
            for k, value in GRAD.items():
                op[64 + row, column(y + k, z)] += value
                op[128 + row, column(y, z + k)] += value
    return op


def stream_operator():
    op = np.zeros((256, 256), np.float32)
    for part, taps in enumerate((GRAD, CURV)):
        for x in range(128):
            for k, value in taps.items():
                at = x + k
                if 0 <= at < 128:
                    op[at, part * 128 + x] += value
                else:
                    halo = at + 2 if at < 0 else at - 128 + 2
                    for j in range(32):
                        op[128 + 4 * j + halo, part * 128 + x] += value
    return op


def lane_masks():
    m, row, lane = np.meshgrid(np.arange(8), np.arange(64), np.arange(128), indexing="ij")
    return (lane // 4 == 4 * m + row // 16).astype(np.float32)


def lane_pick():
    op = np.zeros((128, 256), np.float32)
    for j in range(32):
        op[126, 4 * j] = op[127, 4 * j + 1] = 1
        op[0, 128 + 4 * j + 2] = op[1, 128 + 4 * j + 3] = 1
    return op


def span_pick():
    op = np.zeros((32, 64), np.float32)
    for y in range(8):
        for k in range(2):
            op[2 * y + k, 8 * y + k] = 1
            op[16 + 2 * y + k, 8 * y + 6 + k] = 1
    return op


def in_vmem(array):
    return pltpu.with_memory_space_constraint(array, pltpu.VMEM)


def any_space():
    return pl.BlockSpec(memory_space=pl.ANY)


def wall_pack(snap, first, count):
    def body(snap, low, high, sems):
        one = pltpu.make_async_copy(snap.at[pl.ds(first, count), pl.ds(0, 16)], low, sems.at[0])
        two = pltpu.make_async_copy(snap.at[pl.ds(first, count), pl.ds(48, 16)], high, sems.at[1])
        one.start()
        two.start()
        one.wait()
        two.wait()

    shape = pltpu.VMEM((count, 16, 128), BF16)
    vmem = pl.BlockSpec(memory_space=pltpu.VMEM)
    return pl.pallas_call(
        body,
        out_shape=(shape, shape),
        in_specs=[any_space()],
        out_specs=(vmem, vmem),
        scratch_shapes=[pltpu.SemaphoreType.DMA((2,))],
        name="wall_pack",
    )(snap)


def side_pack_body(snap, span, lanes, masks, low, high, right, left):
    for group in range(right.shape[0]):
        to_right = jnp.zeros((16, 128), F32)
        to_left = jnp.zeros((16, 128), F32)
        for pair in range(4):
            a = snap[8 * group + 2 * pair]
            b = snap[8 * group + 2 * pair + 1]
            picked = jnp.dot(span[...], jnp.concatenate([a, b], axis=1), preferred_element_type=F32).astype(BF16)
            for i in range(2):
                unit = 8 * group + 2 * pair + i
                low[unit] = picked[:16, 128 * i : 128 * (i + 1)]
                high[unit] = picked[16:, 128 * i : 128 * (i + 1)]
            ends = jnp.dot(jnp.concatenate([a, b], axis=0), lanes[...], preferred_element_type=F32)
            for i in range(2):
                for q in range(4):
                    rows = slice(64 * i + 16 * q, 64 * i + 16 * q + 16)
                    mask = masks[2 * pair + i, 16 * q : 16 * q + 16].astype(F32)
                    to_right += ends[rows, :128] * mask
                    to_left += ends[rows, 128:] * mask
        right[group] = to_right.astype(BF16)
        left[group] = to_left.astype(BF16)


def side_pack(snap, steps=4):
    units = snap.shape[0]
    n, g = units // steps, units // 8 // steps
    whole = lambda *shape: pl.BlockSpec(shape, lambda i: (0,) * len(shape))
    return pl.pallas_call(
        side_pack_body,
        grid=(steps,),
        out_shape=(
            jax.ShapeDtypeStruct((units, 16, 128), BF16),
            jax.ShapeDtypeStruct((units, 16, 128), BF16),
            jax.ShapeDtypeStruct((units // 8, 16, 128), BF16),
            jax.ShapeDtypeStruct((units // 8, 16, 128), BF16),
        ),
        in_specs=[
            pl.BlockSpec((n, 64, 128), lambda i: (i, 0, 0)),
            whole(32, 64),
            whole(128, 256),
            whole(8, 64, 128),
        ],
        out_specs=(
            pl.BlockSpec((n, 16, 128), lambda i: (i, 0, 0)),
            pl.BlockSpec((n, 16, 128), lambda i: (i, 0, 0)),
            pl.BlockSpec((g, 16, 128), lambda i: (i, 0, 0)),
            pl.BlockSpec((g, 16, 128), lambda i: (i, 0, 0)),
        ),
        name="side_pack",
    )(snap, jnp.asarray(span_pick(), BF16), jnp.asarray(lane_pick(), BF16), jnp.asarray(lane_masks(), BF16))


def same_span(total, count):
    rows = lax.broadcasted_iota(jnp.int32, total.shape, 0) % 8
    lanes = lax.broadcasted_iota(jnp.int32, total.shape, 1)
    kept = jnp.where(rows == lanes % 8, total, 0.0).reshape(128, 8, 8 * count).sum(axis=1)
    s = lax.broadcasted_iota(jnp.int32, (count, 8 * count), 0)
    at = lax.broadcasted_iota(jnp.int32, (count, 8 * count), 1)
    group = (at // 8 == s).astype(F32)
    return lax.dot_general(group, kept, NT, precision=HIGH, preferred_element_type=F32)


def project(modes, data, total):
    for k in range(12):
        a = jnp.concatenate([modes[2 * k].reshape(1024, 128), modes[2 * k + 1].reshape(1024, 128)], axis=1)
        b = jnp.concatenate([data[2 * k], data[2 * k + 1]], axis=1)
        part = lax.dot_general(a, b, NT, preferred_element_type=F32)
        if k == 0:
            total[...] = part
        else:
            total[...] += part


def snap_project_body(modes, snap, out, modes_in, snap_in, total, sems):
    copies = []
    for k in range(24):
        copies.append(pltpu.make_async_copy(modes.at[:, k], modes_in.at[k], sems.at[0, k]))
        copies.append(pltpu.make_async_copy(snap.at[:, k], snap_in.at[k], sems.at[1, k]))
    for c in copies:
        c.start()
    for c in copies:
        c.wait()

    class Rows:
        def __getitem__(self, k):
            return snap_in[k].reshape(512, 128)

    project(modes_in, Rows(), total)
    out[...] = same_span(total[...], 64)


def snap_project(modes, snap):
    return pl.pallas_call(
        snap_project_body,
        out_shape=jax.ShapeDtypeStruct((64, 128), F32),
        in_specs=[any_space(), any_space()],
        out_specs=pl.BlockSpec(memory_space=pltpu.VMEM),
        scratch_shapes=[
            pltpu.VMEM((24, 128, 8, 128), BF16),
            pltpu.VMEM((24, 64, 8, 128), BF16),
            pltpu.VMEM((1024, 512), F32),
            pltpu.SemaphoreType.DMA((2, 24)),
        ],
        name="snap_project",
    )(modes, snap)


def feature_body(
    first, modes, snap, y_low, y_high, z_low, z_high, x_low, x_high, plane, stream, masks, out, modes_in, field, total, sems
):
    step = pl.program_id(0)
    steps = pl.num_programs(0)
    copies = [pltpu.make_async_copy(modes.at[:, k], modes_in.at[k], sems.at[k]) for k in range(24)]

    @pl.when(step == 0)
    def _():
        for c in copies:
            c.start()

    count = snap.shape[0] // 3
    near = step * (3 * count)
    far = near + 3 * first
    x_at = pl.ds(far // 8, 3 * count // 8)
    x_halo = x_low[x_at] + x_high[x_at]
    for pair in range(count // 2):
        units = [[3 * (2 * pair + i) + c for c in range(3)] for i in range(2)]
        cells = [[snap[u] for u in row] for row in units]
        velocity = [[v.astype(F32) * (1.0 / 12.0) for v in row] for row in cells]
        along = []
        for i in range(2):
            inside = jnp.concatenate(cells[i], axis=0)
            beside = jnp.concatenate(
                [jnp.concatenate([x_halo[u // 8]] * 4, axis=0) * masks[u % 8] for u in units[i]], axis=0
            )
            along.append(
                jnp.dot(jnp.concatenate([inside, beside], axis=1), stream[...], preferred_element_type=F32)
            )
        for c in range(3):
            padded = [
                jnp.concatenate(
                    [cells[i][c], y_low[near + u], y_high[near + u], z_low[far + u], z_high[far + u]], axis=0
                )
                for i, u in ((0, units[0][c]), (1, units[1][c]))
            ]
            across = jnp.dot(plane[...], jnp.concatenate(padded, axis=1), preferred_element_type=F32)
            both = []
            for i in range(2):
                lanes = slice(128 * i, 128 * (i + 1))
                rows = slice(64 * c, 64 * (c + 1))
                laplace = across[0:64, lanes] + along[i][rows, 128:256]
                advect = (
                    velocity[i][0] * along[i][rows, 0:128]
                    + velocity[i][1] * across[64:128, lanes]
                    + velocity[i][2] * across[128:192, lanes]
                )
                both.append((laplace * (VISCOSITY / 12.0) - advect).reshape(8, 8, 128))
            stacked = jnp.concatenate(both, axis=1).astype(BF16)
            start = pl.multiple_of((step * count + 2 * pair) * 8, 16)
            field[8 * c : 8 * c + 8, pl.ds(start, 16), :] = stacked

    @pl.when(step == steps - 1)
    def _():
        for c in copies:
            c.wait()
        project(modes_in, field, total)
        out[...] = same_span(total[...], out.shape[0])


def feature_project(modes, snap, y_low, y_high, z_low, z_high, x_low, x_high, first, count, steps=4):
    n = 3 * count // steps
    off = 3 * first // n
    there = lambda *shape: pl.BlockSpec(shape, lambda i: (i + off,) + (0,) * (len(shape) - 1))
    whole = lambda *shape: pl.BlockSpec(shape, lambda i: (0,) * len(shape))
    resident = pl.BlockSpec(memory_space=pltpu.VMEM)
    return pl.pallas_call(
        functools.partial(feature_body, first),
        grid=(steps,),
        out_shape=jax.ShapeDtypeStruct((count, 128), F32),
        in_specs=[
            any_space(),
            there(n, 64, 128),
            resident,
            resident,
            resident,
            resident,
            resident,
            resident,
            whole(192, 128),
            whole(256, 256),
            whole(8, 64, 128),
        ],
        out_specs=whole(count, 128),
        scratch_shapes=[
            pltpu.VMEM((24, 128, 8, 128), BF16),
            pltpu.VMEM((24, 8 * count, 128), BF16),
            pltpu.VMEM((1024, 8 * count), F32),
            pltpu.SemaphoreType.DMA((24,)),
        ],
        name="feature_project",
    )(
        modes,
        snap,
        *map(in_vmem, (y_low, y_high, z_low, z_high, x_low, x_high)),
        jnp.asarray(plane_operator(), BF16),
        jnp.asarray(stream_operator(), BF16),
        jnp.asarray(lane_masks(), BF16),
    )


def gram_body(core, mine, other, snap_out, feature_out, gram_snap, gram_feature, gram_quad):
    first = core[0] == 0
    rs = jnp.where(first, mine[...], other[...])
    rf = jnp.where(first, other[...], mine[...])
    snap_out[...] = rs
    feature_out[...] = rf
    dot = functools.partial(lax.dot_general, precision=HIGH, preferred_element_type=F32)
    gram_snap[...] = dot(rs, rs, TN) * (1.0 / 64)
    gram_feature[...] = dot(rf, rs, TN) * (1.0 / 64)
    products = dot(rs, rs, NT) * (1.0 / 128)
    gram_quad[...] = products * products


def grams(core, mine, other):
    shape = lambda *s: jax.ShapeDtypeStruct(s, F32)
    vmem = pl.BlockSpec(memory_space=pltpu.VMEM)
    return pl.pallas_call(
        gram_body,
        in_specs=[pl.BlockSpec(memory_space=pltpu.SMEM), vmem, vmem],
        out_shape=(shape(64, 128), shape(64, 128), shape(128, 128), shape(128, 128), shape(64, 64)),
        name="grams",
    )(core, in_vmem(mine), in_vmem(other))


def shifted(value, axis, count, by, closed):
    pairs = [(i, (i + by) % count) for i in range(count) if closed or 0 <= i + by < count]
    return lax.ppermute(value, axis, pairs)


def swapped(value, axis, partners):
    return lax.ppermute(value, axis, list(enumerate(partners)))


ROUNDS = (
    ("gx", (1, 0, 3, 2)),
    ("gx", (3, 2, 1, 0)),
    ("gy", (1, 0, 3, 2)),
    ("gy", (3, 2, 1, 0)),
    ("gz_0", (1, 0, 3, 2, 5, 4, 7, 6)),
    ("gz_0", (2, 3, 0, 1, 6, 7, 4, 5)),
    ("gz_0", (6, 7, 4, 5, 2, 3, 0, 1)),
)
CHUNKS = ((0, 32), (32, 32))


def shards(snapshots, modes):
    units = snapshots.reshape(192, 64, 128)
    modes = modes.reshape(128, 24, 8, 128)
    walls = []
    for first, count in CHUNKS:
        low, high = wall_pack(units, 3 * first, 3 * count)
        up = shifted(high, "gy", 4, 1, False)
        down = shifted(low, "gy", 4, -1, False)
        walls.append((up, down))
    low, high, right, left = side_pack(units)
    z_low = shifted(high, GZ, 16, 1, True)
    z_high = shifted(low, GZ, 16, -1, True)
    x_low = shifted(right, "gx", 4, 1, True)
    x_high = shifted(left, "gx", 4, -1, True)
    parts = [snap_project(modes, snapshots.reshape(64, 24, 8, 128))]
    for (first, count), (y_low, y_high) in zip(CHUNKS, walls):
        parts.append(
            feature_project(modes, units, y_low, y_high, z_low, z_high, x_low, x_high, first, count)
        )
    core = lax.axis_index("gz_1")
    snap_part, feature_part = parts[0], jnp.concatenate(parts[1:], axis=0)
    mine = jnp.where(core == 0, snap_part, feature_part)
    total = mine + swapped(jnp.where(core == 0, feature_part, snap_part), "gz_1", (1, 0))
    for axis, partners in ROUNDS:
        total = total + swapped(total, axis, partners)
    rs, rf, gram_snap, gram_feature, gram_quad = grams(
        core.reshape(1).astype(jnp.int32), total, swapped(total, "gz_1", (1, 0))
    )
    return rs.T, rf.T, gram_snap, gram_feature, gram_quad


def solution(mesh):
    finer = Mesh(
        mesh.devices.reshape(mesh.shape["gx"], mesh.shape["gy"], 8, 2), ("gx", "gy", "gz_0", "gz_1")
    )
    placed = (P(None, None, "gy", GZ, "gx"), P(None, None, "gy", GZ, "gx"))

    return jax.shard_map(shards, mesh=finer, in_specs=placed, out_specs=(P(), P(), P(), P(), P()), check_vma=False)
```

time: 162 us -> 101 us (0.62)
  blocking collectives: 60.5 us -> 0 us
  local copies, waits for them, and re-layouts: 47.9 us -> 0.75 us
  Pallas kernels: 0 us -> 38.1 us
  other arithmetic: 30.2 us -> 1.49 us
  starting transfers between devices: 11.5 us -> 38.7 us
  waiting for transfers between devices: 0.02 us -> 20.6 us
  matrix products: 10.8 us -> 0 us
    all_to_all x2 -> x0, blocking collectives: 60.5 us -> none  [sent_to_all(): lax.all_to_all(jnp.broadcast_to(shard[None], (length, *shard.shape)), axi...]
    pallas_call x0 -> x7, Pallas kernels: none -> 38.1 us  [the longest x2 18.6 us: feature_project(): pl.pallas_call(functools.partial(feature_body, first), grid=(steps,), out...]
    convert_element_type x2 -> x0, other arithmetic: 27.3 us -> none  [the longest x1 22.9 us: feature_field(): return (viscosity * laplace - advect).astype(jnp.bfloat16)]
    ppermute x6 -> x17, starting transfers between devices: 11.5 us -> 38.7 us  [the longest x9 23.2 us: swapped(): return lax.ppermute(value, axis, list(enumerate(partners)))]
    ppermute x6 -> x17, waiting for transfers between devices: 0.02 us -> 20.6 us  [the longest x9 18.1 us: swapped(): return lax.ppermute(value, axis, list(enumerate(partners)))]
    unnamed x13 -> x6, local copies, waits for them, and re-layouts: 20.2 us -> 0.75 us
    ppermute x3 -> x0, local copies, waits for them, and re-layouts: 14.8 us -> none  [the longest x2 8.81 us: padded_2(): lax.ppermute(tail, axis, [(i, (i + 1) % count) for i in range(ends)])]
    dot_general x4 -> x0, matrix products: 10.8 us -> none  [the longest x1 8.07 us: project(): lax.dot_general(modes_flat, data_flat, (((1,), (1,)), ((), ())), preferre...]
  transfers between devices with their start and end apart: 6 -> 17, of which waited for: 0 -> 10; matrix products, arithmetic and copies ran while one was open for 29% -> 0% of each run, Pallas kernels for 0% -> 22%
where the time goes in v1:
time: 101 us; the launch traced here: 100 us
  starting transfers between devices  38.7 us (38%)
  Pallas kernels  38.1 us (38%)
  waiting for transfers between devices  20.6 us (20%)
  other arithmetic  1.49 us (1%)
    ppermute x9, starting transfers between devices, swapped(): return lax.ppermute(value, axis, list(enumerate(partners)))  23.2 us
    pallas_call x2, Pallas kernels, feature_project(): pl.pallas_call(functools.partial(feature_body, first), grid=(steps,), out...  18.6 us
    ppermute x9, waiting for transfers between devices, swapped(): return lax.ppermute(value, axis, list(enumerate(partners)))  18.1 us
    ppermute x8, starting transfers between devices, shifted(): return lax.ppermute(value, axis, pairs)  15.6 us
    pallas_call x1, Pallas kernels, snap_project(): pl.pallas_call(snap_project_body, out_shape=jax.ShapeDtypeStruct((64, 128...  9.07 us
    pallas_call x1, Pallas kernels, side_pack(): pl.pallas_call(side_pack_body, grid=(steps,), out_shape=(jax.ShapeDtypeSt...  5.48 us
    pallas_call x2, Pallas kernels, wall_pack(): pl.pallas_call(body, out_shape=(shape, shape), in_specs=[any_space()], ou...  3.95 us
    ppermute x8, waiting for transfers between devices, shifted(): return lax.ppermute(value, axis, pairs)  2.52 us
  transfers between devices with their start and end apart: 17, of which 10 were waited for; matrix products, arithmetic and copies ran while one was open for 0% of the time, Pallas kernels for 22%

profile of v1, /device:TPU:1, one launch (start us, length us, event | category | flops | bytes accessed | tf_op | source)
XLA Modules:
  0.0 100.4 jit_solution(16795718315497158390)
XLA Ops:
  0.6 5.5 %side_pack.1 = (bf16[192,16,128]{2,1,0:T(8,128)(2,1)}, bf16[192,16,128]{2,1,0:T(8,128)(2,1)}, bf16[24,16,128]{2,1,0:T(8,128)(2,1)}, bf16[24,16,128]{2,1,0:T(8,128)(2,1)}) custom-call(bf16[192,64,128]{2,1,0:T(8,128)(2,1)} %bitcast.6, bf16[32,64]{1,0:T(8,128)(2,1)} %constant.16.clone.span, bf16[128,256]{1,0:T(8,128)(2,1)} %constant.17.clone.lanes, ...), custom_call_target="tpu_custom_call" | custom-call | tf_op jit(solution)/shard_map/side_pack/pallas_call | solution.py:144
  6.1 3.0 %collective-permute-start.2 = (bf16[192,16,128]{2,1,0:T(8,128)(2,1)}, bf16[192,16,128]{2,1,0:T(8,128)(2,1)S(1)}, u32[]{:S(2)}, u32[]{:S(2)}) collective-permute-start(bf16[192,16,128]{2,1,0:T(8,128)(2,1)} %get-tuple-element.20), channel_id=1, source_target_pairs={{0,1},{1,2},{2,3},{3,4},{4,5},{5,6},{6,7},{7,8},{8,9},{9,10},{10,1... | collective-permute-start | bytes 2359304 | tf_op jit(solution)/shard_map/ppermute | solution.py:352
  9.1 0.2 collective-permute-start.3
  9.3 2.0 %wall_pack.2 = (bf16[96,16,128]{2,1,0:T(8,128)(2,1)}, bf16[96,16,128]{2,1,0:T(8,128)(2,1)}) custom-call(bf16[192,64,128]{2,1,0:T(8,128)(2,1)} %bitcast.7), custom_call_target="tpu_custom_call" | custom-call | tf_op jit(solution)/shard_map/wall_pack/pallas_call | solution.py:107
  11.4 3.0 %collective-permute-start = (bf16[96,16,128]{2,1,0:T(8,128)(2,1)}, bf16[96,16,128]{2,1,0:T(8,128)(2,1)S(1)}, u32[]{:S(2)}, u32[]{:S(2)}) collective-permute-start(bf16[96,16,128]{2,1,0:T(8,128)(2,1)} %get-tuple-element.18), channel_id=1, source_target_pairs={{0,16},{16,32},{32,48},{1,17},{17,33},{33,49},{2,18},{18,34},{34,5... | collective-permute-start | bytes 1179656 | tf_op jit(solution)/shard_map/ppermute | solution.py:352
  14.4 1.3 %collective-permute-start.4 = (bf16[24,16,128]{2,1,0:T(8,128)(2,1)}, bf16[24,16,128]{2,1,0:T(8,128)(2,1)S(1)}, u32[]{:S(2)}, u32[]{:S(2)}) collective-permute-start(bf16[24,16,128]{2,1,0:T(8,128)(2,1)} %get-tuple-element.22), channel_id=1, source_target_pairs={{0,64},{64,128},{128,192},{192,0},{1,65},{65,129},{129,193},{193,1... | collective-permute-start | bytes 294920 | tf_op jit(solution)/shard_map/ppermute | solution.py:352
  15.7 1.5 %collective-permute-start.5 = (bf16[24,16,128]{2,1,0:T(8,128)(2,1)}, bf16[24,16,128]{2,1,0:T(8,128)(2,1)S(1)}, u32[]{:S(2)}, u32[]{:S(2)}) collective-permute-start(bf16[24,16,128]{2,1,0:T(8,128)(2,1)} %get-tuple-element.23), channel_id=1, source_target_pairs={{0,192},{64,0},{128,64},{192,128},{1,193},{65,1},{129,65},{193,129... | collective-permute-start | bytes 294920 | tf_op jit(solution)/shard_map/ppermute | solution.py:352
  17.2 2.5 %collective-permute-done.4.x_low = bf16[24,16,128]{2,1,0:T(8,128)(2,1)S(1)} collective-permute-done((bf16[24,16,128]{2,1,0:T(8,128)(2,1)}, bf16[24,16,128]{2,1,0:T(8,128)(2,1)S(1)}, u32[]{:S(2)}, u32[]{:S(2)}) %collective-permute-start.4) | collective-permute-done | bytes 98336 | tf_op jit(solution)/shard_map/ppermute | solution.py:352
  19.7 1.3 %collective-permute-start.1 = (bf16[96,16,128]{2,1,0:T(8,128)(2,1)}, bf16[96,16,128]{2,1,0:T(8,128)(2,1)S(1)}, u32[]{:S(2)}, u32[]{:S(2)}) collective-permute-start(bf16[96,16,128]{2,1,0:T(8,128)(2,1)} %get-tuple-element.19), channel_id=1, source_target_pairs={{16,0},{32,16},{48,32},{17,1},{33,17},{49,33},{18,2},{34,18},{50,3... | collective-permute-start | bytes 1179656 | tf_op jit(solution)/shard_map/ppermute | solution.py:352
  21.0 1.9 %wall_pack.3 = (bf16[96,16,128]{2,1,0:T(8,128)(2,1)S(1)}, bf16[96,16,128]{2,1,0:T(8,128)(2,1)}) custom-call(bf16[192,64,128]{2,1,0:T(8,128)(2,1)} %bitcast.8), custom_call_target="tpu_custom_call" | custom-call | tf_op jit(solution)/shard_map/wall_pack/pallas_call | solution.py:107
  22.9 0.0 copy-start
  22.9 0.7 copy-done
  23.6 0.0 collective-permute-done.5.x_high
  23.6 4.0 %collective-permute-start.6 = (bf16[96,16,128]{2,1,0:T(8,128)(2,1)}, bf16[96,16,128]{2,1,0:T(8,128)(2,1)S(1)}, u32[]{:S(2)}, u32[]{:S(2)}) collective-permute-start(bf16[96,16,128]{2,1,0:T(8,128)(2,1)} %get-tuple-element.24), channel_id=1, source_target_pairs={{0,16},{16,32},{32,48},{1,17},{17,33},{33,49},{2,18},{18,34},{34,5... | collective-permute-start | bytes 1179656 | tf_op jit(solution)/shard_map/ppermute | solution.py:352
  27.6 0.0 collective-permute-done.y_low
  27.6 1.3 %collective-permute-start.7 = (bf16[96,16,128]{2,1,0:T(8,128)(2,1)}, bf16[96,16,128]{2,1,0:T(8,128)(2,1)S(1)}, u32[]{:S(2)}, u32[]{:S(2)}) collective-permute-start(bf16[96,16,128]{2,1,0:T(8,128)(2,1)} %copy-done), channel_id=1, source_target_pairs={{16,0},{32,16},{48,32},{17,1},{33,17},{49,33},{18,2},{34,18},{50,3... | collective-permute-start | bytes 1179656 | tf_op jit(solution)/shard_map/ppermute | solution.py:352
  29.0 9.1 %snap_project.1 = f32[64,128]{1,0:T(8,128)} custom-call(bf16[128,24,8,128]{3,2,1,0:T(8,128)(2,1)} %bitcast.12, bf16[64,24,8,128]{3,2,1,0:T(8,128)(2,1)} %bitcast.9), custom_call_target="tpu_custom_call" | custom-call | tf_op jit(solution)/shard_map/snap_project/pallas_call | solution.py:209
  38.0 0.0 collective-permute-done.1.y_high
  38.0 0.0 collective-permute-done.2.z_low
  38.1 0.0 collective-permute-done.3.z_high
  38.1 9.3 %feature_project.2 = f32[32,128]{1,0:T(8,128)} custom-call(bf16[128,24,8,128]{3,2,1,0:T(8,128)(2,1)} %bitcast.13, bf16[192,64,128]{2,1,0:T(8,128)(2,1)} %bitcast.10, bf16[96,16,128]{2,1,0:T(8,128)(2,1)S(1)} %collective-permute-done.y_low, bf16[96,16,128]{2,1,0:T(8,128)(2,1)S(1)} %collective-permute-done.1.y_high, ...), custom_call_target="tpu_custom_call" | custom-call | tf_op jit(solution)/shard_map/feature_project/pallas_call | solution.py:291
  47.3 0.0 copy-start.1
  47.3 0.0 copy-start.2
  47.4 0.0 collective-permute-done.6.y_low
  47.4 0.0 collective-permute-done.7.y_high
  47.4 9.3 %feature_project.3 = f32[32,128]{1,0:T(8,128)} custom-call(bf16[128,24,8,128]{3,2,1,0:T(8,128)(2,1)} %bitcast.14, bf16[192,64,128]{2,1,0:T(8,128)(2,1)} %bitcast.11, bf16[96,16,128]{2,1,0:T(8,128)(2,1)S(1)} %collective-permute-done.6.y_low, bf16[96,16,128]{2,1,0:T(8,128)(2,1)S(1)} %collective-permute-done.7.y_high, ...), custom_call_target="tpu_custom_call" | custom-call | tf_op jit(solution)/shard_map/feature_project/pallas_call | solution.py:291
  56.7 0.0 copy-done.1
  56.7 0.0 copy-done.2
  56.7 0.7 fusion
  57.4 5.5 %collective-permute-start.8 = (f32[64,128]{1,0:T(8,128)S(1)}, f32[64,128]{1,0:T(8,128)S(1)}, u32[]{:S(2)}, u32[]{:S(2)}) collective-permute-start(f32[64,128]{1,0:T(8,128)S(1)} %fusion), channel_id=1, source_target_pairs={{0,1},{1,0},{2,3},{3,2},{4,5},{5,4},{6,7},{7,6},{8,9},{9,8},{10,11... | collective-permute-start | bytes 98312 | tf_op jit(solution)/shard_map/ppermute | solution.py:356
  62.9 0.9 collective-permute-done.8
  63.8 0.7 select_add_fusion
  64.5 0.0 collective-permute-start.9
  64.5 2.8 %collective-permute-done.9 = f32[64,128]{1,0:T(8,128)S(1)} collective-permute-done((f32[64,128]{1,0:T(8,128)S(1)}, f32[64,128]{1,0:T(8,128)S(1)}, u32[]{:S(2)}, u32[]{:S(2)}) %collective-permute-start.9) | collective-permute-done | bytes 32800 | tf_op jit(solution)/shard_map/ppermute | solution.py:356
  67.3 1.2 %collective-permute-start.10 = (f32[64,128]{1,0:T(8,128)S(1)}, f32[64,128]{1,0:T(8,128)S(1)}, u32[]{:S(2)}, u32[]{:S(2)}) collective-permute-start(f32[64,128]{1,0:T(8,128)S(1)} %add.25), channel_id=1, source_target_pairs={{0,192},{64,128},{128,64},{192,0},{1,193},{65,129},{129,65},{193,1... | collective-permute-start | bytes 98312 | tf_op jit(solution)/shard_map/ppermute | solution.py:356
  68.5 2.7 %collective-permute-done.10 = f32[64,128]{1,0:T(8,128)S(1)} collective-permute-done((f32[64,128]{1,0:T(8,128)S(1)}, f32[64,128]{1,0:T(8,128)S(1)}, u32[]{:S(2)}, u32[]{:S(2)}) %collective-permute-start.10) | collective-permute-done | bytes 32800 | tf_op jit(solution)/shard_map/ppermute | solution.py:356
  71.3 2.4 %collective-permute-start.11 = (f32[64,128]{1,0:T(8,128)S(1)}, f32[64,128]{1,0:T(8,128)S(1)}, u32[]{:S(2)}, u32[]{:S(2)}) collective-permute-start(f32[64,128]{1,0:T(8,128)S(1)} %add.26), channel_id=1, source_target_pairs={{0,16},{16,0},{32,48},{48,32},{1,17},{17,1},{33,49},{49,33},{2,18}... | collective-permute-start | bytes 98312 | tf_op jit(solution)/shard_map/ppermute | solution.py:356
  73.6 1.3 %collective-permute-done.11 = f32[64,128]{1,0:T(8,128)S(1)} collective-permute-done((f32[64,128]{1,0:T(8,128)S(1)}, f32[64,128]{1,0:T(8,128)S(1)}, u32[]{:S(2)}, u32[]{:S(2)}) %collective-permute-start.11) | collective-permute-done | bytes 32800 | tf_op jit(solution)/shard_map/ppermute | solution.py:356
  74.9 2.9 %collective-permute-start.12 = (f32[64,128]{1,0:T(8,128)S(1)}, f32[64,128]{1,0:T(8,128)S(1)}, u32[]{:S(2)}, u32[]{:S(2)}) collective-permute-start(f32[64,128]{1,0:T(8,128)S(1)} %add.27), channel_id=1, source_target_pairs={{0,48},{16,32},{32,16},{48,0},{1,49},{17,33},{33,17},{49,1},{2,50}... | collective-permute-start | bytes 98312 | tf_op jit(solution)/shard_map/ppermute | solution.py:356
  77.8 1.3 %collective-permute-done.12 = f32[64,128]{1,0:T(8,128)S(1)} collective-permute-done((f32[64,128]{1,0:T(8,128)S(1)}, f32[64,128]{1,0:T(8,128)S(1)}, u32[]{:S(2)}, u32[]{:S(2)}) %collective-permute-start.12) | collective-permute-done | bytes 32800 | tf_op jit(solution)/shard_map/ppermute | solution.py:356
  79.1 0.0 collective-permute-start.13
  79.1 2.8 %collective-permute-done.13 = f32[64,128]{1,0:T(8,128)S(1)} collective-permute-done((f32[64,128]{1,0:T(8,128)S(1)}, f32[64,128]{1,0:T(8,128)S(1)}, u32[]{:S(2)}, u32[]{:S(2)}) %collective-permute-start.13) | collective-permute-done | bytes 32800 | tf_op jit(solution)/shard_map/ppermute | solution.py:356
  81.9 0.7 collective-permute-start.14
  82.6 3.1 %collective-permute-done.14 = f32[64,128]{1,0:T(8,128)S(1)} collective-permute-done((f32[64,128]{1,0:T(8,128)S(1)}, f32[64,128]{1,0:T(8,128)S(1)}, u32[]{:S(2)}, u32[]{:S(2)}) %collective-permute-start.14) | collective-permute-done | bytes 32800 | tf_op jit(solution)/shard_map/ppermute | solution.py:356
  85.6 2.4 %collective-permute-start.15 = (f32[64,128]{1,0:T(8,128)S(1)}, f32[64,128]{1,0:T(8,128)S(1)}, u32[]{:S(2)}, u32[]{:S(2)}) collective-permute-start(f32[64,128]{1,0:T(8,128)S(1)} %add.30), channel_id=1, source_target_pairs={{0,12},{2,14},{4,8},{6,10},{8,4},{10,6},{12,0},{14,2},{1,13},{3,15... | collective-permute-start | bytes 98312 | tf_op jit(solution)/shard_map/ppermute | solution.py:356
  88.1 2.4 %collective-permute-done.15 = f32[64,128]{1,0:T(8,128)S(1)} collective-permute-done((f32[64,128]{1,0:T(8,128)S(1)}, f32[64,128]{1,0:T(8,128)S(1)}, u32[]{:S(2)}, u32[]{:S(2)}) %collective-permute-start.15) | collective-permute-done | bytes 32800 | tf_op jit(solution)/shard_map/ppermute | solution.py:356
  90.5 8.1 %collective-permute-start.16 = (f32[64,128]{1,0:T(8,128)S(1)}, f32[64,128]{1,0:T(8,128)S(1)}, u32[]{:S(2)}, u32[]{:S(2)}) collective-permute-start(f32[64,128]{1,0:T(8,128)S(1)} %add.31.mine), channel_id=1, source_target_pairs={{0,1},{1,0},{2,3},{3,2},{4,5},{5,4},{6,7},{7,6},{8,9},{9,8},{10,11... | collective-permute-start | bytes 98312 | tf_op jit(solution)/shard_map/ppermute | solution.py:356
  98.6 0.9 collective-permute-done.16.other
  99.4 1.0 grams.1
  (7 shorter events, 0.0 us)
Async XLA Ops:
  6.1 31.9 %collective-permute-start.2 = (bf16[192,16,128]{2,1,0:T(8,128)(2,1)}, bf16[192,16,128]{2,1,0:T(8,128)(2,1)S(1)}, u32[]{:S(2)}, u32[]{:S(2)}) collective-permute-start(bf16[192,16,128]{2,1,0:T(8,128)(2,1)} %get-tuple-element.20), channel_id=1, source_target_pairs={{0,1},{1,2},{2,3},{3,4},{4,5},{5,6},{6,7},{7,8},{8,9},{9,10},{10,1... | collective-permute-start | bytes 2359304 | tf_op jit(solution)/shard_map/ppermute | solution.py:352
  9.1 28.9 %collective-permute-start.3 = (bf16[192,16,128]{2,1,0:T(8,128)(2,1)}, bf16[192,16,128]{2,1,0:T(8,128)(2,1)S(1)}, u32[]{:S(2)}, u32[]{:S(2)}) collective-permute-start(bf16[192,16,128]{2,1,0:T(8,128)(2,1)} %get-tuple-element.21), channel_id=1, source_target_pairs={{0,15},{1,0},{2,1},{3,2},{4,3},{5,4},{6,5},{7,6},{8,7},{9,8},{10,9... | collective-permute-start | bytes 2359304 | tf_op jit(solution)/shard_map/ppermute | solution.py:352
  11.4 16.3 %collective-permute-start = (bf16[96,16,128]{2,1,0:T(8,128)(2,1)}, bf16[96,16,128]{2,1,0:T(8,128)(2,1)S(1)}, u32[]{:S(2)}, u32[]{:S(2)}) collective-permute-start(bf16[96,16,128]{2,1,0:T(8,128)(2,1)} %get-tuple-element.18), channel_id=1, source_target_pairs={{0,16},{16,32},{32,48},{1,17},{17,33},{33,49},{2,18},{18,34},{34,5... | collective-permute-start | bytes 1179656 | tf_op jit(solution)/shard_map/ppermute | solution.py:352
  14.4 5.3 %collective-permute-start.4 = (bf16[24,16,128]{2,1,0:T(8,128)(2,1)}, bf16[24,16,128]{2,1,0:T(8,128)(2,1)S(1)}, u32[]{:S(2)}, u32[]{:S(2)}) collective-permute-start(bf16[24,16,128]{2,1,0:T(8,128)(2,1)} %get-tuple-element.22), channel_id=1, source_target_pairs={{0,64},{64,128},{128,192},{192,0},{1,65},{65,129},{129,193},{193,1... | collective-permute-start | bytes 294920 | tf_op jit(solution)/shard_map/ppermute | solution.py:352
  15.7 7.9 %collective-permute-start.5 = (bf16[24,16,128]{2,1,0:T(8,128)(2,1)}, bf16[24,16,128]{2,1,0:T(8,128)(2,1)S(1)}, u32[]{:S(2)}, u32[]{:S(2)}) collective-permute-start(bf16[24,16,128]{2,1,0:T(8,128)(2,1)} %get-tuple-element.23), channel_id=1, source_target_pairs={{0,192},{64,0},{128,64},{192,128},{1,193},{65,1},{129,65},{193,129... | collective-permute-start | bytes 294920 | tf_op jit(solution)/shard_map/ppermute | solution.py:352
  19.7 18.4 %collective-permute-start.1 = (bf16[96,16,128]{2,1,0:T(8,128)(2,1)}, bf16[96,16,128]{2,1,0:T(8,128)(2,1)S(1)}, u32[]{:S(2)}, u32[]{:S(2)}) collective-permute-start(bf16[96,16,128]{2,1,0:T(8,128)(2,1)} %get-tuple-element.19), channel_id=1, source_target_pairs={{16,0},{32,16},{48,32},{17,1},{33,17},{49,33},{18,2},{34,18},{50,3... | collective-permute-start | bytes 1179656 | tf_op jit(solution)/shard_map/ppermute | solution.py:352
  22.9 0.7 copy-start
  23.6 23.7 %collective-permute-start.6 = (bf16[96,16,128]{2,1,0:T(8,128)(2,1)}, bf16[96,16,128]{2,1,0:T(8,128)(2,1)S(1)}, u32[]{:S(2)}, u32[]{:S(2)}) collective-permute-start(bf16[96,16,128]{2,1,0:T(8,128)(2,1)} %get-tuple-element.24), channel_id=1, source_target_pairs={{0,16},{16,32},{32,48},{1,17},{17,33},{33,49},{2,18},{18,34},{34,5... | collective-permute-start | bytes 1179656 | tf_op jit(solution)/shard_map/ppermute | solution.py:352
  27.6 19.7 %collective-permute-start.7 = (bf16[96,16,128]{2,1,0:T(8,128)(2,1)}, bf16[96,16,128]{2,1,0:T(8,128)(2,1)S(1)}, u32[]{:S(2)}, u32[]{:S(2)}) collective-permute-start(bf16[96,16,128]{2,1,0:T(8,128)(2,1)} %copy-done), channel_id=1, source_target_pairs={{16,0},{32,16},{48,32},{17,1},{33,17},{49,33},{18,2},{34,18},{50,3... | collective-permute-start | bytes 1179656 | tf_op jit(solution)/shard_map/ppermute | solution.py:352
  47.3 9.4 %copy-start.1 = (f32[64,128]{1,0:T(8,128)S(1)}, f32[64,128]{1,0:T(8,128)}, u32[]{:S(2)}) copy-start(f32[64,128]{1,0:T(8,128)} %snap_project.1) | copy-start | bytes 98308
  47.3 9.4 %copy-start.2 = (f32[32,128]{1,0:T(8,128)S(1)}, f32[32,128]{1,0:T(8,128)}, u32[]{:S(2)}) copy-start(f32[32,128]{1,0:T(8,128)} %feature_project.2) | copy-start | bytes 49156
  57.4 6.3 %collective-permute-start.8 = (f32[64,128]{1,0:T(8,128)S(1)}, f32[64,128]{1,0:T(8,128)S(1)}, u32[]{:S(2)}, u32[]{:S(2)}) collective-permute-start(f32[64,128]{1,0:T(8,128)S(1)} %fusion), channel_id=1, source_target_pairs={{0,1},{1,0},{2,3},{3,2},{4,5},{5,4},{6,7},{7,6},{8,9},{9,8},{10,11... | collective-permute-start | bytes 98312 | tf_op jit(solution)/shard_map/ppermute | solution.py:356
  64.5 2.8 %collective-permute-start.9 = (f32[64,128]{1,0:T(8,128)S(1)}, f32[64,128]{1,0:T(8,128)S(1)}, u32[]{:S(2)}, u32[]{:S(2)}) collective-permute-start(f32[64,128]{1,0:T(8,128)S(1)} %select_add_fusion), channel_id=1, source_target_pairs={{0,64},{64,0},{128,192},{192,128},{1,65},{65,1},{129,193},{193,129... | collective-permute-start | bytes 98312 | tf_op jit(solution)/shard_map/ppermute | solution.py:356
  67.3 4.0 %collective-permute-start.10 = (f32[64,128]{1,0:T(8,128)S(1)}, f32[64,128]{1,0:T(8,128)S(1)}, u32[]{:S(2)}, u32[]{:S(2)}) collective-permute-start(f32[64,128]{1,0:T(8,128)S(1)} %add.25), channel_id=1, source_target_pairs={{0,192},{64,128},{128,64},{192,0},{1,193},{65,129},{129,65},{193,1... | collective-permute-start | bytes 98312 | tf_op jit(solution)/shard_map/ppermute | solution.py:356
  71.3 3.7 %collective-permute-start.11 = (f32[64,128]{1,0:T(8,128)S(1)}, f32[64,128]{1,0:T(8,128)S(1)}, u32[]{:S(2)}, u32[]{:S(2)}) collective-permute-start(f32[64,128]{1,0:T(8,128)S(1)} %add.26), channel_id=1, source_target_pairs={{0,16},{16,0},{32,48},{48,32},{1,17},{17,1},{33,49},{49,33},{2,18}... | collective-permute-start | bytes 98312 | tf_op jit(solution)/shard_map/ppermute | solution.py:356
  74.9 4.2 %collective-permute-start.12 = (f32[64,128]{1,0:T(8,128)S(1)}, f32[64,128]{1,0:T(8,128)S(1)}, u32[]{:S(2)}, u32[]{:S(2)}) collective-permute-start(f32[64,128]{1,0:T(8,128)S(1)} %add.27), channel_id=1, source_target_pairs={{0,48},{16,32},{32,16},{48,0},{1,49},{17,33},{33,17},{49,1},{2,50}... | collective-permute-start | bytes 98312 | tf_op jit(solution)/shard_map/ppermute | solution.py:356
  79.1 2.8 %collective-permute-start.13 = (f32[64,128]{1,0:T(8,128)S(1)}, f32[64,128]{1,0:T(8,128)S(1)}, u32[]{:S(2)}, u32[]{:S(2)}) collective-permute-start(f32[64,128]{1,0:T(8,128)S(1)} %add.28), channel_id=1, source_target_pairs={{0,2},{2,0},{4,6},{6,4},{8,10},{10,8},{12,14},{14,12},{1,3},{3,1},... | collective-permute-start | bytes 98312 | tf_op jit(solution)/shard_map/ppermute | solution.py:356
  81.9 3.7 %collective-permute-start.14 = (f32[64,128]{1,0:T(8,128)S(1)}, f32[64,128]{1,0:T(8,128)S(1)}, u32[]{:S(2)}, u32[]{:S(2)}) collective-permute-start(f32[64,128]{1,0:T(8,128)S(1)} %add.29), channel_id=1, source_target_pairs={{0,4},{2,6},{4,0},{6,2},{8,12},{10,14},{12,8},{14,10},{1,5},{3,7},... | collective-permute-start | bytes 98312 | tf_op jit(solution)/shard_map/ppermute | solution.py:356
  85.6 4.9 %collective-permute-start.15 = (f32[64,128]{1,0:T(8,128)S(1)}, f32[64,128]{1,0:T(8,128)S(1)}, u32[]{:S(2)}, u32[]{:S(2)}) collective-permute-start(f32[64,128]{1,0:T(8,128)S(1)} %add.30), channel_id=1, source_target_pairs={{0,12},{2,14},{4,8},{6,10},{8,4},{10,6},{12,0},{14,2},{1,13},{3,15... | collective-permute-start | bytes 98312 | tf_op jit(solution)/shard_map/ppermute | solution.py:356
  90.5 8.9 %collective-permute-start.16 = (f32[64,128]{1,0:T(8,128)S(1)}, f32[64,128]{1,0:T(8,128)S(1)}, u32[]{:S(2)}, u32[]{:S(2)}) collective-permute-start(f32[64,128]{1,0:T(8,128)S(1)} %add.31.mine), channel_id=1, source_target_pairs={{0,1},{1,0},{2,3},{3,2},{4,5},{5,4},{6,7},{7,6},{8,9},{9,8},{10,11... | collective-permute-start | bytes 98312 | tf_op jit(solution)/shard_map/ppermute | solution.py:356

commit v2 on v0

v2 whole, which is shorter than its diff:
```python
import functools

import jax
import jax.numpy as jnp
import numpy as np
from jax import lax
from jax.experimental import pallas as pl
from jax.experimental.pallas import tpu as pltpu
from jax.sharding import Mesh
from jax.sharding import PartitionSpec as P


GZ = ("gz_0", "gz_1")
BF16 = jnp.bfloat16
F32 = jnp.float32
VISCOSITY = 0.1
VMEM_LIMIT = 24 * 2**20
HIGH = lax.Precision.HIGHEST
NT = (((1,), (1,)), ((), ()))
TN = (((0,), (0,)), ((), ()))

GRAD = {-2: 1.0, -1: -8.0, 1: 8.0, 2: -1.0}
CURV = {-2: -1.0, -1: 16.0, 0: -30.0, 1: 16.0, 2: -1.0}


def span_operator():
    op = np.zeros((128, 96), np.float32)

    def column(y, z):
        if z < 0:
            return 64 + y * 2 + z + 2
        if z > 7:
            return 80 + y * 2 + z - 8
        return y * 8 + z

    for y in range(8):
        for z in range(8):
            row = y * 8 + z
            for k, value in CURV.items():
                op[row, column(y, z + k)] += value
                if 0 <= y + k < 8:
                    op[row, column(y + k, z)] += value
            for k, value in GRAD.items():
                op[64 + row, column(y, z + k)] += value
    return op


def stream_operator():
    op = np.zeros((256, 256), np.float32)
    for part, taps in enumerate((GRAD, CURV)):
        for x in range(128):
            for k, value in taps.items():
                at = x + k
                if 0 <= at < 128:
                    op[at, part * 128 + x] += value
                else:
                    halo = at + 2 if at < 0 else at - 128 + 2
                    for j in range(32):
                        op[128 + 4 * j + halo, part * 128 + x] += value
    return op


def lane_masks():
    m, row, lane = np.meshgrid(np.arange(8), np.arange(64), np.arange(128), indexing="ij")
    return (lane // 4 == 4 * m + row // 16).astype(np.float32)


def in_vmem(array):
    return pltpu.with_memory_space_constraint(array, pltpu.VMEM)


def from_hbm(array):
    return pltpu.with_memory_space_constraint(array, pltpu.HBM)


def in_hbm():
    return pl.BlockSpec(memory_space=pltpu.HBM)


def resident():
    return pl.BlockSpec(memory_space=pltpu.VMEM)


def wall_pack_body(snap, low, high, low_in, high_in, sems):
    ends = ((0, low, low_in), (48, high, high_in))
    reads = [pltpu.make_async_copy(snap.at[:, pl.ds(row, 16)], at, sems.at[i]) for i, (row, _, at) in enumerate(ends)]
    writes = [pltpu.make_async_copy(at, to, sems.at[2 + i]) for i, (_, to, at) in enumerate(ends)]
    for c in reads:
        c.start()
    for r, w in zip(reads, writes):
        r.wait()
        w.start()
    for w in writes:
        w.wait()


def wall_pack(snap):
    shape = jax.ShapeDtypeStruct((192, 16, 128), BF16)
    block = pltpu.VMEM((192, 16, 128), BF16)
    return pl.pallas_call(
        wall_pack_body,
        out_shape=(shape, shape),
        in_specs=[in_hbm()],
        out_specs=(in_hbm(), in_hbm()),
        scratch_shapes=[block, block, pltpu.SemaphoreType.DMA((4,))],
        compiler_params=pltpu.CompilerParams(vmem_limit_bytes=VMEM_LIMIT),
        name="wall_pack",
    )(from_hbm(snap))


def side_pack_body(snap, low, high, right, left):
    grid = lambda shape: [lax.broadcasted_iota(jnp.int32, shape, d) for d in range(2)]
    row, col = grid((32, 64))
    wanted = (row % 16) // 2 * 8 + row % 2 + jnp.where(row < 16, 0, 6)
    span = (col == wanted).astype(F32).astype(BF16)
    row, col = grid((128, 256))
    last = (col < 128) & (col % 4 < 2) & (row == 126 + col % 4)
    first = (col >= 128) & (col % 4 >= 2) & (row == col % 4 - 2)
    lanes = (last | first).astype(F32).astype(BF16)
    lane = lax.broadcasted_iota(jnp.int32, (16, 128), 1) // 4

    def group_of(group, _):
        units = [snap[8 * group + m] for m in range(8)]
        for pair in range(4):
            both = jnp.concatenate(units[2 * pair : 2 * pair + 2], axis=1)
            picked = jnp.dot(span, both, preferred_element_type=F32).astype(BF16)
            for i in range(2):
                low[8 * group + 2 * pair + i] = picked[:16, 128 * i : 128 * (i + 1)]
                high[8 * group + 2 * pair + i] = picked[16:, 128 * i : 128 * (i + 1)]
        ends = jnp.dot(jnp.concatenate(units, axis=0), lanes, preferred_element_type=F32)
        to_right = jnp.zeros((16, 128), F32)
        to_left = jnp.zeros((16, 128), F32)
        for j in range(32):
            to_right = jnp.where(lane == j, ends[16 * j : 16 * j + 16, :128], to_right)
            to_left = jnp.where(lane == j, ends[16 * j : 16 * j + 16, 128:], to_left)
        right[group] = to_right.astype(BF16)
        left[group] = to_left.astype(BF16)
        return _

    lax.fori_loop(0, 24, group_of, 0, unroll=4)


def side_pack(snap):
    wide, slim = jax.ShapeDtypeStruct((192, 16, 128), BF16), jax.ShapeDtypeStruct((24, 16, 128), BF16)
    return pl.pallas_call(
        side_pack_body,
        out_shape=(wide, wide, slim, slim),
        in_specs=[resident()],
        out_specs=(resident(),) * 4,
        compiler_params=pltpu.CompilerParams(vmem_limit_bytes=VMEM_LIMIT),
        name="side_pack",
    )(in_vmem(snap))


def same_span(total, out):
    lanes = lax.broadcasted_iota(jnp.int32, (128, 128), 1) % 8
    s = lax.broadcasted_iota(jnp.int32, (16, 128), 0)
    at = lax.broadcasted_iota(jnp.int32, (16, 128), 1)
    group = (at // 8 == s).astype(F32)
    for block in range(4):
        kept = total[block, pl.ds(0, 128, stride=8), :]
        for z in range(1, 8):
            kept = jnp.where(lanes == z, total[block, pl.ds(z, 128, stride=8), :], kept)
        out[16 * block : 16 * block + 16] = lax.dot_general(
            group, kept, NT, precision=HIGH, preferred_element_type=F32
        )


def add_products(modes, planes, data, total, base):
    a = jnp.concatenate([modes[k].reshape(1024, 128) for k in planes], axis=1)
    part = lax.dot_general(a, jnp.concatenate(data, axis=1), NT, preferred_element_type=F32)
    for block in range(4):
        lanes = part[:, 128 * block : 128 * block + 128]
        total[block] = lanes if base is None else base[block] + lanes


def snap_project_body(modes, snap, out, modes_in, snap_in, total, sems):
    copies = []
    for k in range(24):
        copies.append(pltpu.make_async_copy(modes.at[:, k], modes_in.at[k], sems.at[0, k]))
        copies.append(pltpu.make_async_copy(snap.at[:, k], snap_in.at[k], sems.at[1, k]))
    for c in copies:
        c.start()
    for k in range(0, 24, 4):
        for c in copies[2 * k : 2 * k + 8]:
            c.wait()
        planes = range(k, k + 4)
        add_products(modes_in, planes, [snap_in[p].reshape(512, 128) for p in planes], total, total if k else None)
    same_span(total, out)


def snap_project(modes, snap):
    return pl.pallas_call(
        snap_project_body,
        out_shape=(jax.ShapeDtypeStruct((64, 128), F32), jax.ShapeDtypeStruct((24, 128, 8, 128), BF16)),
        in_specs=[in_hbm(), in_hbm()],
        out_specs=(resident(), resident()),
        scratch_shapes=[
            pltpu.VMEM((24, 64, 8, 128), BF16),
            pltpu.VMEM((4, 1024, 128), F32),
            pltpu.SemaphoreType.DMA((2, 24)),
        ],
        compiler_params=pltpu.CompilerParams(vmem_limit_bytes=VMEM_LIMIT),
        name="snap_project",
    )(from_hbm(modes), from_hbm(snap))


def feature_body(
    modes_in, snap, z_low, z_high, x_low, x_high, span, stream, masks, total, edges, field
):
    def block(step, _):
        for pair in range(4):
            base = 24 * step + 6 * pair
            units = [[6 * pair + 3 * i + c for c in range(3)] for i in range(2)]
            cells = [[snap[base + 3 * i + c] for c in range(3)] for i in range(2)]
            inside = jnp.concatenate(cells[0] + cells[1], axis=0)
            beside = []
            for u in units[0] + units[1]:
                halo = x_low[3 * step + u // 8] + x_high[3 * step + u // 8]
                beside.append(jnp.concatenate([halo] * 4, axis=0) * masks[u % 8])
            beside = jnp.concatenate(beside, axis=0)
            along = jnp.dot(jnp.concatenate([inside, beside], axis=1), stream[...], preferred_element_type=F32)
            wide = [[v.astype(F32).reshape(8, 8, 128) for v in row] for row in cells]
            velocity = [[v * (1.0 / 12.0) for v in row] for row in wide]
            for c in range(3):
                padded = [
                    jnp.concatenate(
                        [cells[i][c], z_low[base + 3 * i + c], z_high[base + 3 * i + c]], axis=0
                    )
                    for i in range(2)
                ]
                across = jnp.dot(span[...], jnp.concatenate(padded, axis=1), preferred_element_type=F32)
                both = []
                for i in range(2):
                    none = jnp.zeros((2, 8, 128), F32)
                    ext = jnp.concatenate([none, wide[i][c], none], axis=0)
                    near, far = ext[3:11] - ext[1:9], ext[4:12] - ext[0:8]
                    lanes = slice(128 * i, 128 * (i + 1))
                    rows = slice(192 * i + 64 * c, 192 * i + 64 * (c + 1))
                    cube = lambda part: part.reshape(8, 8, 128)
                    laplace = cube(across[0:64, lanes]) + cube(along[rows, 128:256])
                    advect = (
                        velocity[i][0] * cube(along[rows, 0:128])
                        + velocity[i][1] * (8.0 * near - far)
                        + velocity[i][2] * cube(across[64:128, lanes])
                    )
                    value = laplace * (VISCOSITY / 12.0) - advect
                    both.append(value[2:6])
                    edges[base + 3 * i + c, 0:2] = value[0:2]
                    edges[base + 3 * i + c, 2:4] = value[6:8]
                start = pl.multiple_of((8 * step + 2 * pair) * 8, 16)
                field[4 * c : 4 * c + 4, pl.ds(start, 16), :] = jnp.concatenate(both, axis=1).astype(BF16)
        return _

    lax.fori_loop(0, 8, block, 0)
    for c in range(3):
        planes = range(8 * c + 2, 8 * c + 6)
        add_products(modes_in, planes, [field[4 * c + k] for k in range(4)], total, total if c else None)


def feature_project(modes_in, snap, z_low, z_high, x_low, x_high):
    consts = [jnp.asarray(v, BF16) for v in (span_operator(), stream_operator(), lane_masks())]
    return pl.pallas_call(
        feature_body,
        out_shape=(
            jax.ShapeDtypeStruct((4, 1024, 128), F32),
            jax.ShapeDtypeStruct((192, 4, 8, 128), F32),
        ),
        in_specs=[resident()] * 9,
        out_specs=(resident(), resident()),
        scratch_shapes=[pltpu.VMEM((12, 512, 128), BF16)],
        compiler_params=pltpu.CompilerParams(vmem_limit_bytes=VMEM_LIMIT),
        name="feature_project",
    )(*map(in_vmem, (modes_in, snap, z_low, z_high, x_low, x_high)), *consts)


def edge_body(modes_in, snap, edges, y_low, y_high, inner, out, field, total):
    k = VISCOSITY / 12.0

    def block(step, _):
        base = 12 * step
        values = []
        for i in range(4):
            wall = snap[base + 3 * i + 1].astype(F32) * (1.0 / 12.0)
            wall = wall.reshape(8, 8, 128)
            below_near, below_far = 16.0 * k + 8.0 * wall[0], k + wall[0]
            above_near, above_far = 16.0 * k - 8.0 * wall[7], k - wall[7]
            second, seventh = k + wall[1], k - wall[6]
            row = []
            for c in range(3):
                u = base + 3 * i + c
                below = y_low[u].astype(F32).reshape(2, 8, 128)
                above = y_high[u].astype(F32).reshape(2, 8, 128)
                value = edges[u]
                row.append(
                    jnp.stack(
                        [
                            value[0] + (below_near * below[1] - below_far * below[0]),
                            value[1] - second * below[1],
                            value[2] - seventh * above[0],
                            value[3] + (above_near * above[0] - above_far * above[1]),
                        ]
                    )
                )
            values.append(row)
        for pair in range(2):
            start = pl.multiple_of((4 * step + 2 * pair) * 8, 16)
            for c in range(3):
                both = jnp.concatenate([values[2 * pair][c], values[2 * pair + 1][c]], axis=1)
                field[4 * c : 4 * c + 4, pl.ds(start, 16), :] = both.astype(BF16)
        return _

    lax.fori_loop(0, 16, block, 0, unroll=4)
    for c in range(3):
        planes = [8 * c, 8 * c + 1, 8 * c + 6, 8 * c + 7]
        add_products(modes_in, planes, [field[4 * c + p] for p in range(4)], total, total if c else inner)
    same_span(total, out)


def edge_project(modes_in, snap, edges, y_low, y_high, inner):
    return pl.pallas_call(
        edge_body,
        out_shape=jax.ShapeDtypeStruct((64, 128), F32),
        in_specs=[resident()] * 6,
        out_specs=resident(),
        scratch_shapes=[pltpu.VMEM((12, 512, 128), BF16), pltpu.VMEM((4, 1024, 128), F32)],
        compiler_params=pltpu.CompilerParams(vmem_limit_bytes=VMEM_LIMIT),
        name="edge_project",
    )(*map(in_vmem, (modes_in, snap, edges, y_low, y_high, inner)))


def gram_body(core, mine, other, snap_out, feature_out, gram_snap, gram_feature, gram_quad):
    first = core[0] == 0
    rs = jnp.where(first, mine[...], other[...])
    rf = jnp.where(first, other[...], mine[...])
    snap_out[...] = rs
    feature_out[...] = rf
    dot = functools.partial(lax.dot_general, precision=HIGH, preferred_element_type=F32)
    gram_snap[...] = dot(rs, rs, TN) * (1.0 / 64)
    gram_feature[...] = dot(rf, rs, TN) * (1.0 / 64)
    products = dot(rs, rs, NT) * (1.0 / 128)
    gram_quad[...] = products * products


def grams(core, mine, other):
    shape = lambda *s: jax.ShapeDtypeStruct(s, F32)
    vmem = pl.BlockSpec(memory_space=pltpu.VMEM)
    return pl.pallas_call(
        gram_body,
        in_specs=[pl.BlockSpec(memory_space=pltpu.SMEM), vmem, vmem],
        out_shape=(shape(64, 128), shape(64, 128), shape(128, 128), shape(128, 128), shape(64, 64)),
        compiler_params=pltpu.CompilerParams(vmem_limit_bytes=VMEM_LIMIT),
        name="grams",
    )(core, in_vmem(mine), in_vmem(other))


def shifted(value, axis, count, by, closed):
    pairs = [(i, (i + by) % count) for i in range(count) if closed or 0 <= i + by < count]
    return lax.ppermute(value, axis, pairs)


def swapped(value, axis, partners):
    return lax.ppermute(value, axis, list(enumerate(partners)))


ROUNDS = (
    ("gx", (1, 0, 3, 2)),
    ("gx", (3, 2, 1, 0)),
    ("gy", (1, 0, 3, 2)),
    ("gy", (3, 2, 1, 0)),
    ("gz_0", (1, 0, 3, 2, 5, 4, 7, 6)),
    ("gz_0", (2, 3, 0, 1, 6, 7, 4, 5)),
    ("gz_0", (6, 7, 4, 5, 2, 3, 0, 1)),
)


def shards(snapshots, modes):
    units = snapshots.reshape(192, 64, 128)
    low, high = wall_pack(units)
    y_low = shifted(high, "gy", 4, 1, False)
    y_high = shifted(low, "gy", 4, -1, False)
    low, high, right, left = side_pack(units)
    z_low = shifted(high, GZ, 16, 1, True)
    z_high = shifted(low, GZ, 16, -1, True)
    x_low = shifted(right, "gx", 4, 1, True)
    x_high = shifted(left, "gx", 4, -1, True)
    snap_part, modes_in = snap_project(modes.reshape(128, 24, 8, 128), snapshots.reshape(64, 24, 8, 128))
    inner, edges = feature_project(modes_in, units, z_low, z_high, x_low, x_high)
    feature_part = edge_project(modes_in, units, edges, y_low, y_high, inner)
    core = lax.axis_index("gz_1")
    mine = jnp.where(core == 0, snap_part, feature_part)
    total = mine + swapped(jnp.where(core == 0, feature_part, snap_part), "gz_1", (1, 0))
    for axis, partners in ROUNDS:
        total = total + swapped(total, axis, partners)
    rs, rf, gram_snap, gram_feature, gram_quad = grams(
        core.reshape(1).astype(jnp.int32), total, swapped(total, "gz_1", (1, 0))
    )
    return rs.T, rf.T, gram_snap, gram_feature, gram_quad


def solution(mesh):
    finer = Mesh(
        mesh.devices.reshape(mesh.shape["gx"], mesh.shape["gy"], 8, 2), ("gx", "gy", "gz_0", "gz_1")
    )
    placed = (P(None, None, "gy", GZ, "gx"), P(None, None, "gy", GZ, "gx"))

    return jax.shard_map(shards, mesh=finer, in_specs=placed, out_specs=(P(), P(), P(), P(), P()), check_vma=False)
```

time: 162 us -> 91.3 us (0.56)
  blocking collectives: 60.5 us -> 0 us
  local copies, waits for them, and re-layouts: 47.9 us -> 8.08 us
  other arithmetic: 30.2 us -> 0.05 us
  Pallas kernels: 0 us -> 26.3 us
  waiting for transfers between devices: 0.02 us -> 22.2 us
  starting transfers between devices: 11.5 us -> 33.5 us
  matrix products: 10.8 us -> 0 us
    all_to_all x2 -> x0, blocking collectives: 60.5 us -> none  [sent_to_all(): lax.all_to_all(jnp.broadcast_to(shard[None], (length, *shard.shape)), axi...]
    convert_element_type x2 -> x0, other arithmetic: 27.3 us -> none  [the longest x1 22.9 us: feature_field(): return (viscosity * laplace - advect).astype(jnp.bfloat16)]
    pallas_call x0 -> x6, Pallas kernels: none -> 26.3 us  [the longest x1 8.08 us: feature_project(): pl.pallas_call(feature_body, out_shape=(jax.ShapeDtypeStruct((4, 1024, 12...]
    ppermute x6 -> x15, waiting for transfers between devices: 0.02 us -> 22.2 us  [the longest x9 18.4 us: swapped(): return lax.ppermute(value, axis, list(enumerate(partners)))]
    ppermute x6 -> x15, starting transfers between devices: 11.5 us -> 33.5 us  [the longest x9 22.5 us: swapped(): return lax.ppermute(value, axis, list(enumerate(partners)))]
    ppermute x3 -> x0, local copies, waits for them, and re-layouts: 14.8 us -> none  [the longest x2 8.81 us: padded_2(): lax.ppermute(tail, axis, [(i, (i + 1) % count) for i in range(ends)])]
    unnamed x13 -> x14, local copies, waits for them, and re-layouts: 20.2 us -> 8.08 us
    dot_general x4 -> x0, matrix products: 10.8 us -> none  [the longest x1 8.07 us: project(): lax.dot_general(modes_flat, data_flat, (((1,), (1,)), ((), ())), preferre...]
  transfers between devices with their start and end apart: 6 -> 15, of which waited for: 0 -> 10; matrix products, arithmetic and copies ran while one was open for 29% -> 0% of each run, Pallas kernels for 0% -> 19%
where the time goes in v2:
time: 91.3 us; the launch traced here: 90.9 us
  starting transfers between devices  33.5 us (37%)
  Pallas kernels  26.3 us (29%)
  waiting for transfers between devices  22.2 us (24%)
  local copies, waits for them, and re-layouts  8.08 us (9%)
    ppermute x9, starting transfers between devices, swapped(): return lax.ppermute(value, axis, list(enumerate(partners)))  22.5 us
    ppermute x9, waiting for transfers between devices, swapped(): return lax.ppermute(value, axis, list(enumerate(partners)))  18.4 us
    ppermute x6, starting transfers between devices, shifted(): return lax.ppermute(value, axis, pairs)  11 us
    pallas_call x1, Pallas kernels, feature_project(): pl.pallas_call(feature_body, out_shape=(jax.ShapeDtypeStruct((4, 1024, 12...  8.08 us
    unnamed x14, local copies, waits for them, and re-layouts  8.08 us
    pallas_call x1, Pallas kernels, snap_project(): pl.pallas_call(snap_project_body, out_shape=(jax.ShapeDtypeStruct((64, 12...  6.48 us
    pallas_call x1, Pallas kernels, edge_project(): pl.pallas_call(edge_body, out_shape=jax.ShapeDtypeStruct((64, 128), F32),...  4.35 us
    pallas_call x1, Pallas kernels, side_pack(): pl.pallas_call(side_pack_body, out_shape=(wide, wide, slim, slim), in_spe...  4.09 us
  transfers between devices with their start and end apart: 15, of which 10 were waited for; matrix products, arithmetic and copies ran while one was open for 0% of the time, Pallas kernels for 19%

profile of v2, /device:TPU:1, one launch (start us, length us, event | category | flops | bytes accessed | tf_op | source)
XLA Modules:
  0.0 90.9 jit_solution(2388874274899456149)
XLA Ops:
  0.6 0.0 copy-start
  0.6 1.9 %copy-done = bf16[64,3,8,8,128]{4,3,2,1,0:T(8,128)(2,1)S(1)} copy-done((bf16[64,3,8,8,128]{4,3,2,1,0:T(8,128)(2,1)S(1)}, bf16[64,3,8,8,128]{4,3,2,1,0:T(8,128)(2,1)}, u32[]{:S(2)}) %copy-start) | copy-done | bytes 3145752
  2.5 4.1 %side_pack.1 = (bf16[192,16,128]{2,1,0:T(8,128)(2,1)}, bf16[192,16,128]{2,1,0:T(8,128)(2,1)}, bf16[24,16,128]{2,1,0:T(8,128)(2,1)S(1)}, bf16[24,16,128]{2,1,0:T(8,128)(2,1)}) custom-call(bf16[192,64,128]{2,1,0:T(8,128)(2,1)S(1)} %bitcast.8), custom_call_target="tpu_custom_call" | custom-call | tf_op jit(solution)/shard_map/side_pack/pallas_call | solution.py:145
  6.6 3.0 %collective-permute-start = (bf16[192,16,128]{2,1,0:T(8,128)(2,1)}, bf16[192,16,128]{2,1,0:T(8,128)(2,1)}, u32[]{:S(2)}, u32[]{:S(2)}) collective-permute-start(bf16[192,16,128]{2,1,0:T(8,128)(2,1)} %get-tuple-element.22), channel_id=1, source_target_pairs={{0,1},{1,2},{2,3},{3,4},{4,5},{5,6},{6,7},{7,8},{8,9},{9,10},{10,1... | collective-permute-start | bytes 2359304 | tf_op jit(solution)/shard_map/ppermute | solution.py:359
  9.6 0.2 collective-permute-start.1
  9.8 2.3 %wall_pack.1 = (bf16[192,16,128]{2,1,0:T(8,128)(2,1)}, bf16[192,16,128]{2,1,0:T(8,128)(2,1)}) custom-call(bf16[192,64,128]{2,1,0:T(8,128)(2,1)} %bitcast.6), custom_call_target="tpu_custom_call" | custom-call | tf_op jit(solution)/shard_map/wall_pack/pallas_call | solution.py:100
  12.1 4.0 %collective-permute-start.4 = (bf16[192,16,128]{2,1,0:T(8,128)(2,1)}, bf16[192,16,128]{2,1,0:T(8,128)(2,1)}, u32[]{:S(2)}, u32[]{:S(2)}) collective-permute-start(bf16[192,16,128]{2,1,0:T(8,128)(2,1)} %get-tuple-element.27), channel_id=1, source_target_pairs={{0,16},{16,32},{32,48},{1,17},{17,33},{33,49},{2,18},{18,34},{34,5... | collective-permute-start | bytes 2359304 | tf_op jit(solution)/shard_map/ppermute | solution.py:359
  16.1 1.3 %collective-permute-start.5 = (bf16[192,16,128]{2,1,0:T(8,128)(2,1)}, bf16[192,16,128]{2,1,0:T(8,128)(2,1)}, u32[]{:S(2)}, u32[]{:S(2)}) collective-permute-start(bf16[192,16,128]{2,1,0:T(8,128)(2,1)} %get-tuple-element.28), channel_id=1, source_target_pairs={{16,0},{32,16},{48,32},{17,1},{33,17},{49,33},{18,2},{34,18},{50,3... | collective-permute-start | bytes 2359304 | tf_op jit(solution)/shard_map/ppermute | solution.py:359
  17.4 1.3 %collective-permute-start.2 = (bf16[24,16,128]{2,1,0:T(8,128)(2,1)S(1)}, bf16[24,16,128]{2,1,0:T(8,128)(2,1)S(1)}, u32[]{:S(2)}, u32[]{:S(2)}) collective-permute-start(bf16[24,16,128]{2,1,0:T(8,128)(2,1)S(1)} %get-tuple-element.24), channel_id=1, source_target_pairs={{0,64},{64,128},{128,192},{192,0},{1,65},{65,129},{129,193},{193,1... | collective-permute-start | bytes 294920 | tf_op jit(solution)/shard_map/ppermute | solution.py:359
  18.7 3.9 %collective-permute-done.2.x_low = bf16[24,16,128]{2,1,0:T(8,128)(2,1)S(1)} collective-permute-done((bf16[24,16,128]{2,1,0:T(8,128)(2,1)S(1)}, bf16[24,16,128]{2,1,0:T(8,128)(2,1)S(1)}, u32[]{:S(2)}, u32[]{:S(2)}) %collective-permute-start.2) | collective-permute-done | bytes 98336 | tf_op jit(solution)/shard_map/ppermute | solution.py:359
  22.6 1.3 %collective-permute-start.3 = (bf16[24,16,128]{2,1,0:T(8,128)(2,1)}, bf16[24,16,128]{2,1,0:T(8,128)(2,1)}, u32[]{:S(2)}, u32[]{:S(2)}) collective-permute-start(bf16[24,16,128]{2,1,0:T(8,128)(2,1)} %get-tuple-element.25), channel_id=1, source_target_pairs={{0,192},{64,0},{128,64},{192,128},{1,193},{65,1},{129,65},{193,129... | collective-permute-start | bytes 294920 | tf_op jit(solution)/shard_map/ppermute | solution.py:359
  23.8 0.0 copy-start.1
  23.8 0.0 copy-start.4
  23.8 0.0 copy-start.5
  23.8 6.5 %snap_project.1 = (f32[64,128]{1,0:T(8,128)S(1)}, bf16[24,128,8,128]{3,2,1,0:T(8,128)(2,1)S(1)}) custom-call(bf16[128,24,8,128]{3,2,1,0:T(8,128)(2,1)} %bitcast.11, bf16[64,24,8,128]{3,2,1,0:T(8,128)(2,1)} %bitcast.7), custom_call_target="tpu_custom_call" | custom-call | tf_op jit(solution)/shard_map/snap_project/pallas_call | solution.py:193
  30.3 0.0 copy-start.2
  30.3 2.6 %copy-done.2 = bf16[24,128,8,128]{3,2,1,0:T(8,128)(2,1)} copy-done((bf16[24,128,8,128]{3,2,1,0:T(8,128)(2,1)}, bf16[24,128,8,128]{3,2,1,0:T(8,128)(2,1)S(1)}, u32[]{:S(2)}) %copy-start.2) | copy-done | bytes 6291480
  33.0 0.0 collective-permute-done.3.x_high
  33.0 0.0 collective-permute-done.z_low
  33.0 0.0 collective-permute-done.1.z_high
  33.0 0.0 copy-done.1
  33.0 0.0 copy-done.4
  33.0 0.0 copy-done.5
  33.0 0.0 copy-start.3
  33.0 2.8 %copy-done.3 = bf16[24,128,8,128]{3,2,1,0:T(8,128)(2,1)S(1)} copy-done((bf16[24,128,8,128]{3,2,1,0:T(8,128)(2,1)S(1)}, bf16[24,128,8,128]{3,2,1,0:T(8,128)(2,1)}, u32[]{:S(2)}) %copy-start.3) | copy-done | bytes 6291480
  35.8 0.0 copy-start.6
  35.8 0.8 copy-done.6
  36.6 8.1 %feature_project.1 = (f32[4,1024,128]{2,1,0:T(8,128)S(1)}, f32[192,4,8,128]{3,2,1,0:T(8,128)S(1)}) custom-call(bf16[24,128,8,128]{3,2,1,0:T(8,128)(2,1)S(1)} %copy-done.3, bf16[192,64,128]{2,1,0:T(8,128)(2,1)S(1)} %bitcast.9, bf16[192,16,128]{2,1,0:T(8,128)(2,1)} %collective-permute-done.z_low, bf16[192,16,128]{2,1,0:T(8,128)(2,1)} %collective-permute-done.1.z_high, ...), custom_call_target="tpu_custom_call" | custom-call | tf_op jit(solution)/shard_map/feature_project/pallas_call | solution.py:263
  44.7 0.0 collective-permute-done.4.y_low
  44.7 0.0 collective-permute-done.5.y_high
  44.7 4.3 %edge_project.1 = f32[64,128]{1,0:T(8,128)S(1)} custom-call(bf16[24,128,8,128]{3,2,1,0:T(8,128)(2,1)S(1)} %copy-done.3, bf16[192,64,128]{2,1,0:T(8,128)(2,1)S(1)} %bitcast.10, f32[192,4,8,128]{3,2,1,0:T(8,128)S(1)} %get-tuple-element.26.edges, bf16[192,16,128]{2,1,0:T(8,128)(2,1)} %collective-permute-done.4.y_low, ...), custom_call_target="tpu_custom_call" | custom-call | tf_op jit(solution)/shard_map/edge_project/pallas_call | solution.py:321
  49.0 5.2 %collective-permute-start.6 = (f32[64,128]{1,0:T(8,128)S(1)}, f32[64,128]{1,0:T(8,128)S(1)}, u32[]{:S(2)}, u32[]{:S(2)}) collective-permute-start(f32[64,128]{1,0:T(8,128)S(1)} %broadcast_select_fusion), channel_id=1, source_target_pairs={{0,1},{1,0},{2,3},{3,2},{4,5},{5,4},{6,7},{7,6},{8,9},{9,8},{10,11... | collective-permute-start | bytes 98312 | tf_op jit(solution)/shard_map/ppermute | solution.py:363
  54.2 0.9 collective-permute-done.6
  55.1 0.2 collective-permute-start.7
  55.3 2.6 %collective-permute-done.7 = f32[64,128]{1,0:T(8,128)S(1)} collective-permute-done((f32[64,128]{1,0:T(8,128)S(1)}, f32[64,128]{1,0:T(8,128)S(1)}, u32[]{:S(2)}, u32[]{:S(2)}) %collective-permute-start.7) | collective-permute-done | bytes 32800 | tf_op jit(solution)/shard_map/ppermute | solution.py:363
  57.8 0.6 collective-permute-start.8
  58.4 3.4 %collective-permute-done.8 = f32[64,128]{1,0:T(8,128)S(1)} collective-permute-done((f32[64,128]{1,0:T(8,128)S(1)}, f32[64,128]{1,0:T(8,128)S(1)}, u32[]{:S(2)}, u32[]{:S(2)}) %collective-permute-start.8) | collective-permute-done | bytes 32800 | tf_op jit(solution)/shard_map/ppermute | solution.py:363
  61.8 2.4 %collective-permute-start.9 = (f32[64,128]{1,0:T(8,128)S(1)}, f32[64,128]{1,0:T(8,128)S(1)}, u32[]{:S(2)}, u32[]{:S(2)}) collective-permute-start(f32[64,128]{1,0:T(8,128)S(1)} %add.26), channel_id=1, source_target_pairs={{0,16},{16,0},{32,48},{48,32},{1,17},{17,1},{33,49},{49,33},{2,18}... | collective-permute-start | bytes 98312 | tf_op jit(solution)/shard_map/ppermute | solution.py:363
  64.2 1.3 %collective-permute-done.9 = f32[64,128]{1,0:T(8,128)S(1)} collective-permute-done((f32[64,128]{1,0:T(8,128)S(1)}, f32[64,128]{1,0:T(8,128)S(1)}, u32[]{:S(2)}, u32[]{:S(2)}) %collective-permute-start.9) | collective-permute-done | bytes 32800 | tf_op jit(solution)/shard_map/ppermute | solution.py:363
  65.5 2.8 %collective-permute-start.10 = (f32[64,128]{1,0:T(8,128)S(1)}, f32[64,128]{1,0:T(8,128)S(1)}, u32[]{:S(2)}, u32[]{:S(2)}) collective-permute-start(f32[64,128]{1,0:T(8,128)S(1)} %add.27), channel_id=1, source_target_pairs={{0,48},{16,32},{32,16},{48,0},{1,49},{17,33},{33,17},{49,1},{2,50}... | collective-permute-start | bytes 98312 | tf_op jit(solution)/shard_map/ppermute | solution.py:363
  68.3 1.3 %collective-permute-done.10 = f32[64,128]{1,0:T(8,128)S(1)} collective-permute-done((f32[64,128]{1,0:T(8,128)S(1)}, f32[64,128]{1,0:T(8,128)S(1)}, u32[]{:S(2)}, u32[]{:S(2)}) %collective-permute-start.10) | collective-permute-done | bytes 32800 | tf_op jit(solution)/shard_map/ppermute | solution.py:363
  69.6 0.0 collective-permute-start.11
  69.6 2.8 %collective-permute-done.11 = f32[64,128]{1,0:T(8,128)S(1)} collective-permute-done((f32[64,128]{1,0:T(8,128)S(1)}, f32[64,128]{1,0:T(8,128)S(1)}, u32[]{:S(2)}, u32[]{:S(2)}) %collective-permute-start.11) | collective-permute-done | bytes 32800 | tf_op jit(solution)/shard_map/ppermute | solution.py:363
  72.4 0.9 %collective-permute-start.12 = (f32[64,128]{1,0:T(8,128)S(1)}, f32[64,128]{1,0:T(8,128)S(1)}, u32[]{:S(2)}, u32[]{:S(2)}) collective-permute-start(f32[64,128]{1,0:T(8,128)S(1)} %add.29), channel_id=1, source_target_pairs={{0,4},{2,6},{4,0},{6,2},{8,12},{10,14},{12,8},{14,10},{1,5},{3,7},... | collective-permute-start | bytes 98312 | tf_op jit(solution)/shard_map/ppermute | solution.py:363
  73.3 2.8 %collective-permute-done.12 = f32[64,128]{1,0:T(8,128)S(1)} collective-permute-done((f32[64,128]{1,0:T(8,128)S(1)}, f32[64,128]{1,0:T(8,128)S(1)}, u32[]{:S(2)}, u32[]{:S(2)}) %collective-permute-start.12) | collective-permute-done | bytes 32800 | tf_op jit(solution)/shard_map/ppermute | solution.py:363
  76.1 2.4 %collective-permute-start.13 = (f32[64,128]{1,0:T(8,128)S(1)}, f32[64,128]{1,0:T(8,128)S(1)}, u32[]{:S(2)}, u32[]{:S(2)}) collective-permute-start(f32[64,128]{1,0:T(8,128)S(1)} %add.30), channel_id=1, source_target_pairs={{0,12},{2,14},{4,8},{6,10},{8,4},{10,6},{12,0},{14,2},{1,13},{3,15... | collective-permute-start | bytes 98312 | tf_op jit(solution)/shard_map/ppermute | solution.py:363
  78.5 2.5 %collective-permute-done.13 = f32[64,128]{1,0:T(8,128)S(1)} collective-permute-done((f32[64,128]{1,0:T(8,128)S(1)}, f32[64,128]{1,0:T(8,128)S(1)}, u32[]{:S(2)}, u32[]{:S(2)}) %collective-permute-start.13) | collective-permute-done | bytes 32800 | tf_op jit(solution)/shard_map/ppermute | solution.py:363
  81.0 8.1 %collective-permute-start.14 = (f32[64,128]{1,0:T(8,128)S(1)}, f32[64,128]{1,0:T(8,128)S(1)}, u32[]{:S(2)}, u32[]{:S(2)}) collective-permute-start(f32[64,128]{1,0:T(8,128)S(1)} %add.31.mine), channel_id=1, source_target_pairs={{0,1},{1,0},{2,3},{3,2},{4,5},{5,4},{6,7},{7,6},{8,9},{9,8},{10,11... | collective-permute-start | bytes 98312 | tf_op jit(solution)/shard_map/ppermute | solution.py:363
  89.1 0.9 collective-permute-done.14.other
  90.0 1.0 %grams.1 = (f32[64,128]{1,0:T(8,128)}, f32[64,128]{1,0:T(8,128)}, f32[128,128]{1,0:T(8,128)}, f32[128,128]{1,0:T(8,128)}, f32[64,64]{1,0:T(8,128)}) custom-call(s32[1]{0:T(128)} %bitcast.core, f32[64,128]{1,0:T(8,128)S(1)} %add.31.mine, f32[64,128]{1,0:T(8,128)S(1)} %collective-permute-done.14.other), custom_call_target="tpu_custom_call" | custom-call | tf_op jit(solution)/shard_map/grams/pallas_call | solution.py:348
  (9 shorter events, 0.0 us)
Async XLA Ops:
  0.6 1.9 %copy-start = (bf16[64,3,8,8,128]{4,3,2,1,0:T(8,128)(2,1)S(1)}, bf16[64,3,8,8,128]{4,3,2,1,0:T(8,128)(2,1)}, u32[]{:S(2)}) copy-start(bf16[64,3,8,8,128]{4,3,2,1,0:T(8,128)(2,1)} %param.5) | copy-start | bytes 9437188
  6.6 26.4 %collective-permute-start = (bf16[192,16,128]{2,1,0:T(8,128)(2,1)}, bf16[192,16,128]{2,1,0:T(8,128)(2,1)}, u32[]{:S(2)}, u32[]{:S(2)}) collective-permute-start(bf16[192,16,128]{2,1,0:T(8,128)(2,1)} %get-tuple-element.22), channel_id=1, source_target_pairs={{0,1},{1,2},{2,3},{3,4},{4,5},{5,6},{6,7},{7,8},{8,9},{9,10},{10,1... | collective-permute-start | bytes 2359304 | tf_op jit(solution)/shard_map/ppermute | solution.py:359
  9.6 23.4 %collective-permute-start.1 = (bf16[192,16,128]{2,1,0:T(8,128)(2,1)}, bf16[192,16,128]{2,1,0:T(8,128)(2,1)}, u32[]{:S(2)}, u32[]{:S(2)}) collective-permute-start(bf16[192,16,128]{2,1,0:T(8,128)(2,1)} %get-tuple-element.23), channel_id=1, source_target_pairs={{0,15},{1,0},{2,1},{3,2},{4,3},{5,4},{6,5},{7,6},{8,7},{9,8},{10,9... | collective-permute-start | bytes 2359304 | tf_op jit(solution)/shard_map/ppermute | solution.py:359
  12.1 32.5 %collective-permute-start.4 = (bf16[192,16,128]{2,1,0:T(8,128)(2,1)}, bf16[192,16,128]{2,1,0:T(8,128)(2,1)}, u32[]{:S(2)}, u32[]{:S(2)}) collective-permute-start(bf16[192,16,128]{2,1,0:T(8,128)(2,1)} %get-tuple-element.27), channel_id=1, source_target_pairs={{0,16},{16,32},{32,48},{1,17},{17,33},{33,49},{2,18},{18,34},{34,5... | collective-permute-start | bytes 2359304 | tf_op jit(solution)/shard_map/ppermute | solution.py:359
  16.1 28.5 %collective-permute-start.5 = (bf16[192,16,128]{2,1,0:T(8,128)(2,1)}, bf16[192,16,128]{2,1,0:T(8,128)(2,1)}, u32[]{:S(2)}, u32[]{:S(2)}) collective-permute-start(bf16[192,16,128]{2,1,0:T(8,128)(2,1)} %get-tuple-element.28), channel_id=1, source_target_pairs={{16,0},{32,16},{48,32},{17,1},{33,17},{49,33},{18,2},{34,18},{50,3... | collective-permute-start | bytes 2359304 | tf_op jit(solution)/shard_map/ppermute | solution.py:359
  17.4 5.2 %collective-permute-start.2 = (bf16[24,16,128]{2,1,0:T(8,128)(2,1)S(1)}, bf16[24,16,128]{2,1,0:T(8,128)(2,1)S(1)}, u32[]{:S(2)}, u32[]{:S(2)}) collective-permute-start(bf16[24,16,128]{2,1,0:T(8,128)(2,1)S(1)} %get-tuple-element.24), channel_id=1, source_target_pairs={{0,64},{64,128},{128,192},{192,0},{1,65},{65,129},{129,193},{193,1... | collective-permute-start | bytes 294920 | tf_op jit(solution)/shard_map/ppermute | solution.py:359
  22.6 10.4 %collective-permute-start.3 = (bf16[24,16,128]{2,1,0:T(8,128)(2,1)}, bf16[24,16,128]{2,1,0:T(8,128)(2,1)}, u32[]{:S(2)}, u32[]{:S(2)}) collective-permute-start(bf16[24,16,128]{2,1,0:T(8,128)(2,1)} %get-tuple-element.25), channel_id=1, source_target_pairs={{0,192},{64,0},{128,64},{192,128},{1,193},{65,1},{129,65},{193,129... | collective-permute-start | bytes 294920 | tf_op jit(solution)/shard_map/ppermute | solution.py:359
  23.8 9.2 %copy-start.1 = (bf16[64,3,8,8,128]{4,3,2,1,0:T(8,128)(2,1)S(1)}, bf16[64,3,8,8,128]{4,3,2,1,0:T(8,128)(2,1)}, u32[]{:S(2)}) copy-start(bf16[64,3,8,8,128]{4,3,2,1,0:T(8,128)(2,1)} %param.5) | copy-start | bytes 9437188
  23.8 9.2 %copy-start.4 = (bf16[256,256]{1,0:T(8,128)(2,1)S(1)}, bf16[256,256]{1,0:T(8,128)(2,1)}, u32[]{:S(2)}) copy-start(bf16[256,256]{1,0:T(8,128)(2,1)} %constant.13.clone.stream) | copy-start | bytes 393220
  23.8 9.2 %copy-start.5 = (bf16[8,64,128]{2,1,0:T(8,128)(2,1)S(1)}, bf16[8,64,128]{2,1,0:T(8,128)(2,1)}, u32[]{:S(2)}) copy-start(bf16[8,64,128]{2,1,0:T(8,128)(2,1)} %constant.14.clone.masks) | copy-start | bytes 393220
  30.3 2.7 %copy-start.2 = (bf16[24,128,8,128]{3,2,1,0:T(8,128)(2,1)}, bf16[24,128,8,128]{3,2,1,0:T(8,128)(2,1)S(1)}, u32[]{:S(2)}) copy-start(bf16[24,128,8,128]{3,2,1,0:T(8,128)(2,1)S(1)} %get-tuple-element.21.modes_in) | copy-start | bytes 18874372
  33.0 2.8 %copy-start.3 = (bf16[24,128,8,128]{3,2,1,0:T(8,128)(2,1)S(1)}, bf16[24,128,8,128]{3,2,1,0:T(8,128)(2,1)}, u32[]{:S(2)}) copy-start(bf16[24,128,8,128]{3,2,1,0:T(8,128)(2,1)} %copy-done.2) | copy-start | bytes 18874372
  35.8 0.8 copy-start.6
  49.0 6.0 %collective-permute-start.6 = (f32[64,128]{1,0:T(8,128)S(1)}, f32[64,128]{1,0:T(8,128)S(1)}, u32[]{:S(2)}, u32[]{:S(2)}) collective-permute-start(f32[64,128]{1,0:T(8,128)S(1)} %broadcast_select_fusion), channel_id=1, source_target_pairs={{0,1},{1,0},{2,3},{3,2},{4,5},{5,4},{6,7},{7,6},{8,9},{9,8},{10,11... | collective-permute-start | bytes 98312 | tf_op jit(solution)/shard_map/ppermute | solution.py:363
  55.1 2.8 %collective-permute-start.7 = (f32[64,128]{1,0:T(8,128)S(1)}, f32[64,128]{1,0:T(8,128)S(1)}, u32[]{:S(2)}, u32[]{:S(2)}) collective-permute-start(f32[64,128]{1,0:T(8,128)S(1)} %select_add_fusion), channel_id=1, source_target_pairs={{0,64},{64,0},{128,192},{192,128},{1,65},{65,1},{129,193},{193,129... | collective-permute-start | bytes 98312 | tf_op jit(solution)/shard_map/ppermute | solution.py:363
  57.8 4.0 %collective-permute-start.8 = (f32[64,128]{1,0:T(8,128)S(1)}, f32[64,128]{1,0:T(8,128)S(1)}, u32[]{:S(2)}, u32[]{:S(2)}) collective-permute-start(f32[64,128]{1,0:T(8,128)S(1)} %add.25), channel_id=1, source_target_pairs={{0,192},{64,128},{128,64},{192,0},{1,193},{65,129},{129,65},{193,1... | collective-permute-start | bytes 98312 | tf_op jit(solution)/shard_map/ppermute | solution.py:363
  61.8 3.7 %collective-permute-start.9 = (f32[64,128]{1,0:T(8,128)S(1)}, f32[64,128]{1,0:T(8,128)S(1)}, u32[]{:S(2)}, u32[]{:S(2)}) collective-permute-start(f32[64,128]{1,0:T(8,128)S(1)} %add.26), channel_id=1, source_target_pairs={{0,16},{16,0},{32,48},{48,32},{1,17},{17,1},{33,49},{49,33},{2,18}... | collective-permute-start | bytes 98312 | tf_op jit(solution)/shard_map/ppermute | solution.py:363
  65.5 4.1 %collective-permute-start.10 = (f32[64,128]{1,0:T(8,128)S(1)}, f32[64,128]{1,0:T(8,128)S(1)}, u32[]{:S(2)}, u32[]{:S(2)}) collective-permute-start(f32[64,128]{1,0:T(8,128)S(1)} %add.27), channel_id=1, source_target_pairs={{0,48},{16,32},{32,16},{48,0},{1,49},{17,33},{33,17},{49,1},{2,50}... | collective-permute-start | bytes 98312 | tf_op jit(solution)/shard_map/ppermute | solution.py:363
  69.6 2.8 %collective-permute-start.11 = (f32[64,128]{1,0:T(8,128)S(1)}, f32[64,128]{1,0:T(8,128)S(1)}, u32[]{:S(2)}, u32[]{:S(2)}) collective-permute-start(f32[64,128]{1,0:T(8,128)S(1)} %add.28), channel_id=1, source_target_pairs={{0,2},{2,0},{4,6},{6,4},{8,10},{10,8},{12,14},{14,12},{1,3},{3,1},... | collective-permute-start | bytes 98312 | tf_op jit(solution)/shard_map/ppermute | solution.py:363
  72.4 3.7 %collective-permute-start.12 = (f32[64,128]{1,0:T(8,128)S(1)}, f32[64,128]{1,0:T(8,128)S(1)}, u32[]{:S(2)}, u32[]{:S(2)}) collective-permute-start(f32[64,128]{1,0:T(8,128)S(1)} %add.29), channel_id=1, source_target_pairs={{0,4},{2,6},{4,0},{6,2},{8,12},{10,14},{12,8},{14,10},{1,5},{3,7},... | collective-permute-start | bytes 98312 | tf_op jit(solution)/shard_map/ppermute | solution.py:363
  76.1 4.9 %collective-permute-start.13 = (f32[64,128]{1,0:T(8,128)S(1)}, f32[64,128]{1,0:T(8,128)S(1)}, u32[]{:S(2)}, u32[]{:S(2)}) collective-permute-start(f32[64,128]{1,0:T(8,128)S(1)} %add.30), channel_id=1, source_target_pairs={{0,12},{2,14},{4,8},{6,10},{8,4},{10,6},{12,0},{14,2},{1,13},{3,15... | collective-permute-start | bytes 98312 | tf_op jit(solution)/shard_map/ppermute | solution.py:363
  81.0 8.9 %collective-permute-start.14 = (f32[64,128]{1,0:T(8,128)S(1)}, f32[64,128]{1,0:T(8,128)S(1)}, u32[]{:S(2)}, u32[]{:S(2)}) collective-permute-start(f32[64,128]{1,0:T(8,128)S(1)} %add.31.mine), channel_id=1, source_target_pairs={{0,1},{1,0},{2,3},{3,2},{4,5},{5,4},{6,7},{7,6},{8,9},{9,8},{10,11... | collective-permute-start | bytes 98312 | tf_op jit(solution)/shard_map/ppermute | solution.py:363

commit v3 on v2

--- a/solution.py
+++ b/solution.py
@@ -81,28 +81,30 @@
     return pl.BlockSpec(memory_space=pltpu.VMEM)
 
 
-def wall_pack_body(snap, low, high, low_in, high_in, sems):
-    ends = ((0, low, low_in), (48, high, high_in))
-    reads = [pltpu.make_async_copy(snap.at[:, pl.ds(row, 16)], at, sems.at[i]) for i, (row, _, at) in enumerate(ends)]
-    writes = [pltpu.make_async_copy(at, to, sems.at[2 + i]) for i, (_, to, at) in enumerate(ends)]
+def wall_pack_body(snap, low, high, units, sems):
+    parts = (pl.ds(0, 16), pl.ds(48, 16), pl.ds(16, 32))
+    reads = [pltpu.make_async_copy(snap.at[:, at], units.at[:, at], sems.at[i]) for i, at in enumerate(parts)]
+    writes = [
+        pltpu.make_async_copy(units.at[:, at], to, sems.at[3 + i]) for i, (at, to) in enumerate(zip(parts, (low, high)))
+    ]
     for c in reads:
         c.start()
     for r, w in zip(reads, writes):
         r.wait()
         w.start()
+    reads[2].wait()
     for w in writes:
         w.wait()
 
 
 def wall_pack(snap):
     shape = jax.ShapeDtypeStruct((192, 16, 128), BF16)
-    block = pltpu.VMEM((192, 16, 128), BF16)
     return pl.pallas_call(
         wall_pack_body,
-        out_shape=(shape, shape),
+        out_shape=(shape, shape, jax.ShapeDtypeStruct((192, 64, 128), BF16)),
         in_specs=[in_hbm()],
-        out_specs=(in_hbm(), in_hbm()),
-        scratch_shapes=[block, block, pltpu.SemaphoreType.DMA((4,))],
+        out_specs=(in_hbm(), in_hbm(), resident()),
+        scratch_shapes=[pltpu.SemaphoreType.DMA((5,))],
         compiler_params=pltpu.CompilerParams(vmem_limit_bytes=VMEM_LIMIT),
         name="wall_pack",
     )(from_hbm(snap))
@@ -152,26 +154,27 @@
     )(in_vmem(snap))
 
 
-def same_span(total, out):
-    lanes = lax.broadcasted_iota(jnp.int32, (128, 128), 1) % 8
+def same_span(total, half, out):
+    lanes = lax.broadcasted_iota(jnp.int32, (64, 128), 1) % 8
     s = lax.broadcasted_iota(jnp.int32, (16, 128), 0)
     at = lax.broadcasted_iota(jnp.int32, (16, 128), 1)
     group = (at // 8 == s).astype(F32)
     for block in range(4):
-        kept = total[block, pl.ds(0, 128, stride=8), :]
+        kept = total[block, pl.ds(512 * half, 64, stride=8), :]
         for z in range(1, 8):
-            kept = jnp.where(lanes == z, total[block, pl.ds(z, 128, stride=8), :], kept)
-        out[16 * block : 16 * block + 16] = lax.dot_general(
+            kept = jnp.where(lanes == z, total[block, pl.ds(512 * half + z, 64, stride=8), :], kept)
+        out[16 * block : 16 * block + 16, 64 * half : 64 * half + 64] = lax.dot_general(
             group, kept, NT, precision=HIGH, preferred_element_type=F32
         )
 
 
-def add_products(modes, planes, data, total, base):
-    a = jnp.concatenate([modes[k].reshape(1024, 128) for k in planes], axis=1)
+def add_products(modes, half, planes, data, total, base):
+    a = jnp.concatenate([modes[k, 64 * half : 64 * half + 64].reshape(512, 128) for k in planes], axis=1)
     part = lax.dot_general(a, jnp.concatenate(data, axis=1), NT, preferred_element_type=F32)
+    rows = slice(512 * half, 512 * half + 512)
     for block in range(4):
         lanes = part[:, 128 * block : 128 * block + 128]
-        total[block] = lanes if base is None else base[block] + lanes
+        total[block, rows] = lanes if base is None else base[block, rows] + lanes
 
 
 def snap_project_body(modes, snap, out, modes_in, snap_in, total, sems):
@@ -181,12 +184,15 @@
         copies.append(pltpu.make_async_copy(snap.at[:, k], snap_in.at[k], sems.at[1, k]))
     for c in copies:
         c.start()
-    for k in range(0, 24, 4):
-        for c in copies[2 * k : 2 * k + 8]:
-            c.wait()
-        planes = range(k, k + 4)
-        add_products(modes_in, planes, [snap_in[p].reshape(512, 128) for p in planes], total, total if k else None)
-    same_span(total, out)
+    for half, size in ((0, 6), (1, 12)):
+        for k in range(0, 24, size):
+            if half == 0:
+                for c in copies[2 * k : 2 * (k + size)]:
+                    c.wait()
+            planes = range(k, k + size)
+            data = [snap_in[p].reshape(512, 128) for p in planes]
+            add_products(modes_in, half, planes, data, total, total if k else None)
+        same_span(total, half, out)
 
 
 def snap_project(modes, snap):
@@ -253,9 +259,9 @@
         return _
 
     lax.fori_loop(0, 8, block, 0)
-    for c in range(3):
-        planes = range(8 * c + 2, 8 * c + 6)
-        add_products(modes_in, planes, [field[4 * c + k] for k in range(4)], total, total if c else None)
+    planes = [8 * c + y for c in range(3) for y in range(2, 6)]
+    for half in range(2):
+        add_products(modes_in, half, planes, [field[k] for k in range(12)], total, None)
 
 
 def feature_project(modes_in, snap, z_low, z_high, x_low, x_high):
@@ -276,6 +282,8 @@
 
 def edge_body(modes_in, snap, edges, y_low, y_high, inner, out, field, total):
     k = VISCOSITY / 12.0
+    row = lax.axis_index("gy")
+    has_below, has_above = row > 0, row < 3
 
     def block(step, _):
         base = 12 * step
@@ -289,8 +297,8 @@
             row = []
             for c in range(3):
                 u = base + 3 * i + c
-                below = y_low[u].astype(F32).reshape(2, 8, 128)
-                above = y_high[u].astype(F32).reshape(2, 8, 128)
+                below = jnp.where(has_below, y_low[u].astype(F32), 0.0).reshape(2, 8, 128)
+                above = jnp.where(has_above, y_high[u].astype(F32), 0.0).reshape(2, 8, 128)
                 value = edges[u]
                 row.append(
                     jnp.stack(
@@ -311,10 +319,10 @@
         return _
 
     lax.fori_loop(0, 16, block, 0, unroll=4)
-    for c in range(3):
-        planes = [8 * c, 8 * c + 1, 8 * c + 6, 8 * c + 7]
-        add_products(modes_in, planes, [field[4 * c + p] for p in range(4)], total, total if c else inner)
-    same_span(total, out)
+    planes = [8 * c + y for c in range(3) for y in (0, 1, 6, 7)]
+    for half in range(2):
+        add_products(modes_in, half, planes, [field[k] for k in range(12)], total, inner)
+        same_span(total, half, out)
 
 
 def edge_project(modes_in, snap, edges, y_low, y_high, inner):
@@ -329,8 +337,8 @@
     )(*map(in_vmem, (modes_in, snap, edges, y_low, y_high, inner)))
 
 
-def gram_body(core, mine, other, snap_out, feature_out, gram_snap, gram_feature, gram_quad):
-    first = core[0] == 0
+def gram_body(mine, other, snap_out, feature_out, gram_snap, gram_feature, gram_quad):
+    first = lax.axis_index("gz_1") == 0
     rs = jnp.where(first, mine[...], other[...])
     rf = jnp.where(first, other[...], mine[...])
     snap_out[...] = rs
@@ -342,25 +350,28 @@
     gram_quad[...] = products * products
 
 
-def grams(core, mine, other):
+def grams(mine, other):
     shape = lambda *s: jax.ShapeDtypeStruct(s, F32)
     vmem = pl.BlockSpec(memory_space=pltpu.VMEM)
     return pl.pallas_call(
         gram_body,
-        in_specs=[pl.BlockSpec(memory_space=pltpu.SMEM), vmem, vmem],
+        in_specs=[vmem, vmem],
         out_shape=(shape(64, 128), shape(64, 128), shape(128, 128), shape(128, 128), shape(64, 64)),
         compiler_params=pltpu.CompilerParams(vmem_limit_bytes=VMEM_LIMIT),
         name="grams",
-    )(core, in_vmem(mine), in_vmem(other))
-
-
-def shifted(value, axis, count, by, closed):
-    pairs = [(i, (i + by) % count) for i in range(count) if closed or 0 <= i + by < count]
-    return lax.ppermute(value, axis, pairs)
+    )(in_vmem(mine), in_vmem(other))
+
+
+def shifted(value, axis, count, by):
+    return lax.ppermute(value, axis, [(i, (i + by) % count) for i in range(count)])
 
 
 def swapped(value, axis, partners):
     return lax.ppermute(value, axis, list(enumerate(partners)))
+
+
+def other_core(value):
+    return lax.ppermute(value, "gz_1", [(0, 1), (1, 0)])
 
 
 ROUNDS = (
@@ -375,26 +386,23 @@
 
 
 def shards(snapshots, modes):
-    units = snapshots.reshape(192, 64, 128)
-    low, high = wall_pack(units)
-    y_low = shifted(high, "gy", 4, 1, False)
-    y_high = shifted(low, "gy", 4, -1, False)
+    low, high, units = wall_pack(snapshots.reshape(192, 64, 128))
+    y_low = shifted(high, "gy", 4, 1)
+    y_high = shifted(low, "gy", 4, -1)
     low, high, right, left = side_pack(units)
-    z_low = shifted(high, GZ, 16, 1, True)
-    z_high = shifted(low, GZ, 16, -1, True)
-    x_low = shifted(right, "gx", 4, 1, True)
-    x_high = shifted(left, "gx", 4, -1, True)
+    z_low = shifted(high, GZ, 16, 1)
+    z_high = shifted(low, GZ, 16, -1)
+    x_low = shifted(right, "gx", 4, 1)
+    x_high = shifted(left, "gx", 4, -1)
     snap_part, modes_in = snap_project(modes.reshape(128, 24, 8, 128), snapshots.reshape(64, 24, 8, 128))
     inner, edges = feature_project(modes_in, units, z_low, z_high, x_low, x_high)
     feature_part = edge_project(modes_in, units, edges, y_low, y_high, inner)
     core = lax.axis_index("gz_1")
     mine = jnp.where(core == 0, snap_part, feature_part)
-    total = mine + swapped(jnp.where(core == 0, feature_part, snap_part), "gz_1", (1, 0))
+    total = mine + other_core(jnp.where(core == 0, feature_part, snap_part))
     for axis, partners in ROUNDS:
         total = total + swapped(total, axis, partners)
-    rs, rf, gram_snap, gram_feature, gram_quad = grams(
-        core.reshape(1).astype(jnp.int32), total, swapped(total, "gz_1", (1, 0))
-    )
+    rs, rf, gram_snap, gram_feature, gram_quad = grams(total, other_core(total))
     return rs.T, rf.T, gram_snap, gram_feature, gram_quad
 
 

time: 91.3 us -> 87.4 us (0.957)
  starting transfers between devices: 33.5 us -> 27.6 us
  waiting for transfers between devices: 22.2 us -> 24.9 us
  local copies, waits for them, and re-layouts: 8.08 us -> 6.2 us
  Pallas kernels: 26.3 us -> 27.7 us
    ppermute x9 -> x7, starting transfers between devices: 22.5 us -> 5.68 us  [swapped(): return lax.ppermute(value, axis, list(enumerate(partners)))]
    ppermute x6 -> x8, starting transfers between devices: 11 us -> 21.9 us  [the longest x2 13.8 us: other_core(): return lax.ppermute(value, 'gz_1', [(0, 1), (1, 0)])]
    unnamed x14 -> x10, local copies, waits for them, and re-layouts: 8.08 us -> 6.2 us
    ppermute x6 -> x8, waiting for transfers between devices: 3.88 us -> 5.72 us  [the longest x6 4 us: shifted(): lax.ppermute(value, axis, [(i, (i + by) % count) for i in range(count)])]
    pallas_call x1, Pallas kernels: 6.48 us -> 7.51 us  [snap_project(): pl.pallas_call(snap_project_body, out_shape=(jax.ShapeDtypeStruct((64, 12...]
    ppermute x9 -> x7, waiting for transfers between devices: 18.4 us -> 19.2 us  [swapped(): return lax.ppermute(value, axis, list(enumerate(partners)))]
  transfers between devices with their start and end apart: 15 -> 15, of which waited for: 10 -> 10; matrix products, arithmetic and copies ran while one was open for 0% -> 0% of each run, Pallas kernels for 19% -> 18%
where the time goes in v3:
time: 87.4 us; the launch traced here: 87.2 us
  Pallas kernels  27.7 us (32%)
  starting transfers between devices  27.6 us (32%)
  waiting for transfers between devices  24.9 us (28%)
  local copies, waits for them, and re-layouts  6.2 us (7%)
    ppermute x7, waiting for transfers between devices, swapped(): return lax.ppermute(value, axis, list(enumerate(partners)))  19.2 us
    ppermute x2, starting transfers between devices, other_core(): return lax.ppermute(value, 'gz_1', [(0, 1), (1, 0)])  13.8 us
    ppermute x6, starting transfers between devices, shifted(): lax.ppermute(value, axis, [(i, (i + by) % count) for i in range(count)])  8.12 us
    pallas_call x1, Pallas kernels, feature_project(): pl.pallas_call(feature_body, out_shape=(jax.ShapeDtypeStruct((4, 1024, 12...  8.09 us
    pallas_call x1, Pallas kernels, snap_project(): pl.pallas_call(snap_project_body, out_shape=(jax.ShapeDtypeStruct((64, 12...  7.51 us
    unnamed x10, local copies, waits for them, and re-layouts  6.2 us
    ppermute x7, starting transfers between devices, swapped(): return lax.ppermute(value, axis, list(enumerate(partners)))  5.68 us
    pallas_call x1, Pallas kernels, edge_project(): pl.pallas_call(edge_body, out_shape=jax.ShapeDtypeStruct((64, 128), F32),...  4.74 us
  transfers between devices with their start and end apart: 15, of which 10 were waited for; matrix products, arithmetic and copies ran while one was open for 0% of the time, Pallas kernels for 18%

profile of v3, /device:TPU:1, one launch (start us, length us, event | category | flops | bytes accessed | tf_op | source)
XLA Modules:
  0.0 87.2 jit_solution(8745615462031542312)
XLA Ops:
  0.6 2.3 %wall_pack.1 = (bf16[192,16,128]{2,1,0:T(8,128)(2,1)}, bf16[192,16,128]{2,1,0:T(8,128)(2,1)}, bf16[192,64,128]{2,1,0:T(8,128)(2,1)S(1)}) custom-call(bf16[192,64,128]{2,1,0:T(8,128)(2,1)} %bitcast.5), custom_call_target="tpu_custom_call" | custom-call | tf_op jit(solution)/shard_map/wall_pack/pallas_call | solution.py:102
  3.0 4.1 %side_pack.1 = (bf16[192,16,128]{2,1,0:T(8,128)(2,1)}, bf16[192,16,128]{2,1,0:T(8,128)(2,1)}, bf16[24,16,128]{2,1,0:T(8,128)(2,1)S(1)}, bf16[24,16,128]{2,1,0:T(8,128)(2,1)}) custom-call(bf16[192,64,128]{2,1,0:T(8,128)(2,1)S(1)} %get-tuple-element.23.snap), custom_call_target="tpu_custom_call" | custom-call | tf_op jit(solution)/shard_map/side_pack/pallas_call | solution.py:147
  7.0 3.0 %collective-permute-start = (bf16[192,16,128]{2,1,0:T(8,128)(2,1)}, bf16[192,16,128]{2,1,0:T(8,128)(2,1)}, u32[]{:S(2)}, u32[]{:S(2)}) collective-permute-start(bf16[192,16,128]{2,1,0:T(8,128)(2,1)} %get-tuple-element.24), channel_id=1, source_target_pairs={{0,1},{1,2},{2,3},{3,4},{4,5},{5,6},{6,7},{7,8},{8,9},{9,10},{10,1... | collective-permute-start | bytes 2359304 | tf_op jit(solution)/shard_map/ppermute | solution.py:366
  10.1 0.2 collective-permute-start.1
  10.2 1.1 %collective-permute-start.4 = (bf16[192,16,128]{2,1,0:T(8,128)(2,1)}, bf16[192,16,128]{2,1,0:T(8,128)(2,1)}, u32[]{:S(2)}, u32[]{:S(2)}) collective-permute-start(bf16[192,16,128]{2,1,0:T(8,128)(2,1)} %get-tuple-element.29), channel_id=1, source_target_pairs={{0,16},{16,32},{32,48},{48,0},{1,17},{17,33},{33,49},{49,1},{2,18}... | collective-permute-start | bytes 2359304 | tf_op jit(solution)/shard_map/ppermute | solution.py:366
  11.4 1.6 %collective-permute-start.5 = (bf16[192,16,128]{2,1,0:T(8,128)(2,1)}, bf16[192,16,128]{2,1,0:T(8,128)(2,1)}, u32[]{:S(2)}, u32[]{:S(2)}) collective-permute-start(bf16[192,16,128]{2,1,0:T(8,128)(2,1)} %get-tuple-element.30), channel_id=1, source_target_pairs={{0,48},{16,0},{32,16},{48,32},{1,49},{17,1},{33,17},{49,33},{2,50}... | collective-permute-start | bytes 2359304 | tf_op jit(solution)/shard_map/ppermute | solution.py:366
  12.9 1.1 %collective-permute-start.2 = (bf16[24,16,128]{2,1,0:T(8,128)(2,1)S(1)}, bf16[24,16,128]{2,1,0:T(8,128)(2,1)S(1)}, u32[]{:S(2)}, u32[]{:S(2)}) collective-permute-start(bf16[24,16,128]{2,1,0:T(8,128)(2,1)S(1)} %get-tuple-element.26), channel_id=1, source_target_pairs={{0,64},{64,128},{128,192},{192,0},{1,65},{65,129},{129,193},{193,1... | collective-permute-start | bytes 294920 | tf_op jit(solution)/shard_map/ppermute | solution.py:366
  14.0 4.0 %collective-permute-done.2.x_low = bf16[24,16,128]{2,1,0:T(8,128)(2,1)S(1)} collective-permute-done((bf16[24,16,128]{2,1,0:T(8,128)(2,1)S(1)}, bf16[24,16,128]{2,1,0:T(8,128)(2,1)S(1)}, u32[]{:S(2)}, u32[]{:S(2)}) %collective-permute-start.2) | collective-permute-done | bytes 98336 | tf_op jit(solution)/shard_map/ppermute | solution.py:366
  18.0 1.1 %collective-permute-start.3 = (bf16[24,16,128]{2,1,0:T(8,128)(2,1)}, bf16[24,16,128]{2,1,0:T(8,128)(2,1)}, u32[]{:S(2)}, u32[]{:S(2)}) collective-permute-start(bf16[24,16,128]{2,1,0:T(8,128)(2,1)} %get-tuple-element.27), channel_id=1, source_target_pairs={{0,192},{64,0},{128,64},{192,128},{1,193},{65,1},{129,65},{193,129... | collective-permute-start | bytes 294920 | tf_op jit(solution)/shard_map/ppermute | solution.py:366
  19.1 0.0 copy-start.2
  19.1 0.0 copy-start.3
  19.1 7.5 %snap_project.1 = (f32[64,128]{1,0:T(8,128)S(1)}, bf16[24,128,8,128]{3,2,1,0:T(8,128)(2,1)S(1)}) custom-call(bf16[128,24,8,128]{3,2,1,0:T(8,128)(2,1)} %bitcast.7, bf16[64,24,8,128]{3,2,1,0:T(8,128)(2,1)} %bitcast.6), custom_call_target="tpu_custom_call" | custom-call | tf_op jit(solution)/shard_map/snap_project/pallas_call | solution.py:199
  26.7 0.0 copy-start
  26.7 2.7 %copy-done = bf16[24,128,8,128]{3,2,1,0:T(8,128)(2,1)} copy-done((bf16[24,128,8,128]{3,2,1,0:T(8,128)(2,1)}, bf16[24,128,8,128]{3,2,1,0:T(8,128)(2,1)S(1)}, u32[]{:S(2)}) %copy-start) | copy-done | bytes 6291480
  29.3 0.0 collective-permute-done.3.x_high
  29.3 0.0 collective-permute-done.z_low
  29.3 0.0 collective-permute-done.1.z_high
  29.3 0.0 copy-done.2
  29.4 0.0 copy-done.3
  29.4 0.0 copy-start.1
  29.4 2.8 %copy-done.1 = bf16[24,128,8,128]{3,2,1,0:T(8,128)(2,1)S(1)} copy-done((bf16[24,128,8,128]{3,2,1,0:T(8,128)(2,1)S(1)}, bf16[24,128,8,128]{3,2,1,0:T(8,128)(2,1)}, u32[]{:S(2)}) %copy-start.1) | copy-done | bytes 6291480
  32.1 0.0 copy-start.4
  32.1 0.8 copy-done.4
  32.9 8.1 %feature_project.1 = (f32[4,1024,128]{2,1,0:T(8,128)S(1)}, f32[192,4,8,128]{3,2,1,0:T(8,128)S(1)}) custom-call(bf16[24,128,8,128]{3,2,1,0:T(8,128)(2,1)S(1)} %copy-done.1, bf16[192,64,128]{2,1,0:T(8,128)(2,1)S(1)} %get-tuple-element.23.snap, bf16[192,16,128]{2,1,0:T(8,128)(2,1)} %collective-permute-done.z_low, ...), custom_call_target="tpu_custom_call" | custom-call | tf_op jit(solution)/shard_map/feature_project/pallas_call | solution.py:269
  41.0 0.0 collective-permute-done.4.y_low
  41.0 0.0 collective-permute-done.5.y_high
  41.0 4.7 %edge_project.1 = f32[64,128]{1,0:T(8,128)S(1)} custom-call(bf16[24,128,8,128]{3,2,1,0:T(8,128)(2,1)S(1)} %copy-done.1, bf16[192,64,128]{2,1,0:T(8,128)(2,1)S(1)} %get-tuple-element.23.snap, f32[192,4,8,128]{3,2,1,0:T(8,128)S(1)} %get-tuple-element.28.edges, bf16[192,16,128]{2,1,0:T(8,128)(2,1)} %collective-permute-done.4.y_low, ...), custom_call_target="tpu_custom_call" | custom-call | tf_op jit(solution)/shard_map/edge_project/pallas_call | solution.py:329
  45.8 5.4 %collective-permute-start.6 = (f32[64,128]{1,0:T(8,128)S(1)}, f32[64,128]{1,0:T(8,128)S(1)}, u32[]{:S(2)}, u32[]{:S(2)}) collective-permute-start(f32[64,128]{1,0:T(8,128)S(1)} %broadcast_select_fusion), channel_id=1, source_target_pairs={{0,1},{1,0},{2,3},{3,2},{4,5},{5,4},{6,7},{7,6},{8,9},{9,8},{10,11... | collective-permute-start | bytes 98312 | tf_op jit(solution)/shard_map/ppermute | solution.py:374
  51.2 0.9 collective-permute-done.6
  52.0 0.2 collective-permute-start.7
  52.2 2.6 %collective-permute-done.7 = f32[64,128]{1,0:T(8,128)S(1)} collective-permute-done((f32[64,128]{1,0:T(8,128)S(1)}, f32[64,128]{1,0:T(8,128)S(1)}, u32[]{:S(2)}, u32[]{:S(2)}) %collective-permute-start.7) | collective-permute-done | bytes 32800 | tf_op jit(solution)/shard_map/ppermute | solution.py:370
  54.8 0.6 collective-permute-start.8
  55.4 3.4 %collective-permute-done.8 = f32[64,128]{1,0:T(8,128)S(1)} collective-permute-done((f32[64,128]{1,0:T(8,128)S(1)}, f32[64,128]{1,0:T(8,128)S(1)}, u32[]{:S(2)}, u32[]{:S(2)}) %collective-permute-start.8) | collective-permute-done | bytes 32800 | tf_op jit(solution)/shard_map/ppermute | solution.py:370
  58.8 0.1 collective-permute-start.9
  58.9 2.7 %collective-permute-done.9 = f32[64,128]{1,0:T(8,128)S(1)} collective-permute-done((f32[64,128]{1,0:T(8,128)S(1)}, f32[64,128]{1,0:T(8,128)S(1)}, u32[]{:S(2)}, u32[]{:S(2)}) %collective-permute-start.9) | collective-permute-done | bytes 32800 | tf_op jit(solution)/shard_map/ppermute | solution.py:370
  61.6 1.5 %collective-permute-start.10 = (f32[64,128]{1,0:T(8,128)S(1)}, f32[64,128]{1,0:T(8,128)S(1)}, u32[]{:S(2)}, u32[]{:S(2)}) collective-permute-start(f32[64,128]{1,0:T(8,128)S(1)} %add.27), channel_id=1, source_target_pairs={{0,48},{16,32},{32,16},{48,0},{1,49},{17,33},{33,17},{49,1},{2,50}... | collective-permute-start | bytes 98312 | tf_op jit(solution)/shard_map/ppermute | solution.py:370
  63.1 2.5 %collective-permute-done.10 = f32[64,128]{1,0:T(8,128)S(1)} collective-permute-done((f32[64,128]{1,0:T(8,128)S(1)}, f32[64,128]{1,0:T(8,128)S(1)}, u32[]{:S(2)}, u32[]{:S(2)}) %collective-permute-start.10) | collective-permute-done | bytes 32800 | tf_op jit(solution)/shard_map/ppermute | solution.py:370
  65.5 0.0 collective-permute-start.11
  65.5 2.8 %collective-permute-done.11 = f32[64,128]{1,0:T(8,128)S(1)} collective-permute-done((f32[64,128]{1,0:T(8,128)S(1)}, f32[64,128]{1,0:T(8,128)S(1)}, u32[]{:S(2)}, u32[]{:S(2)}) %collective-permute-start.11) | collective-permute-done | bytes 32800 | tf_op jit(solution)/shard_map/ppermute | solution.py:370
  68.3 0.9 %collective-permute-start.12 = (f32[64,128]{1,0:T(8,128)S(1)}, f32[64,128]{1,0:T(8,128)S(1)}, u32[]{:S(2)}, u32[]{:S(2)}) collective-permute-start(f32[64,128]{1,0:T(8,128)S(1)} %add.29), channel_id=1, source_target_pairs={{0,4},{2,6},{4,0},{6,2},{8,12},{10,14},{12,8},{14,10},{1,5},{3,7},... | collective-permute-start | bytes 98312 | tf_op jit(solution)/shard_map/ppermute | solution.py:370
  69.2 2.8 %collective-permute-done.12 = f32[64,128]{1,0:T(8,128)S(1)} collective-permute-done((f32[64,128]{1,0:T(8,128)S(1)}, f32[64,128]{1,0:T(8,128)S(1)}, u32[]{:S(2)}, u32[]{:S(2)}) %collective-permute-start.12) | collective-permute-done | bytes 32800 | tf_op jit(solution)/shard_map/ppermute | solution.py:370
  72.1 2.4 %collective-permute-start.13 = (f32[64,128]{1,0:T(8,128)S(1)}, f32[64,128]{1,0:T(8,128)S(1)}, u32[]{:S(2)}, u32[]{:S(2)}) collective-permute-start(f32[64,128]{1,0:T(8,128)S(1)} %add.30), channel_id=1, source_target_pairs={{0,12},{2,14},{4,8},{6,10},{8,4},{10,6},{12,0},{14,2},{1,13},{3,15... | collective-permute-start | bytes 98312 | tf_op jit(solution)/shard_map/ppermute | solution.py:370
  74.5 2.5 %collective-permute-done.13 = f32[64,128]{1,0:T(8,128)S(1)} collective-permute-done((f32[64,128]{1,0:T(8,128)S(1)}, f32[64,128]{1,0:T(8,128)S(1)}, u32[]{:S(2)}, u32[]{:S(2)}) %collective-permute-start.13) | collective-permute-done | bytes 32800 | tf_op jit(solution)/shard_map/ppermute | solution.py:370
  76.9 8.4 %collective-permute-start.14 = (f32[64,128]{1,0:T(8,128)S(1)}, f32[64,128]{1,0:T(8,128)S(1)}, u32[]{:S(2)}, u32[]{:S(2)}) collective-permute-start(f32[64,128]{1,0:T(8,128)S(1)} %add.31.mine), channel_id=1, source_target_pairs={{0,1},{1,0},{2,3},{3,2},{4,5},{5,4},{6,7},{7,6},{8,9},{9,8},{10,11... | collective-permute-start | bytes 98312 | tf_op jit(solution)/shard_map/ppermute | solution.py:374
  85.3 0.9 collective-permute-done.14.other
  86.2 1.0 %grams.1 = (f32[64,128]{1,0:T(8,128)}, f32[64,128]{1,0:T(8,128)}, f32[128,128]{1,0:T(8,128)}, f32[128,128]{1,0:T(8,128)}, f32[64,64]{1,0:T(8,128)}) custom-call(f32[64,128]{1,0:T(8,128)S(1)} %add.31.mine, f32[64,128]{1,0:T(8,128)S(1)} %collective-permute-done.14.other), custom_call_target="tpu_custom_call" | custom-call | tf_op jit(solution)/shard_map/grams/pallas_call | solution.py:356
  (9 shorter events, 0.1 us)
Async XLA Ops:
  7.0 22.3 %collective-permute-start = (bf16[192,16,128]{2,1,0:T(8,128)(2,1)}, bf16[192,16,128]{2,1,0:T(8,128)(2,1)}, u32[]{:S(2)}, u32[]{:S(2)}) collective-permute-start(bf16[192,16,128]{2,1,0:T(8,128)(2,1)} %get-tuple-element.24), channel_id=1, source_target_pairs={{0,1},{1,2},{2,3},{3,4},{4,5},{5,6},{6,7},{7,8},{8,9},{9,10},{10,1... | collective-permute-start | bytes 2359304 | tf_op jit(solution)/shard_map/ppermute | solution.py:366
  10.1 19.3 %collective-permute-start.1 = (bf16[192,16,128]{2,1,0:T(8,128)(2,1)}, bf16[192,16,128]{2,1,0:T(8,128)(2,1)}, u32[]{:S(2)}, u32[]{:S(2)}) collective-permute-start(bf16[192,16,128]{2,1,0:T(8,128)(2,1)} %get-tuple-element.25), channel_id=1, source_target_pairs={{0,15},{1,0},{2,1},{3,2},{4,3},{5,4},{6,5},{7,6},{8,7},{9,8},{10,9... | collective-permute-start | bytes 2359304 | tf_op jit(solution)/shard_map/ppermute | solution.py:366
  10.2 30.8 %collective-permute-start.4 = (bf16[192,16,128]{2,1,0:T(8,128)(2,1)}, bf16[192,16,128]{2,1,0:T(8,128)(2,1)}, u32[]{:S(2)}, u32[]{:S(2)}) collective-permute-start(bf16[192,16,128]{2,1,0:T(8,128)(2,1)} %get-tuple-element.29), channel_id=1, source_target_pairs={{0,16},{16,32},{32,48},{48,0},{1,17},{17,33},{33,49},{49,1},{2,18}... | collective-permute-start | bytes 2359304 | tf_op jit(solution)/shard_map/ppermute | solution.py:366
  11.4 29.7 %collective-permute-start.5 = (bf16[192,16,128]{2,1,0:T(8,128)(2,1)}, bf16[192,16,128]{2,1,0:T(8,128)(2,1)}, u32[]{:S(2)}, u32[]{:S(2)}) collective-permute-start(bf16[192,16,128]{2,1,0:T(8,128)(2,1)} %get-tuple-element.30), channel_id=1, source_target_pairs={{0,48},{16,0},{32,16},{48,32},{1,49},{17,1},{33,17},{49,33},{2,50}... | collective-permute-start | bytes 2359304 | tf_op jit(solution)/shard_map/ppermute | solution.py:366
  12.9 5.1 %collective-permute-start.2 = (bf16[24,16,128]{2,1,0:T(8,128)(2,1)S(1)}, bf16[24,16,128]{2,1,0:T(8,128)(2,1)S(1)}, u32[]{:S(2)}, u32[]{:S(2)}) collective-permute-start(bf16[24,16,128]{2,1,0:T(8,128)(2,1)S(1)} %get-tuple-element.26), channel_id=1, source_target_pairs={{0,64},{64,128},{128,192},{192,0},{1,65},{65,129},{129,193},{193,1... | collective-permute-start | bytes 294920 | tf_op jit(solution)/shard_map/ppermute | solution.py:366
  18.0 11.3 %collective-permute-start.3 = (bf16[24,16,128]{2,1,0:T(8,128)(2,1)}, bf16[24,16,128]{2,1,0:T(8,128)(2,1)}, u32[]{:S(2)}, u32[]{:S(2)}) collective-permute-start(bf16[24,16,128]{2,1,0:T(8,128)(2,1)} %get-tuple-element.27), channel_id=1, source_target_pairs={{0,192},{64,0},{128,64},{192,128},{1,193},{65,1},{129,65},{193,129... | collective-permute-start | bytes 294920 | tf_op jit(solution)/shard_map/ppermute | solution.py:366
  19.1 10.2 %copy-start.2 = (bf16[256,256]{1,0:T(8,128)(2,1)S(1)}, bf16[256,256]{1,0:T(8,128)(2,1)}, u32[]{:S(2)}) copy-start(bf16[256,256]{1,0:T(8,128)(2,1)} %constant.13.clone.stream) | copy-start | bytes 393220
  19.1 10.2 %copy-start.3 = (bf16[8,64,128]{2,1,0:T(8,128)(2,1)S(1)}, bf16[8,64,128]{2,1,0:T(8,128)(2,1)}, u32[]{:S(2)}) copy-start(bf16[8,64,128]{2,1,0:T(8,128)(2,1)} %constant.14.clone.masks) | copy-start | bytes 393220
  26.7 2.7 %copy-start = (bf16[24,128,8,128]{3,2,1,0:T(8,128)(2,1)}, bf16[24,128,8,128]{3,2,1,0:T(8,128)(2,1)S(1)}, u32[]{:S(2)}) copy-start(bf16[24,128,8,128]{3,2,1,0:T(8,128)(2,1)S(1)} %get-tuple-element.22.modes_in) | copy-start | bytes 18874372
  29.4 2.8 %copy-start.1 = (bf16[24,128,8,128]{3,2,1,0:T(8,128)(2,1)S(1)}, bf16[24,128,8,128]{3,2,1,0:T(8,128)(2,1)}, u32[]{:S(2)}) copy-start(bf16[24,128,8,128]{3,2,1,0:T(8,128)(2,1)} %copy-done) | copy-start | bytes 18874372
  32.1 0.8 copy-start.4
  45.8 6.2 %collective-permute-start.6 = (f32[64,128]{1,0:T(8,128)S(1)}, f32[64,128]{1,0:T(8,128)S(1)}, u32[]{:S(2)}, u32[]{:S(2)}) collective-permute-start(f32[64,128]{1,0:T(8,128)S(1)} %broadcast_select_fusion), channel_id=1, source_target_pairs={{0,1},{1,0},{2,3},{3,2},{4,5},{5,4},{6,7},{7,6},{8,9},{9,8},{10,11... | collective-permute-start | bytes 98312 | tf_op jit(solution)/shard_map/ppermute | solution.py:374
  52.0 2.8 %collective-permute-start.7 = (f32[64,128]{1,0:T(8,128)S(1)}, f32[64,128]{1,0:T(8,128)S(1)}, u32[]{:S(2)}, u32[]{:S(2)}) collective-permute-start(f32[64,128]{1,0:T(8,128)S(1)} %select_add_fusion), channel_id=1, source_target_pairs={{0,64},{64,0},{128,192},{192,128},{1,65},{65,1},{129,193},{193,129... | collective-permute-start | bytes 98312 | tf_op jit(solution)/shard_map/ppermute | solution.py:370
  54.8 4.0 %collective-permute-start.8 = (f32[64,128]{1,0:T(8,128)S(1)}, f32[64,128]{1,0:T(8,128)S(1)}, u32[]{:S(2)}, u32[]{:S(2)}) collective-permute-start(f32[64,128]{1,0:T(8,128)S(1)} %add.25), channel_id=1, source_target_pairs={{0,192},{64,128},{128,64},{192,0},{1,193},{65,129},{129,65},{193,1... | collective-permute-start | bytes 98312 | tf_op jit(solution)/shard_map/ppermute | solution.py:370
  58.8 2.8 %collective-permute-start.9 = (f32[64,128]{1,0:T(8,128)S(1)}, f32[64,128]{1,0:T(8,128)S(1)}, u32[]{:S(2)}, u32[]{:S(2)}) collective-permute-start(f32[64,128]{1,0:T(8,128)S(1)} %add.26), channel_id=1, source_target_pairs={{0,16},{16,0},{32,48},{48,32},{1,17},{17,1},{33,49},{49,33},{2,18}... | collective-permute-start | bytes 98312 | tf_op jit(solution)/shard_map/ppermute | solution.py:370
  61.6 4.0 %collective-permute-start.10 = (f32[64,128]{1,0:T(8,128)S(1)}, f32[64,128]{1,0:T(8,128)S(1)}, u32[]{:S(2)}, u32[]{:S(2)}) collective-permute-start(f32[64,128]{1,0:T(8,128)S(1)} %add.27), channel_id=1, source_target_pairs={{0,48},{16,32},{32,16},{48,0},{1,49},{17,33},{33,17},{49,1},{2,50}... | collective-permute-start | bytes 98312 | tf_op jit(solution)/shard_map/ppermute | solution.py:370
  65.5 2.8 %collective-permute-start.11 = (f32[64,128]{1,0:T(8,128)S(1)}, f32[64,128]{1,0:T(8,128)S(1)}, u32[]{:S(2)}, u32[]{:S(2)}) collective-permute-start(f32[64,128]{1,0:T(8,128)S(1)} %add.28), channel_id=1, source_target_pairs={{0,2},{2,0},{4,6},{6,4},{8,10},{10,8},{12,14},{14,12},{1,3},{3,1},... | collective-permute-start | bytes 98312 | tf_op jit(solution)/shard_map/ppermute | solution.py:370
  68.3 3.7 %collective-permute-start.12 = (f32[64,128]{1,0:T(8,128)S(1)}, f32[64,128]{1,0:T(8,128)S(1)}, u32[]{:S(2)}, u32[]{:S(2)}) collective-permute-start(f32[64,128]{1,0:T(8,128)S(1)} %add.29), channel_id=1, source_target_pairs={{0,4},{2,6},{4,0},{6,2},{8,12},{10,14},{12,8},{14,10},{1,5},{3,7},... | collective-permute-start | bytes 98312 | tf_op jit(solution)/shard_map/ppermute | solution.py:370
  72.1 4.9 %collective-permute-start.13 = (f32[64,128]{1,0:T(8,128)S(1)}, f32[64,128]{1,0:T(8,128)S(1)}, u32[]{:S(2)}, u32[]{:S(2)}) collective-permute-start(f32[64,128]{1,0:T(8,128)S(1)} %add.30), channel_id=1, source_target_pairs={{0,12},{2,14},{4,8},{6,10},{8,4},{10,6},{12,0},{14,2},{1,13},{3,15... | collective-permute-start | bytes 98312 | tf_op jit(solution)/shard_map/ppermute | solution.py:370
  76.9 9.3 %collective-permute-start.14 = (f32[64,128]{1,0:T(8,128)S(1)}, f32[64,128]{1,0:T(8,128)S(1)}, u32[]{:S(2)}, u32[]{:S(2)}) collective-permute-start(f32[64,128]{1,0:T(8,128)S(1)} %add.31.mine), channel_id=1, source_target_pairs={{0,1},{1,0},{2,3},{3,2},{4,5},{5,4},{6,7},{7,6},{8,9},{9,8},{10,11... | collective-permute-start | bytes 98312 | tf_op jit(solution)/shard_map/ppermute | solution.py:374

commit v4 on v3

--- a/solution.py
+++ b/solution.py
@@ -14,7 +14,7 @@
 BF16 = jnp.bfloat16
 F32 = jnp.float32
 VISCOSITY = 0.1
-VMEM_LIMIT = 24 * 2**20
+VMEM_LIMIT = 10 * 2**20
 HIGH = lax.Precision.HIGHEST
 NT = (((1,), (1,)), ((), ()))
 TN = (((0,), (0,)), ((), ()))
@@ -110,7 +110,13 @@
     )(from_hbm(snap))
 
 
-def side_pack_body(snap, low, high, right, left):
+def side_pack_body(snap, modes_hbm, snap_hbm, low, high, right, left, modes_in, snap_in, sems):
+    copies = []
+    for k in range(24):
+        copies.append(pltpu.make_async_copy(modes_hbm.at[:, k], modes_in.at[k], sems.at[0, k]))
+        copies.append(pltpu.make_async_copy(snap_hbm.at[:, k], snap_in.at[k], sems.at[1, k]))
+    for c in copies:
+        c.start()
     grid = lambda shape: [lax.broadcasted_iota(jnp.int32, shape, d) for d in range(2)]
     row, col = grid((32, 64))
     wanted = (row % 16) // 2 * 8 + row % 2 + jnp.where(row < 16, 0, 6)
@@ -140,18 +146,28 @@
         return _
 
     lax.fori_loop(0, 24, group_of, 0, unroll=4)
-
-
-def side_pack(snap):
+    for c in copies:
+        c.wait()
+
+
+def side_pack(snap, modes, planes):
     wide, slim = jax.ShapeDtypeStruct((192, 16, 128), BF16), jax.ShapeDtypeStruct((24, 16, 128), BF16)
     return pl.pallas_call(
         side_pack_body,
-        out_shape=(wide, wide, slim, slim),
-        in_specs=[resident()],
-        out_specs=(resident(),) * 4,
+        out_shape=(
+            wide,
+            wide,
+            slim,
+            slim,
+            jax.ShapeDtypeStruct((24, 128, 8, 128), BF16),
+            jax.ShapeDtypeStruct((24, 64, 8, 128), BF16),
+        ),
+        in_specs=[resident(), in_hbm(), in_hbm()],
+        out_specs=(resident(),) * 6,
+        scratch_shapes=[pltpu.SemaphoreType.DMA((2, 24))],
         compiler_params=pltpu.CompilerParams(vmem_limit_bytes=VMEM_LIMIT),
         name="side_pack",
-    )(in_vmem(snap))
+    )(in_vmem(snap), from_hbm(modes), from_hbm(planes))
 
 
 def same_span(total, half, out):
@@ -177,38 +193,25 @@
         total[block, rows] = lanes if base is None else base[block, rows] + lanes
 
 
-def snap_project_body(modes, snap, out, modes_in, snap_in, total, sems):
-    copies = []
-    for k in range(24):
-        copies.append(pltpu.make_async_copy(modes.at[:, k], modes_in.at[k], sems.at[0, k]))
-        copies.append(pltpu.make_async_copy(snap.at[:, k], snap_in.at[k], sems.at[1, k]))
-    for c in copies:
-        c.start()
-    for half, size in ((0, 6), (1, 12)):
-        for k in range(0, 24, size):
-            if half == 0:
-                for c in copies[2 * k : 2 * (k + size)]:
-                    c.wait()
-            planes = range(k, k + size)
+def snap_project_body(modes_in, snap_in, out, total):
+    for half in range(2):
+        for k in range(0, 24, 12):
+            planes = range(k, k + 12)
             data = [snap_in[p].reshape(512, 128) for p in planes]
             add_products(modes_in, half, planes, data, total, total if k else None)
         same_span(total, half, out)
 
 
-def snap_project(modes, snap):
+def snap_project(modes_in, snap_in):
     return pl.pallas_call(
         snap_project_body,
-        out_shape=(jax.ShapeDtypeStruct((64, 128), F32), jax.ShapeDtypeStruct((24, 128, 8, 128), BF16)),
-        in_specs=[in_hbm(), in_hbm()],
-        out_specs=(resident(), resident()),
-        scratch_shapes=[
-            pltpu.VMEM((24, 64, 8, 128), BF16),
-            pltpu.VMEM((4, 1024, 128), F32),
-            pltpu.SemaphoreType.DMA((2, 24)),
-        ],
+        out_shape=jax.ShapeDtypeStruct((64, 128), F32),
+        in_specs=[resident(), resident()],
+        out_specs=resident(),
+        scratch_shapes=[pltpu.VMEM((4, 1024, 128), F32)],
         compiler_params=pltpu.CompilerParams(vmem_limit_bytes=VMEM_LIMIT),
         name="snap_project",
-    )(from_hbm(modes), from_hbm(snap))
+    )(in_vmem(modes_in), in_vmem(snap_in))
 
 
 def feature_body(
@@ -280,7 +283,7 @@
     )(*map(in_vmem, (modes_in, snap, z_low, z_high, x_low, x_high)), *consts)
 
 
-def edge_body(modes_in, snap, edges, y_low, y_high, inner, out, field, total):
+def edge_body(modes_in, snap, edges, y_low, y_high, inner, snap_part, mine, other, out, field, total):
     k = VISCOSITY / 12.0
     row = lax.axis_index("gy")
     has_below, has_above = row > 0, row < 3
@@ -323,18 +326,21 @@
     for half in range(2):
         add_products(modes_in, half, planes, [field[k] for k in range(12)], total, inner)
         same_span(total, half, out)
-
-
-def edge_project(modes_in, snap, edges, y_low, y_high, inner):
+    first = lax.axis_index("gz_1") == 0
+    mine[...] = jnp.where(first, snap_part[...], out[...])
+    other[...] = jnp.where(first, out[...], snap_part[...])
+
+
+def edge_project(modes_in, snap, edges, y_low, y_high, inner, snap_part):
     return pl.pallas_call(
         edge_body,
-        out_shape=jax.ShapeDtypeStruct((64, 128), F32),
-        in_specs=[resident()] * 6,
-        out_specs=resident(),
-        scratch_shapes=[pltpu.VMEM((12, 512, 128), BF16), pltpu.VMEM((4, 1024, 128), F32)],
+        out_shape=(jax.ShapeDtypeStruct((64, 128), F32),) * 2,
+        in_specs=[resident()] * 7,
+        out_specs=(resident(), resident()),
+        scratch_shapes=[pltpu.VMEM((64, 128), F32), pltpu.VMEM((12, 512, 128), BF16), pltpu.VMEM((4, 1024, 128), F32)],
         compiler_params=pltpu.CompilerParams(vmem_limit_bytes=VMEM_LIMIT),
         name="edge_project",
-    )(*map(in_vmem, (modes_in, snap, edges, y_low, y_high, inner)))
+    )(*map(in_vmem, (modes_in, snap, edges, y_low, y_high, inner, snap_part)))
 
 
 def gram_body(mine, other, snap_out, feature_out, gram_snap, gram_feature, gram_quad):
@@ -389,17 +395,17 @@
     low, high, units = wall_pack(snapshots.reshape(192, 64, 128))
     y_low = shifted(high, "gy", 4, 1)
     y_high = shifted(low, "gy", 4, -1)
-    low, high, right, left = side_pack(units)
+    low, high, right, left, modes_in, snap_in = side_pack(
+        units, modes.reshape(128, 24, 8, 128), snapshots.reshape(64, 24, 8, 128)
+    )
     z_low = shifted(high, GZ, 16, 1)
     z_high = shifted(low, GZ, 16, -1)
     x_low = shifted(right, "gx", 4, 1)
     x_high = shifted(left, "gx", 4, -1)
-    snap_part, modes_in = snap_project(modes.reshape(128, 24, 8, 128), snapshots.reshape(64, 24, 8, 128))
+    snap_part = snap_project(modes_in, snap_in)
     inner, edges = feature_project(modes_in, units, z_low, z_high, x_low, x_high)
-    feature_part = edge_project(modes_in, units, edges, y_low, y_high, inner)
-    core = lax.axis_index("gz_1")
-    mine = jnp.where(core == 0, snap_part, feature_part)
-    total = mine + other_core(jnp.where(core == 0, feature_part, snap_part))
+    mine, other = edge_project(modes_in, units, edges, y_low, y_high, inner, snap_part)
+    total = mine + other_core(other)
     for axis, partners in ROUNDS:
         total = total + swapped(total, axis, partners)
     rs, rf, gram_snap, gram_feature, gram_quad = grams(total, other_core(total))

time: 87.4 us -> 75.1 us (0.86)
  local copies, waits for them, and re-layouts: 6.2 us -> 0.01 us
  Pallas kernels: 27.7 us -> 21.7 us
    unnamed x10 -> x6, local copies, waits for them, and re-layouts: 6.2 us -> 0.01 us
    pallas_call x3, Pallas kernels: 16.3 us -> 12.1 us  [the longest x1 4.39 us: side_pack(): pl.pallas_call(side_pack_body, out_shape=(wide, wide, slim, slim, jax.Sha...]
    pallas_call x1, Pallas kernels: 8.09 us -> 6.71 us  [feature_project(): pl.pallas_call(feature_body, out_shape=(jax.ShapeDtypeStruct((4, 1024, 12...]
  transfers between devices with their start and end apart: 15 -> 15, of which waited for: 10 -> 10; matrix products, arithmetic and copies ran while one was open for 0% -> 0% of each run, Pallas kernels for 18% -> 15%
where the time goes in v4:
time: 75.1 us; the launch traced here: 75 us
  starting transfers between devices  28.3 us (38%)
  waiting for transfers between devices  24.1 us (32%)
  Pallas kernels  21.7 us (29%)
    ppermute x7, waiting for transfers between devices, swapped(): return lax.ppermute(value, axis, list(enumerate(partners)))  18.5 us
    ppermute x2, starting transfers between devices, other_core(): return lax.ppermute(value, 'gz_1', [(0, 1), (1, 0)])  13.9 us
    ppermute x6, starting transfers between devices, shifted(): lax.ppermute(value, axis, [(i, (i + by) % count) for i in range(count)])  8.1 us
    pallas_call x1, Pallas kernels, feature_project(): pl.pallas_call(feature_body, out_shape=(jax.ShapeDtypeStruct((4, 1024, 12...  6.71 us
    ppermute x7, starting transfers between devices, swapped(): return lax.ppermute(value, axis, list(enumerate(partners)))  6.34 us
    pallas_call x1, Pallas kernels, side_pack(): pl.pallas_call(side_pack_body, out_shape=(wide, wide, slim, slim, jax.Sha...  4.39 us
    pallas_call x1, Pallas kernels, snap_project(): pl.pallas_call(snap_project_body, out_shape=jax.ShapeDtypeStruct((64, 128...  4.27 us
    ppermute x6, waiting for transfers between devices, shifted(): lax.ppermute(value, axis, [(i, (i + by) % count) for i in range(count)])  3.92 us
  transfers between devices with their start and end apart: 15, of which 10 were waited for; matrix products, arithmetic and copies ran while one was open for 0% of the time, Pallas kernels for 15%

profile of v4, /device:TPU:1, one launch (start us, length us, event | category | flops | bytes accessed | tf_op | source)
XLA Modules:
  0.0 75.0 jit_solution(13976190477460425070)
XLA Ops:
  0.6 2.0 %wall_pack.1 = (bf16[192,16,128]{2,1,0:T(8,128)(2,1)S(1)}, bf16[192,16,128]{2,1,0:T(8,128)(2,1)S(1)}, bf16[192,64,128]{2,1,0:T(8,128)(2,1)S(1)}) custom-call(bf16[192,64,128]{2,1,0:T(8,128)(2,1)} %bitcast.5), custom_call_target="tpu_custom_call" | custom-call | tf_op jit(solution)/shard_map/wall_pack/pallas_call | solution.py:102
  2.6 4.4 %side_pack.1 = (bf16[192,16,128]{2,1,0:T(8,128)(2,1)S(1)}, bf16[192,16,128]{2,1,0:T(8,128)(2,1)S(1)}, bf16[24,16,128]{2,1,0:T(8,128)(2,1)S(1)}, bf16[24,16,128]{...) custom-call(bf16[192,64,128]{2,1,0:T(8,128)(2,1)S(1)} %get-tuple-element.23.snap, ...), custom_call_target="tpu_custom_call" | custom-call | tf_op jit(solution)/shard_map/side_pack/pallas_call | solution.py:155
  7.0 3.0 %collective-permute-start = (bf16[192,16,128]{2,1,0:T(8,128)(2,1)S(1)}, bf16[192,16,128]{2,1,0:T(8,128)(2,1)S(1)}, u32[]{:S(2)}, u32[]{:S(2)}) collective-permute-start(bf16[192,16,128]{2,1,0:T(8,128)(2,1)S(1)} %get-tuple-element.25), channel_id=1, source_target_pairs={{0,1},{1,2},{2,3},{3,4},{4,5},{5,6},{6,7},{7,8},{8,9},{9,10},{10,1... | collective-permute-start | bytes 2359304 | tf_op jit(solution)/shard_map/ppermute | solution.py:372
  10.0 0.2 collective-permute-start.1
  10.2 1.1 %collective-permute-start.4 = (bf16[192,16,128]{2,1,0:T(8,128)(2,1)S(1)}, bf16[192,16,128]{2,1,0:T(8,128)(2,1)S(1)}, u32[]{:S(2)}, u32[]{:S(2)}) collective-permute-start(bf16[192,16,128]{2,1,0:T(8,128)(2,1)S(1)} %get-tuple-element.30), channel_id=1, source_target_pairs={{0,16},{16,32},{32,48},{48,0},{1,17},{17,33},{33,49},{49,1},{2,18}... | collective-permute-start | bytes 2359304 | tf_op jit(solution)/shard_map/ppermute | solution.py:372
  11.3 1.6 %collective-permute-start.5 = (bf16[192,16,128]{2,1,0:T(8,128)(2,1)S(1)}, bf16[192,16,128]{2,1,0:T(8,128)(2,1)S(1)}, u32[]{:S(2)}, u32[]{:S(2)}) collective-permute-start(bf16[192,16,128]{2,1,0:T(8,128)(2,1)S(1)} %get-tuple-element.31), channel_id=1, source_target_pairs={{0,48},{16,0},{32,16},{48,32},{1,49},{17,1},{33,17},{49,33},{2,50}... | collective-permute-start | bytes 2359304 | tf_op jit(solution)/shard_map/ppermute | solution.py:372
  12.9 1.1 %collective-permute-start.2 = (bf16[24,16,128]{2,1,0:T(8,128)(2,1)S(1)}, bf16[24,16,128]{2,1,0:T(8,128)(2,1)S(1)}, u32[]{:S(2)}, u32[]{:S(2)}) collective-permute-start(bf16[24,16,128]{2,1,0:T(8,128)(2,1)S(1)} %get-tuple-element.27), channel_id=1, source_target_pairs={{0,64},{64,128},{128,192},{192,0},{1,65},{65,129},{129,193},{193,1... | collective-permute-start | bytes 294920 | tf_op jit(solution)/shard_map/ppermute | solution.py:372
  14.0 3.9 %collective-permute-done.2.x_low = bf16[24,16,128]{2,1,0:T(8,128)(2,1)S(1)} collective-permute-done((bf16[24,16,128]{2,1,0:T(8,128)(2,1)S(1)}, bf16[24,16,128]{2,1,0:T(8,128)(2,1)S(1)}, u32[]{:S(2)}, u32[]{:S(2)}) %collective-permute-start.2) | collective-permute-done | bytes 98336 | tf_op jit(solution)/shard_map/ppermute | solution.py:372
  17.9 1.1 %collective-permute-start.3 = (bf16[24,16,128]{2,1,0:T(8,128)(2,1)S(1)}, bf16[24,16,128]{2,1,0:T(8,128)(2,1)S(1)}, u32[]{:S(2)}, u32[]{:S(2)}) collective-permute-start(bf16[24,16,128]{2,1,0:T(8,128)(2,1)S(1)} %get-tuple-element.28), channel_id=1, source_target_pairs={{0,192},{64,0},{128,64},{192,128},{1,193},{65,1},{129,65},{193,129... | collective-permute-start | bytes 294920 | tf_op jit(solution)/shard_map/ppermute | solution.py:372
  19.0 0.0 copy-start
  19.0 0.0 copy-start.1
  19.0 0.0 copy-start.2
  19.0 4.3 %snap_project.1.snap_part = f32[64,128]{1,0:T(8,128)S(1)} custom-call(bf16[24,128,8,128]{3,2,1,0:T(8,128)(2,1)S(1)} %get-tuple-element.24.modes_in, bf16[24,64,8,128]{3,2,1,0:T(8,128)(2,1)S(1)} %get-tuple-element.33.snap_in), custom_call_target="tpu_custom_call" | custom-call | tf_op jit(solution)/shard_map/snap_project/pallas_call | solution.py:206
  23.3 0.0 collective-permute-done.3.x_high
  23.3 0.0 collective-permute-done.z_low
  23.3 0.0 collective-permute-done.1.z_high
  23.3 0.0 copy-done
  23.4 0.0 copy-done.1
  23.4 0.0 copy-done.2
  23.4 6.7 %feature_project.1 = (f32[4,1024,128]{2,1,0:T(8,128)S(1)}, f32[192,4,8,128]{3,2,1,0:T(8,128)S(1)}) custom-call(bf16[24,128,8,128]{3,2,1,0:T(8,128)(2,1)S(1)} %get-tuple-element.24.modes_in, bf16[192,64,128]{2,1,0:T(8,128)(2,1)S(1)} %get-tuple-element.23.snap, bf16[192,16,128]{2,1,0:T(8,128)(2,1)S(1)} %collective-permute-done.z_low, ...), custom_call_target="tpu_custom_call" | custom-call | tf_op jit(solution)/shard_map/feature_project/pallas_call | solution.py:272
  30.1 0.0 collective-permute-done.4.y_low
  30.1 0.0 collective-permute-done.5.y_high
  30.1 3.4 %edge_project.1 = (f32[64,128]{1,0:T(8,128)S(1)}, f32[64,128]{1,0:T(8,128)S(1)}) custom-call(bf16[24,128,8,128]{3,2,1,0:T(8,128)(2,1)S(1)} %get-tuple-element.24.modes_in, bf16[192,64,128]{2,1,0:T(8,128)(2,1)S(1)} %get-tuple-element.23.snap, f32[192,4,8,128]{3,2,1,0:T(8,128)S(1)} %get-tuple-element.29.edges, ...), custom_call_target="tpu_custom_call" | custom-call | tf_op jit(solution)/shard_map/edge_project/pallas_call | solution.py:335
  33.5 5.5 %collective-permute-start.6 = (f32[64,128]{1,0:T(8,128)S(1)}, f32[64,128]{1,0:T(8,128)S(1)}, u32[]{:S(2)}, u32[]{:S(2)}) collective-permute-start(f32[64,128]{1,0:T(8,128)S(1)} %get-tuple-element.35), channel_id=1, source_target_pairs={{0,1},{1,0},{2,3},{3,2},{4,5},{5,4},{6,7},{7,6},{8,9},{9,8},{10,11... | collective-permute-start | bytes 98312 | tf_op jit(solution)/shard_map/ppermute | solution.py:380
  39.0 0.9 %collective-permute-done.6 = f32[64,128]{1,0:T(8,128)S(1)} collective-permute-done((f32[64,128]{1,0:T(8,128)S(1)}, f32[64,128]{1,0:T(8,128)S(1)}, u32[]{:S(2)}, u32[]{:S(2)}) %collective-permute-start.6) | collective-permute-done | bytes 32800 | tf_op jit(solution)/shard_map/ppermute | solution.py:380
  39.8 0.2 collective-permute-start.7
  40.0 2.6 %collective-permute-done.7 = f32[64,128]{1,0:T(8,128)S(1)} collective-permute-done((f32[64,128]{1,0:T(8,128)S(1)}, f32[64,128]{1,0:T(8,128)S(1)}, u32[]{:S(2)}, u32[]{:S(2)}) %collective-permute-start.7) | collective-permute-done | bytes 32800 | tf_op jit(solution)/shard_map/ppermute | solution.py:376
  42.6 1.2 %collective-permute-start.8 = (f32[64,128]{1,0:T(8,128)S(1)}, f32[64,128]{1,0:T(8,128)S(1)}, u32[]{:S(2)}, u32[]{:S(2)}) collective-permute-start(f32[64,128]{1,0:T(8,128)S(1)} %add.25), channel_id=1, source_target_pairs={{0,192},{64,128},{128,64},{192,0},{1,193},{65,129},{129,65},{193,1... | collective-permute-start | bytes 98312 | tf_op jit(solution)/shard_map/ppermute | solution.py:376
  43.8 2.7 %collective-permute-done.8 = f32[64,128]{1,0:T(8,128)S(1)} collective-permute-done((f32[64,128]{1,0:T(8,128)S(1)}, f32[64,128]{1,0:T(8,128)S(1)}, u32[]{:S(2)}, u32[]{:S(2)}) %collective-permute-start.8) | collective-permute-done | bytes 32800 | tf_op jit(solution)/shard_map/ppermute | solution.py:376
  46.6 0.1 collective-permute-start.9
  46.7 2.7 %collective-permute-done.9 = f32[64,128]{1,0:T(8,128)S(1)} collective-permute-done((f32[64,128]{1,0:T(8,128)S(1)}, f32[64,128]{1,0:T(8,128)S(1)}, u32[]{:S(2)}, u32[]{:S(2)}) %collective-permute-start.9) | collective-permute-done | bytes 32800 | tf_op jit(solution)/shard_map/ppermute | solution.py:376
  49.4 1.5 %collective-permute-start.10 = (f32[64,128]{1,0:T(8,128)S(1)}, f32[64,128]{1,0:T(8,128)S(1)}, u32[]{:S(2)}, u32[]{:S(2)}) collective-permute-start(f32[64,128]{1,0:T(8,128)S(1)} %add.27), channel_id=1, source_target_pairs={{0,48},{16,32},{32,16},{48,0},{1,49},{17,33},{33,17},{49,1},{2,50}... | collective-permute-start | bytes 98312 | tf_op jit(solution)/shard_map/ppermute | solution.py:376
  50.9 2.5 %collective-permute-done.10 = f32[64,128]{1,0:T(8,128)S(1)} collective-permute-done((f32[64,128]{1,0:T(8,128)S(1)}, f32[64,128]{1,0:T(8,128)S(1)}, u32[]{:S(2)}, u32[]{:S(2)}) %collective-permute-start.10) | collective-permute-done | bytes 32800 | tf_op jit(solution)/shard_map/ppermute | solution.py:376
  53.3 0.0 collective-permute-start.11
  53.4 2.8 %collective-permute-done.11 = f32[64,128]{1,0:T(8,128)S(1)} collective-permute-done((f32[64,128]{1,0:T(8,128)S(1)}, f32[64,128]{1,0:T(8,128)S(1)}, u32[]{:S(2)}, u32[]{:S(2)}) %collective-permute-start.11) | collective-permute-done | bytes 32800 | tf_op jit(solution)/shard_map/ppermute | solution.py:376
  56.1 0.9 %collective-permute-start.12 = (f32[64,128]{1,0:T(8,128)S(1)}, f32[64,128]{1,0:T(8,128)S(1)}, u32[]{:S(2)}, u32[]{:S(2)}) collective-permute-start(f32[64,128]{1,0:T(8,128)S(1)} %add.29), channel_id=1, source_target_pairs={{0,4},{2,6},{4,0},{6,2},{8,12},{10,14},{12,8},{14,10},{1,5},{3,7},... | collective-permute-start | bytes 98312 | tf_op jit(solution)/shard_map/ppermute | solution.py:376
  57.0 2.8 %collective-permute-done.12 = f32[64,128]{1,0:T(8,128)S(1)} collective-permute-done((f32[64,128]{1,0:T(8,128)S(1)}, f32[64,128]{1,0:T(8,128)S(1)}, u32[]{:S(2)}, u32[]{:S(2)}) %collective-permute-start.12) | collective-permute-done | bytes 32800 | tf_op jit(solution)/shard_map/ppermute | solution.py:376
  59.9 2.4 %collective-permute-start.13 = (f32[64,128]{1,0:T(8,128)S(1)}, f32[64,128]{1,0:T(8,128)S(1)}, u32[]{:S(2)}, u32[]{:S(2)}) collective-permute-start(f32[64,128]{1,0:T(8,128)S(1)} %add.30), channel_id=1, source_target_pairs={{0,12},{2,14},{4,8},{6,10},{8,4},{10,6},{12,0},{14,2},{1,13},{3,15... | collective-permute-start | bytes 98312 | tf_op jit(solution)/shard_map/ppermute | solution.py:376
  62.3 2.5 %collective-permute-done.13 = f32[64,128]{1,0:T(8,128)S(1)} collective-permute-done((f32[64,128]{1,0:T(8,128)S(1)}, f32[64,128]{1,0:T(8,128)S(1)}, u32[]{:S(2)}, u32[]{:S(2)}) %collective-permute-start.13) | collective-permute-done | bytes 32800 | tf_op jit(solution)/shard_map/ppermute | solution.py:376
  64.7 8.4 %collective-permute-start.14 = (f32[64,128]{1,0:T(8,128)S(1)}, f32[64,128]{1,0:T(8,128)S(1)}, u32[]{:S(2)}, u32[]{:S(2)}) collective-permute-start(f32[64,128]{1,0:T(8,128)S(1)} %add.31.mine), channel_id=1, source_target_pairs={{0,1},{1,0},{2,3},{3,2},{4,5},{5,4},{6,7},{7,6},{8,9},{9,8},{10,11... | collective-permute-start | bytes 98312 | tf_op jit(solution)/shard_map/ppermute | solution.py:380
  73.1 0.9 %collective-permute-done.14.other = f32[64,128]{1,0:T(8,128)S(1)} collective-permute-done((f32[64,128]{1,0:T(8,128)S(1)}, f32[64,128]{1,0:T(8,128)S(1)}, u32[]{:S(2)}, u32[]{:S(2)}) %collective-permute-start.14) | collective-permute-done | bytes 32800 | tf_op jit(solution)/shard_map/ppermute | solution.py:380
  74.0 1.0 %grams.1 = (f32[64,128]{1,0:T(8,128)}, f32[64,128]{1,0:T(8,128)}, f32[128,128]{1,0:T(8,128)}, f32[128,128]{1,0:T(8,128)}, f32[64,64]{1,0:T(8,128)}) custom-call(f32[64,128]{1,0:T(8,128)S(1)} %add.31.mine, f32[64,128]{1,0:T(8,128)S(1)} %collective-permute-done.14.other), custom_call_target="tpu_custom_call" | custom-call | tf_op jit(solution)/shard_map/grams/pallas_call | solution.py:362
  (8 shorter events, 0.0 us)
Async XLA Ops:
  7.0 16.3 %collective-permute-start = (bf16[192,16,128]{2,1,0:T(8,128)(2,1)S(1)}, bf16[192,16,128]{2,1,0:T(8,128)(2,1)S(1)}, u32[]{:S(2)}, u32[]{:S(2)}) collective-permute-start(bf16[192,16,128]{2,1,0:T(8,128)(2,1)S(1)} %get-tuple-element.25), channel_id=1, source_target_pairs={{0,1},{1,2},{2,3},{3,4},{4,5},{5,6},{6,7},{7,8},{8,9},{9,10},{10,1... | collective-permute-start | bytes 2359304 | tf_op jit(solution)/shard_map/ppermute | solution.py:372
  10.0 13.3 %collective-permute-start.1 = (bf16[192,16,128]{2,1,0:T(8,128)(2,1)S(1)}, bf16[192,16,128]{2,1,0:T(8,128)(2,1)S(1)}, u32[]{:S(2)}, u32[]{:S(2)}) collective-permute-start(bf16[192,16,128]{2,1,0:T(8,128)(2,1)S(1)} %get-tuple-element.26), channel_id=1, source_target_pairs={{0,15},{1,0},{2,1},{3,2},{4,3},{5,4},{6,5},{7,6},{8,7},{9,8},{10,9... | collective-permute-start | bytes 2359304 | tf_op jit(solution)/shard_map/ppermute | solution.py:372
  10.2 19.8 %collective-permute-start.4 = (bf16[192,16,128]{2,1,0:T(8,128)(2,1)S(1)}, bf16[192,16,128]{2,1,0:T(8,128)(2,1)S(1)}, u32[]{:S(2)}, u32[]{:S(2)}) collective-permute-start(bf16[192,16,128]{2,1,0:T(8,128)(2,1)S(1)} %get-tuple-element.30), channel_id=1, source_target_pairs={{0,16},{16,32},{32,48},{48,0},{1,17},{17,33},{33,49},{49,1},{2,18}... | collective-permute-start | bytes 2359304 | tf_op jit(solution)/shard_map/ppermute | solution.py:372
  11.3 18.8 %collective-permute-start.5 = (bf16[192,16,128]{2,1,0:T(8,128)(2,1)S(1)}, bf16[192,16,128]{2,1,0:T(8,128)(2,1)S(1)}, u32[]{:S(2)}, u32[]{:S(2)}) collective-permute-start(bf16[192,16,128]{2,1,0:T(8,128)(2,1)S(1)} %get-tuple-element.31), channel_id=1, source_target_pairs={{0,48},{16,0},{32,16},{48,32},{1,49},{17,1},{33,17},{49,33},{2,50}... | collective-permute-start | bytes 2359304 | tf_op jit(solution)/shard_map/ppermute | solution.py:372
  12.9 5.0 %collective-permute-start.2 = (bf16[24,16,128]{2,1,0:T(8,128)(2,1)S(1)}, bf16[24,16,128]{2,1,0:T(8,128)(2,1)S(1)}, u32[]{:S(2)}, u32[]{:S(2)}) collective-permute-start(bf16[24,16,128]{2,1,0:T(8,128)(2,1)S(1)} %get-tuple-element.27), channel_id=1, source_target_pairs={{0,64},{64,128},{128,192},{192,0},{1,65},{65,129},{129,193},{193,1... | collective-permute-start | bytes 294920 | tf_op jit(solution)/shard_map/ppermute | solution.py:372
  17.9 5.4 %collective-permute-start.3 = (bf16[24,16,128]{2,1,0:T(8,128)(2,1)S(1)}, bf16[24,16,128]{2,1,0:T(8,128)(2,1)S(1)}, u32[]{:S(2)}, u32[]{:S(2)}) collective-permute-start(bf16[24,16,128]{2,1,0:T(8,128)(2,1)S(1)} %get-tuple-element.28), channel_id=1, source_target_pairs={{0,192},{64,0},{128,64},{192,128},{1,193},{65,1},{129,65},{193,129... | collective-permute-start | bytes 294920 | tf_op jit(solution)/shard_map/ppermute | solution.py:372
  19.0 4.3 %copy-start = (bf16[8,64,128]{2,1,0:T(8,128)(2,1)S(1)}, bf16[8,64,128]{2,1,0:T(8,128)(2,1)}, u32[]{:S(2)}) copy-start(bf16[8,64,128]{2,1,0:T(8,128)(2,1)} %constant.8.clone.masks) | copy-start | bytes 393220
  19.0 4.3 %copy-start.1 = (bf16[256,256]{1,0:T(8,128)(2,1)S(1)}, bf16[256,256]{1,0:T(8,128)(2,1)}, u32[]{:S(2)}) copy-start(bf16[256,256]{1,0:T(8,128)(2,1)} %constant.7.clone.stream) | copy-start | bytes 393220
  19.0 4.3 %copy-start.2 = (bf16[128,96]{1,0:T(8,128)(2,1)S(1)}, bf16[128,96]{1,0:T(8,128)(2,1)}, u32[]{:S(2)}) copy-start(bf16[128,96]{1,0:T(8,128)(2,1)} %constant.6.clone.span) | copy-start | bytes 73732
  33.5 6.3 %collective-permute-start.6 = (f32[64,128]{1,0:T(8,128)S(1)}, f32[64,128]{1,0:T(8,128)S(1)}, u32[]{:S(2)}, u32[]{:S(2)}) collective-permute-start(f32[64,128]{1,0:T(8,128)S(1)} %get-tuple-element.35), channel_id=1, source_target_pairs={{0,1},{1,0},{2,3},{3,2},{4,5},{5,4},{6,7},{7,6},{8,9},{9,8},{10,11... | collective-permute-start | bytes 98312 | tf_op jit(solution)/shard_map/ppermute | solution.py:380
  39.8 2.8 %collective-permute-start.7 = (f32[64,128]{1,0:T(8,128)S(1)}, f32[64,128]{1,0:T(8,128)S(1)}, u32[]{:S(2)}, u32[]{:S(2)}) collective-permute-start(f32[64,128]{1,0:T(8,128)S(1)} %add.24), channel_id=1, source_target_pairs={{0,64},{64,0},{128,192},{192,128},{1,65},{65,1},{129,193},{193,129... | collective-permute-start | bytes 98312 | tf_op jit(solution)/shard_map/ppermute | solution.py:376
  42.6 4.0 %collective-permute-start.8 = (f32[64,128]{1,0:T(8,128)S(1)}, f32[64,128]{1,0:T(8,128)S(1)}, u32[]{:S(2)}, u32[]{:S(2)}) collective-permute-start(f32[64,128]{1,0:T(8,128)S(1)} %add.25), channel_id=1, source_target_pairs={{0,192},{64,128},{128,64},{192,0},{1,193},{65,129},{129,65},{193,1... | collective-permute-start | bytes 98312 | tf_op jit(solution)/shard_map/ppermute | solution.py:376
  46.6 2.8 %collective-permute-start.9 = (f32[64,128]{1,0:T(8,128)S(1)}, f32[64,128]{1,0:T(8,128)S(1)}, u32[]{:S(2)}, u32[]{:S(2)}) collective-permute-start(f32[64,128]{1,0:T(8,128)S(1)} %add.26), channel_id=1, source_target_pairs={{0,16},{16,0},{32,48},{48,32},{1,17},{17,1},{33,49},{49,33},{2,18}... | collective-permute-start | bytes 98312 | tf_op jit(solution)/shard_map/ppermute | solution.py:376
  49.4 4.0 %collective-permute-start.10 = (f32[64,128]{1,0:T(8,128)S(1)}, f32[64,128]{1,0:T(8,128)S(1)}, u32[]{:S(2)}, u32[]{:S(2)}) collective-permute-start(f32[64,128]{1,0:T(8,128)S(1)} %add.27), channel_id=1, source_target_pairs={{0,48},{16,32},{32,16},{48,0},{1,49},{17,33},{33,17},{49,1},{2,50}... | collective-permute-start | bytes 98312 | tf_op jit(solution)/shard_map/ppermute | solution.py:376
  53.3 2.8 %collective-permute-start.11 = (f32[64,128]{1,0:T(8,128)S(1)}, f32[64,128]{1,0:T(8,128)S(1)}, u32[]{:S(2)}, u32[]{:S(2)}) collective-permute-start(f32[64,128]{1,0:T(8,128)S(1)} %add.28), channel_id=1, source_target_pairs={{0,2},{2,0},{4,6},{6,4},{8,10},{10,8},{12,14},{14,12},{1,3},{3,1},... | collective-permute-start | bytes 98312 | tf_op jit(solution)/shard_map/ppermute | solution.py:376
  56.1 3.7 %collective-permute-start.12 = (f32[64,128]{1,0:T(8,128)S(1)}, f32[64,128]{1,0:T(8,128)S(1)}, u32[]{:S(2)}, u32[]{:S(2)}) collective-permute-start(f32[64,128]{1,0:T(8,128)S(1)} %add.29), channel_id=1, source_target_pairs={{0,4},{2,6},{4,0},{6,2},{8,12},{10,14},{12,8},{14,10},{1,5},{3,7},... | collective-permute-start | bytes 98312 | tf_op jit(solution)/shard_map/ppermute | solution.py:376
  59.9 4.9 %collective-permute-start.13 = (f32[64,128]{1,0:T(8,128)S(1)}, f32[64,128]{1,0:T(8,128)S(1)}, u32[]{:S(2)}, u32[]{:S(2)}) collective-permute-start(f32[64,128]{1,0:T(8,128)S(1)} %add.30), channel_id=1, source_target_pairs={{0,12},{2,14},{4,8},{6,10},{8,4},{10,6},{12,0},{14,2},{1,13},{3,15... | collective-permute-start | bytes 98312 | tf_op jit(solution)/shard_map/ppermute | solution.py:376
  64.7 9.3 %collective-permute-start.14 = (f32[64,128]{1,0:T(8,128)S(1)}, f32[64,128]{1,0:T(8,128)S(1)}, u32[]{:S(2)}, u32[]{:S(2)}) collective-permute-start(f32[64,128]{1,0:T(8,128)S(1)} %add.31.mine), channel_id=1, source_target_pairs={{0,1},{1,0},{2,3},{3,2},{4,5},{5,4},{6,7},{7,6},{8,9},{9,8},{10,11... | collective-permute-start | bytes 98312 | tf_op jit(solution)/shard_map/ppermute | solution.py:380

commit v5 on v4

--- a/solution.py
+++ b/solution.py
@@ -326,7 +326,7 @@
     for half in range(2):
         add_products(modes_in, half, planes, [field[k] for k in range(12)], total, inner)
         same_span(total, half, out)
-    first = lax.axis_index("gz_1") == 0
+    first = snap_half_here()
     mine[...] = jnp.where(first, snap_part[...], out[...])
     other[...] = jnp.where(first, out[...], snap_part[...])
 
@@ -344,7 +344,7 @@
 
 
 def gram_body(mine, other, snap_out, feature_out, gram_snap, gram_feature, gram_quad):
-    first = lax.axis_index("gz_1") == 0
+    first = snap_half_here()
     rs = jnp.where(first, mine[...], other[...])
     rf = jnp.where(first, other[...], mine[...])
     snap_out[...] = rs
@@ -372,8 +372,14 @@
     return lax.ppermute(value, axis, [(i, (i + by) % count) for i in range(count)])
 
 
+def snap_half_here():
+    x, y, z = (lax.axis_index(a) for a in ("gx", "gy", "gz_0"))
+    return (lax.axis_index("gz_1") + x + y + z + z // 2) % 2 == 0
+
+
 def swapped(value, axis, partners):
-    return lax.ppermute(value, axis, list(enumerate(partners)))
+    pairs = [(2 * i + core, 2 * p + 1 - core) for i, p in enumerate(partners) for core in range(2)]
+    return lax.ppermute(value, (axis, "gz_1"), pairs)
 
 
 def other_core(value):

time: 75.1 us -> 71.6 us (0.953)
  starting transfers between devices: 28.3 us -> 20.8 us
  waiting for transfers between devices: 24.1 us -> 28.2 us
    ppermute x2, starting transfers between devices: 13.9 us -> 5.86 us  [other_core(): return lax.ppermute(value, 'gz_1', [(0, 1), (1, 0)])]
    ppermute x7, waiting for transfers between devices: 18.5 us -> 22.6 us  [swapped(): return lax.ppermute(value, (axis, 'gz_1'), pairs)]
where the time goes in v5:
time: 71.6 us; the launch traced here: 71.5 us
  waiting for transfers between devices  28.2 us (39%)
  Pallas kernels  21.7 us (30%)
  starting transfers between devices  20.8 us (29%)
  between operations  0.75 us (1%)
    ppermute x7, waiting for transfers between devices, swapped(): return lax.ppermute(value, (axis, 'gz_1'), pairs)  22.6 us
    ppermute x6, starting transfers between devices, shifted(): lax.ppermute(value, axis, [(i, (i + by) % count) for i in range(count)])  8.1 us
    ppermute x7, starting transfers between devices, swapped(): return lax.ppermute(value, (axis, 'gz_1'), pairs)  6.79 us
    pallas_call x1, Pallas kernels, feature_project(): pl.pallas_call(feature_body, out_shape=(jax.ShapeDtypeStruct((4, 1024, 12...  6.71 us
    ppermute x2, starting transfers between devices, other_core(): return lax.ppermute(value, 'gz_1', [(0, 1), (1, 0)])  5.86 us
    pallas_call x1, Pallas kernels, side_pack(): pl.pallas_call(side_pack_body, out_shape=(wide, wide, slim, slim, jax.Sha...  4.39 us
    pallas_call x1, Pallas kernels, snap_project(): pl.pallas_call(snap_project_body, out_shape=jax.ShapeDtypeStruct((64, 128...  4.27 us
    ppermute x6, waiting for transfers between devices, shifted(): lax.ppermute(value, axis, [(i, (i + by) % count) for i in range(count)])  3.92 us
  transfers between devices with their start and end apart: 15, of which 10 were waited for; matrix products, arithmetic and copies ran while one was open for 0% of the time, Pallas kernels for 15%

profile of v5, /device:TPU:1, one launch (start us, length us, event | category | flops | bytes accessed | tf_op | source)
XLA Modules:
  0.0 71.5 jit_solution(17665942749899088560)
XLA Ops:
  0.6 2.0 %wall_pack.1 = (bf16[192,16,128]{2,1,0:T(8,128)(2,1)S(1)}, bf16[192,16,128]{2,1,0:T(8,128)(2,1)S(1)}, bf16[192,64,128]{2,1,0:T(8,128)(2,1)S(1)}) custom-call(bf16[192,64,128]{2,1,0:T(8,128)(2,1)} %bitcast.5), custom_call_target="tpu_custom_call" | custom-call | tf_op jit(solution)/shard_map/wall_pack/pallas_call | solution.py:102
  2.6 4.4 %side_pack.1 = (bf16[192,16,128]{2,1,0:T(8,128)(2,1)S(1)}, bf16[192,16,128]{2,1,0:T(8,128)(2,1)S(1)}, bf16[24,16,128]{2,1,0:T(8,128)(2,1)S(1)}, bf16[24,16,128]{...) custom-call(bf16[192,64,128]{2,1,0:T(8,128)(2,1)S(1)} %get-tuple-element.23.snap, ...), custom_call_target="tpu_custom_call" | custom-call | tf_op jit(solution)/shard_map/side_pack/pallas_call | solution.py:155
  7.0 3.0 %collective-permute-start = (bf16[192,16,128]{2,1,0:T(8,128)(2,1)S(1)}, bf16[192,16,128]{2,1,0:T(8,128)(2,1)S(1)}, u32[]{:S(2)}, u32[]{:S(2)}) collective-permute-start(bf16[192,16,128]{2,1,0:T(8,128)(2,1)S(1)} %get-tuple-element.25), channel_id=1, source_target_pairs={{0,1},{1,2},{2,3},{3,4},{4,5},{5,6},{6,7},{7,8},{8,9},{9,10},{10,1... | collective-permute-start | bytes 2359304 | tf_op jit(solution)/shard_map/ppermute | solution.py:372
  10.0 0.2 collective-permute-start.1
  10.2 1.1 %collective-permute-start.4 = (bf16[192,16,128]{2,1,0:T(8,128)(2,1)S(1)}, bf16[192,16,128]{2,1,0:T(8,128)(2,1)S(1)}, u32[]{:S(2)}, u32[]{:S(2)}) collective-permute-start(bf16[192,16,128]{2,1,0:T(8,128)(2,1)S(1)} %get-tuple-element.30), channel_id=1, source_target_pairs={{0,16},{16,32},{32,48},{48,0},{1,17},{17,33},{33,49},{49,1},{2,18}... | collective-permute-start | bytes 2359304 | tf_op jit(solution)/shard_map/ppermute | solution.py:372
  11.3 1.6 %collective-permute-start.5 = (bf16[192,16,128]{2,1,0:T(8,128)(2,1)S(1)}, bf16[192,16,128]{2,1,0:T(8,128)(2,1)S(1)}, u32[]{:S(2)}, u32[]{:S(2)}) collective-permute-start(bf16[192,16,128]{2,1,0:T(8,128)(2,1)S(1)} %get-tuple-element.31), channel_id=1, source_target_pairs={{0,48},{16,0},{32,16},{48,32},{1,49},{17,1},{33,17},{49,33},{2,50}... | collective-permute-start | bytes 2359304 | tf_op jit(solution)/shard_map/ppermute | solution.py:372
  12.9 1.1 %collective-permute-start.2 = (bf16[24,16,128]{2,1,0:T(8,128)(2,1)S(1)}, bf16[24,16,128]{2,1,0:T(8,128)(2,1)S(1)}, u32[]{:S(2)}, u32[]{:S(2)}) collective-permute-start(bf16[24,16,128]{2,1,0:T(8,128)(2,1)S(1)} %get-tuple-element.27), channel_id=1, source_target_pairs={{0,64},{64,128},{128,192},{192,0},{1,65},{65,129},{129,193},{193,1... | collective-permute-start | bytes 294920 | tf_op jit(solution)/shard_map/ppermute | solution.py:372
  14.0 3.9 %collective-permute-done.2.x_low = bf16[24,16,128]{2,1,0:T(8,128)(2,1)S(1)} collective-permute-done((bf16[24,16,128]{2,1,0:T(8,128)(2,1)S(1)}, bf16[24,16,128]{2,1,0:T(8,128)(2,1)S(1)}, u32[]{:S(2)}, u32[]{:S(2)}) %collective-permute-start.2) | collective-permute-done | bytes 98336 | tf_op jit(solution)/shard_map/ppermute | solution.py:372
  17.9 1.1 %collective-permute-start.3 = (bf16[24,16,128]{2,1,0:T(8,128)(2,1)S(1)}, bf16[24,16,128]{2,1,0:T(8,128)(2,1)S(1)}, u32[]{:S(2)}, u32[]{:S(2)}) collective-permute-start(bf16[24,16,128]{2,1,0:T(8,128)(2,1)S(1)} %get-tuple-element.28), channel_id=1, source_target_pairs={{0,192},{64,0},{128,64},{192,128},{1,193},{65,1},{129,65},{193,129... | collective-permute-start | bytes 294920 | tf_op jit(solution)/shard_map/ppermute | solution.py:372
  19.0 0.0 copy-start
  19.0 0.0 copy-start.1
  19.0 0.0 copy-start.2
  19.0 4.3 %snap_project.1.snap_part = f32[64,128]{1,0:T(8,128)S(1)} custom-call(bf16[24,128,8,128]{3,2,1,0:T(8,128)(2,1)S(1)} %get-tuple-element.24.modes_in, bf16[24,64,8,128]{3,2,1,0:T(8,128)(2,1)S(1)} %get-tuple-element.33.snap_in), custom_call_target="tpu_custom_call" | custom-call | tf_op jit(solution)/shard_map/snap_project/pallas_call | solution.py:206
  23.3 0.0 collective-permute-done.3.x_high
  23.3 0.0 collective-permute-done.z_low
  23.3 0.0 collective-permute-done.1.z_high
  23.3 0.0 copy-done
  23.4 0.0 copy-done.1
  23.4 0.0 copy-done.2
  23.4 6.7 %feature_project.1 = (f32[4,1024,128]{2,1,0:T(8,128)S(1)}, f32[192,4,8,128]{3,2,1,0:T(8,128)S(1)}) custom-call(bf16[24,128,8,128]{3,2,1,0:T(8,128)(2,1)S(1)} %get-tuple-element.24.modes_in, bf16[192,64,128]{2,1,0:T(8,128)(2,1)S(1)} %get-tuple-element.23.snap, bf16[192,16,128]{2,1,0:T(8,128)(2,1)S(1)} %collective-permute-done.z_low, ...), custom_call_target="tpu_custom_call" | custom-call | tf_op jit(solution)/shard_map/feature_project/pallas_call | solution.py:272
  30.1 0.0 collective-permute-done.4.y_low
  30.1 0.0 collective-permute-done.5.y_high
  30.1 3.4 %edge_project.1 = (f32[64,128]{1,0:T(8,128)S(1)}, f32[64,128]{1,0:T(8,128)S(1)}) custom-call(bf16[24,128,8,128]{3,2,1,0:T(8,128)(2,1)S(1)} %get-tuple-element.24.modes_in, bf16[192,64,128]{2,1,0:T(8,128)(2,1)S(1)} %get-tuple-element.23.snap, f32[192,4,8,128]{3,2,1,0:T(8,128)S(1)} %get-tuple-element.29.edges, ...), custom_call_target="tpu_custom_call" | custom-call | tf_op jit(solution)/shard_map/edge_project/pallas_call | solution.py:335
  33.5 5.5 %collective-permute-start.6 = (f32[64,128]{1,0:T(8,128)S(1)}, f32[64,128]{1,0:T(8,128)S(1)}, u32[]{:S(2)}, u32[]{:S(2)}) collective-permute-start(f32[64,128]{1,0:T(8,128)S(1)} %get-tuple-element.35), channel_id=1, source_target_pairs={{0,1},{1,0},{2,3},{3,2},{4,5},{5,4},{6,7},{7,6},{8,9},{9,8},{10,11... | collective-permute-start | bytes 98312 | tf_op jit(solution)/shard_map/ppermute | solution.py:386
  39.0 0.9 %collective-permute-done.6 = f32[64,128]{1,0:T(8,128)S(1)} collective-permute-done((f32[64,128]{1,0:T(8,128)S(1)}, f32[64,128]{1,0:T(8,128)S(1)}, u32[]{:S(2)}, u32[]{:S(2)}) %collective-permute-start.6) | collective-permute-done | bytes 32800 | tf_op jit(solution)/shard_map/ppermute | solution.py:386
  39.8 0.4 collective-permute-start.7
  40.3 2.9 %collective-permute-done.7 = f32[64,128]{1,0:T(8,128)S(1)} collective-permute-done((f32[64,128]{1,0:T(8,128)S(1)}, f32[64,128]{1,0:T(8,128)S(1)}, u32[]{:S(2)}, u32[]{:S(2)}) %collective-permute-start.7) | collective-permute-done | bytes 32800 | tf_op jit(solution)/shard_map/ppermute | solution.py:382
  43.2 1.5 %collective-permute-start.8 = (f32[64,128]{1,0:T(8,128)S(1)}, f32[64,128]{1,0:T(8,128)S(1)}, u32[]{:S(2)}, u32[]{:S(2)}) collective-permute-start(f32[64,128]{1,0:T(8,128)S(1)} %add.25), channel_id=1, source_target_pairs={{0,193},{1,192},{64,129},{65,128},{128,65},{129,64},{192,1},{193,0... | collective-permute-start | bytes 98312 | tf_op jit(solution)/shard_map/ppermute | solution.py:382
  44.7 3.1 %collective-permute-done.8 = f32[64,128]{1,0:T(8,128)S(1)} collective-permute-done((f32[64,128]{1,0:T(8,128)S(1)}, f32[64,128]{1,0:T(8,128)S(1)}, u32[]{:S(2)}, u32[]{:S(2)}) %collective-permute-start.8) | collective-permute-done | bytes 32800 | tf_op jit(solution)/shard_map/ppermute | solution.py:382
  47.8 0.3 collective-permute-start.9
  48.1 3.0 %collective-permute-done.9 = f32[64,128]{1,0:T(8,128)S(1)} collective-permute-done((f32[64,128]{1,0:T(8,128)S(1)}, f32[64,128]{1,0:T(8,128)S(1)}, u32[]{:S(2)}, u32[]{:S(2)}) %collective-permute-start.9) | collective-permute-done | bytes 32800 | tf_op jit(solution)/shard_map/ppermute | solution.py:382
  51.1 1.7 %collective-permute-start.10 = (f32[64,128]{1,0:T(8,128)S(1)}, f32[64,128]{1,0:T(8,128)S(1)}, u32[]{:S(2)}, u32[]{:S(2)}) collective-permute-start(f32[64,128]{1,0:T(8,128)S(1)} %add.27), channel_id=1, source_target_pairs={{0,49},{1,48},{16,33},{17,32},{32,17},{33,16},{48,1},{49,0},{2,51}... | collective-permute-start | bytes 98312 | tf_op jit(solution)/shard_map/ppermute | solution.py:382
  52.9 2.8 %collective-permute-done.10 = f32[64,128]{1,0:T(8,128)S(1)} collective-permute-done((f32[64,128]{1,0:T(8,128)S(1)}, f32[64,128]{1,0:T(8,128)S(1)}, u32[]{:S(2)}, u32[]{:S(2)}) %collective-permute-start.10) | collective-permute-done | bytes 32800 | tf_op jit(solution)/shard_map/ppermute | solution.py:382
  55.7 0.0 collective-permute-start.11
  55.7 3.3 %collective-permute-done.11 = f32[64,128]{1,0:T(8,128)S(1)} collective-permute-done((f32[64,128]{1,0:T(8,128)S(1)}, f32[64,128]{1,0:T(8,128)S(1)}, u32[]{:S(2)}, u32[]{:S(2)}) %collective-permute-start.11) | collective-permute-done | bytes 32800 | tf_op jit(solution)/shard_map/ppermute | solution.py:382
  59.0 0.6 collective-permute-start.12
  59.6 4.2 %collective-permute-done.12 = f32[64,128]{1,0:T(8,128)S(1)} collective-permute-done((f32[64,128]{1,0:T(8,128)S(1)}, f32[64,128]{1,0:T(8,128)S(1)}, u32[]{:S(2)}, u32[]{:S(2)}) %collective-permute-start.12) | collective-permute-done | bytes 32800 | tf_op jit(solution)/shard_map/ppermute | solution.py:382
  63.8 2.2 %collective-permute-start.13 = (f32[64,128]{1,0:T(8,128)S(1)}, f32[64,128]{1,0:T(8,128)S(1)}, u32[]{:S(2)}, u32[]{:S(2)}) collective-permute-start(f32[64,128]{1,0:T(8,128)S(1)} %add.30), channel_id=1, source_target_pairs={{0,13},{1,12},{2,15},{3,14},{4,9},{5,8},{6,11},{7,10},{8,5},{9,4},... | collective-permute-start | bytes 98312 | tf_op jit(solution)/shard_map/ppermute | solution.py:382
  66.0 3.3 %collective-permute-done.13 = f32[64,128]{1,0:T(8,128)S(1)} collective-permute-done((f32[64,128]{1,0:T(8,128)S(1)}, f32[64,128]{1,0:T(8,128)S(1)}, u32[]{:S(2)}, u32[]{:S(2)}) %collective-permute-start.13) | collective-permute-done | bytes 32800 | tf_op jit(solution)/shard_map/ppermute | solution.py:382
  69.3 0.4 collective-permute-start.14
  69.7 0.9 %collective-permute-done.14.other = f32[64,128]{1,0:T(8,128)S(1)} collective-permute-done((f32[64,128]{1,0:T(8,128)S(1)}, f32[64,128]{1,0:T(8,128)S(1)}, u32[]{:S(2)}, u32[]{:S(2)}) %collective-permute-start.14) | collective-permute-done | bytes 32800 | tf_op jit(solution)/shard_map/ppermute | solution.py:386
  70.5 1.0 %grams.1 = (f32[64,128]{1,0:T(8,128)}, f32[64,128]{1,0:T(8,128)}, f32[128,128]{1,0:T(8,128)}, f32[128,128]{1,0:T(8,128)}, f32[64,64]{1,0:T(8,128)}) custom-call(f32[64,128]{1,0:T(8,128)S(1)} %add.31.mine, f32[64,128]{1,0:T(8,128)S(1)} %collective-permute-done.14.other), custom_call_target="tpu_custom_call" | custom-call | tf_op jit(solution)/shard_map/grams/pallas_call | solution.py:362
  (8 shorter events, 0.0 us)
Async XLA Ops:
  7.0 16.3 %collective-permute-start = (bf16[192,16,128]{2,1,0:T(8,128)(2,1)S(1)}, bf16[192,16,128]{2,1,0:T(8,128)(2,1)S(1)}, u32[]{:S(2)}, u32[]{:S(2)}) collective-permute-start(bf16[192,16,128]{2,1,0:T(8,128)(2,1)S(1)} %get-tuple-element.25), channel_id=1, source_target_pairs={{0,1},{1,2},{2,3},{3,4},{4,5},{5,6},{6,7},{7,8},{8,9},{9,10},{10,1... | collective-permute-start | bytes 2359304 | tf_op jit(solution)/shard_map/ppermute | solution.py:372
  10.0 13.3 %collective-permute-start.1 = (bf16[192,16,128]{2,1,0:T(8,128)(2,1)S(1)}, bf16[192,16,128]{2,1,0:T(8,128)(2,1)S(1)}, u32[]{:S(2)}, u32[]{:S(2)}) collective-permute-start(bf16[192,16,128]{2,1,0:T(8,128)(2,1)S(1)} %get-tuple-element.26), channel_id=1, source_target_pairs={{0,15},{1,0},{2,1},{3,2},{4,3},{5,4},{6,5},{7,6},{8,7},{9,8},{10,9... | collective-permute-start | bytes 2359304 | tf_op jit(solution)/shard_map/ppermute | solution.py:372
  10.2 19.8 %collective-permute-start.4 = (bf16[192,16,128]{2,1,0:T(8,128)(2,1)S(1)}, bf16[192,16,128]{2,1,0:T(8,128)(2,1)S(1)}, u32[]{:S(2)}, u32[]{:S(2)}) collective-permute-start(bf16[192,16,128]{2,1,0:T(8,128)(2,1)S(1)} %get-tuple-element.30), channel_id=1, source_target_pairs={{0,16},{16,32},{32,48},{48,0},{1,17},{17,33},{33,49},{49,1},{2,18}... | collective-permute-start | bytes 2359304 | tf_op jit(solution)/shard_map/ppermute | solution.py:372
  11.3 18.8 %collective-permute-start.5 = (bf16[192,16,128]{2,1,0:T(8,128)(2,1)S(1)}, bf16[192,16,128]{2,1,0:T(8,128)(2,1)S(1)}, u32[]{:S(2)}, u32[]{:S(2)}) collective-permute-start(bf16[192,16,128]{2,1,0:T(8,128)(2,1)S(1)} %get-tuple-element.31), channel_id=1, source_target_pairs={{0,48},{16,0},{32,16},{48,32},{1,49},{17,1},{33,17},{49,33},{2,50}... | collective-permute-start | bytes 2359304 | tf_op jit(solution)/shard_map/ppermute | solution.py:372
  12.9 5.0 %collective-permute-start.2 = (bf16[24,16,128]{2,1,0:T(8,128)(2,1)S(1)}, bf16[24,16,128]{2,1,0:T(8,128)(2,1)S(1)}, u32[]{:S(2)}, u32[]{:S(2)}) collective-permute-start(bf16[24,16,128]{2,1,0:T(8,128)(2,1)S(1)} %get-tuple-element.27), channel_id=1, source_target_pairs={{0,64},{64,128},{128,192},{192,0},{1,65},{65,129},{129,193},{193,1... | collective-permute-start | bytes 294920 | tf_op jit(solution)/shard_map/ppermute | solution.py:372
  17.9 5.4 %collective-permute-start.3 = (bf16[24,16,128]{2,1,0:T(8,128)(2,1)S(1)}, bf16[24,16,128]{2,1,0:T(8,128)(2,1)S(1)}, u32[]{:S(2)}, u32[]{:S(2)}) collective-permute-start(bf16[24,16,128]{2,1,0:T(8,128)(2,1)S(1)} %get-tuple-element.28), channel_id=1, source_target_pairs={{0,192},{64,0},{128,64},{192,128},{1,193},{65,1},{129,65},{193,129... | collective-permute-start | bytes 294920 | tf_op jit(solution)/shard_map/ppermute | solution.py:372
  19.0 4.3 %copy-start = (bf16[8,64,128]{2,1,0:T(8,128)(2,1)S(1)}, bf16[8,64,128]{2,1,0:T(8,128)(2,1)}, u32[]{:S(2)}) copy-start(bf16[8,64,128]{2,1,0:T(8,128)(2,1)} %constant.8.clone.masks) | copy-start | bytes 393220
  19.0 4.3 %copy-start.1 = (bf16[256,256]{1,0:T(8,128)(2,1)S(1)}, bf16[256,256]{1,0:T(8,128)(2,1)}, u32[]{:S(2)}) copy-start(bf16[256,256]{1,0:T(8,128)(2,1)} %constant.7.clone.stream) | copy-start | bytes 393220
  19.0 4.3 %copy-start.2 = (bf16[128,96]{1,0:T(8,128)(2,1)S(1)}, bf16[128,96]{1,0:T(8,128)(2,1)}, u32[]{:S(2)}) copy-start(bf16[128,96]{1,0:T(8,128)(2,1)} %constant.6.clone.span) | copy-start | bytes 73732
  33.5 6.3 %collective-permute-start.6 = (f32[64,128]{1,0:T(8,128)S(1)}, f32[64,128]{1,0:T(8,128)S(1)}, u32[]{:S(2)}, u32[]{:S(2)}) collective-permute-start(f32[64,128]{1,0:T(8,128)S(1)} %get-tuple-element.35), channel_id=1, source_target_pairs={{0,1},{1,0},{2,3},{3,2},{4,5},{5,4},{6,7},{7,6},{8,9},{9,8},{10,11... | collective-permute-start | bytes 98312 | tf_op jit(solution)/shard_map/ppermute | solution.py:386
  39.8 3.3 %collective-permute-start.7 = (f32[64,128]{1,0:T(8,128)S(1)}, f32[64,128]{1,0:T(8,128)S(1)}, u32[]{:S(2)}, u32[]{:S(2)}) collective-permute-start(f32[64,128]{1,0:T(8,128)S(1)} %add.24), channel_id=1, source_target_pairs={{0,65},{1,64},{64,1},{65,0},{128,193},{129,192},{192,129},{193,128... | collective-permute-start | bytes 98312 | tf_op jit(solution)/shard_map/ppermute | solution.py:382
  43.2 4.6 %collective-permute-start.8 = (f32[64,128]{1,0:T(8,128)S(1)}, f32[64,128]{1,0:T(8,128)S(1)}, u32[]{:S(2)}, u32[]{:S(2)}) collective-permute-start(f32[64,128]{1,0:T(8,128)S(1)} %add.25), channel_id=1, source_target_pairs={{0,193},{1,192},{64,129},{65,128},{128,65},{129,64},{192,1},{193,0... | collective-permute-start | bytes 98312 | tf_op jit(solution)/shard_map/ppermute | solution.py:382
  47.8 3.3 %collective-permute-start.9 = (f32[64,128]{1,0:T(8,128)S(1)}, f32[64,128]{1,0:T(8,128)S(1)}, u32[]{:S(2)}, u32[]{:S(2)}) collective-permute-start(f32[64,128]{1,0:T(8,128)S(1)} %add.26), channel_id=1, source_target_pairs={{0,17},{1,16},{16,1},{17,0},{32,49},{33,48},{48,33},{49,32},{2,19}... | collective-permute-start | bytes 98312 | tf_op jit(solution)/shard_map/ppermute | solution.py:382
  51.1 4.6 %collective-permute-start.10 = (f32[64,128]{1,0:T(8,128)S(1)}, f32[64,128]{1,0:T(8,128)S(1)}, u32[]{:S(2)}, u32[]{:S(2)}) collective-permute-start(f32[64,128]{1,0:T(8,128)S(1)} %add.27), channel_id=1, source_target_pairs={{0,49},{1,48},{16,33},{17,32},{32,17},{33,16},{48,1},{49,0},{2,51}... | collective-permute-start | bytes 98312 | tf_op jit(solution)/shard_map/ppermute | solution.py:382
  55.7 3.3 %collective-permute-start.11 = (f32[64,128]{1,0:T(8,128)S(1)}, f32[64,128]{1,0:T(8,128)S(1)}, u32[]{:S(2)}, u32[]{:S(2)}) collective-permute-start(f32[64,128]{1,0:T(8,128)S(1)} %add.28), channel_id=1, source_target_pairs={{0,3},{1,2},{2,1},{3,0},{4,7},{5,6},{6,5},{7,4},{8,11},{9,10},{10,... | collective-permute-start | bytes 98312 | tf_op jit(solution)/shard_map/ppermute | solution.py:382
  59.0 4.8 %collective-permute-start.12 = (f32[64,128]{1,0:T(8,128)S(1)}, f32[64,128]{1,0:T(8,128)S(1)}, u32[]{:S(2)}, u32[]{:S(2)}) collective-permute-start(f32[64,128]{1,0:T(8,128)S(1)} %add.29), channel_id=1, source_target_pairs={{0,5},{1,4},{2,7},{3,6},{4,1},{5,0},{6,3},{7,2},{8,13},{9,12},{10,... | collective-permute-start | bytes 98312 | tf_op jit(solution)/shard_map/ppermute | solution.py:382
  63.8 5.5 %collective-permute-start.13 = (f32[64,128]{1,0:T(8,128)S(1)}, f32[64,128]{1,0:T(8,128)S(1)}, u32[]{:S(2)}, u32[]{:S(2)}) collective-permute-start(f32[64,128]{1,0:T(8,128)S(1)} %add.30), channel_id=1, source_target_pairs={{0,13},{1,12},{2,15},{3,14},{4,9},{5,8},{6,11},{7,10},{8,5},{9,4},... | collective-permute-start | bytes 98312 | tf_op jit(solution)/shard_map/ppermute | solution.py:382
  69.3 1.3 %collective-permute-start.14 = (f32[64,128]{1,0:T(8,128)S(1)}, f32[64,128]{1,0:T(8,128)S(1)}, u32[]{:S(2)}, u32[]{:S(2)}) collective-permute-start(f32[64,128]{1,0:T(8,128)S(1)} %add.31.mine), channel_id=1, source_target_pairs={{0,1},{1,0},{2,3},{3,2},{4,5},{5,4},{6,7},{7,6},{8,9},{9,8},{10,11... | collective-permute-start | bytes 98312 | tf_op jit(solution)/shard_map/ppermute | solution.py:386

commit v6 on v5

--- a/solution.py
+++ b/solution.py
@@ -110,18 +110,38 @@
     )(from_hbm(snap))
 
 
-def side_pack_body(snap, modes_hbm, snap_hbm, low, high, right, left, modes_in, snap_in, sems):
-    copies = []
-    for k in range(24):
-        copies.append(pltpu.make_async_copy(modes_hbm.at[:, k], modes_in.at[k], sems.at[0, k]))
-        copies.append(pltpu.make_async_copy(snap_hbm.at[:, k], snap_in.at[k], sems.at[1, k]))
+def plane_copies(array, planes, sems):
+    return [pltpu.make_async_copy(array.at[:, k], planes.at[k], sems.at[k]) for k in range(24)]
+
+
+def span_pack_body(snap, snap_hbm, low, high, snap_in, sems):
+    copies = plane_copies(snap_hbm, snap_in, sems)
     for c in copies:
         c.start()
-    grid = lambda shape: [lax.broadcasted_iota(jnp.int32, shape, d) for d in range(2)]
-    row, col = grid((32, 64))
+    row, col = (lax.broadcasted_iota(jnp.int32, (32, 64), d) for d in range(2))
     wanted = (row % 16) // 2 * 8 + row % 2 + jnp.where(row < 16, 0, 6)
     span = (col == wanted).astype(F32).astype(BF16)
-    row, col = grid((128, 256))
+
+    def group_of(group, _):
+        for pair in range(4):
+            unit = 8 * group + 2 * pair
+            both = jnp.concatenate([snap[unit], snap[unit + 1]], axis=1)
+            picked = jnp.dot(span, both, preferred_element_type=F32).astype(BF16)
+            for i in range(2):
+                low[unit + i] = picked[:16, 128 * i : 128 * (i + 1)]
+                high[unit + i] = picked[16:, 128 * i : 128 * (i + 1)]
+        return _
+
+    lax.fori_loop(0, 24, group_of, 0, unroll=4)
+    for c in copies:
+        c.wait()
+
+
+def stream_pack_body(snap, modes_hbm, right, left, modes_in, sems):
+    copies = plane_copies(modes_hbm, modes_in, sems)
+    for c in copies:
+        c.start()
+    row, col = (lax.broadcasted_iota(jnp.int32, (128, 256), d) for d in range(2))
     last = (col < 128) & (col % 4 < 2) & (row == 126 + col % 4)
     first = (col >= 128) & (col % 4 >= 2) & (row == col % 4 - 2)
     lanes = (last | first).astype(F32).astype(BF16)
@@ -129,12 +149,6 @@
 
     def group_of(group, _):
         units = [snap[8 * group + m] for m in range(8)]
-        for pair in range(4):
-            both = jnp.concatenate(units[2 * pair : 2 * pair + 2], axis=1)
-            picked = jnp.dot(span, both, preferred_element_type=F32).astype(BF16)
-            for i in range(2):
-                low[8 * group + 2 * pair + i] = picked[:16, 128 * i : 128 * (i + 1)]
-                high[8 * group + 2 * pair + i] = picked[16:, 128 * i : 128 * (i + 1)]
         ends = jnp.dot(jnp.concatenate(units, axis=0), lanes, preferred_element_type=F32)
         to_right = jnp.zeros((16, 128), F32)
         to_left = jnp.zeros((16, 128), F32)
@@ -150,24 +164,16 @@
         c.wait()
 
 
-def side_pack(snap, modes, planes):
-    wide, slim = jax.ShapeDtypeStruct((192, 16, 128), BF16), jax.ShapeDtypeStruct((24, 16, 128), BF16)
-    return pl.pallas_call(
-        side_pack_body,
-        out_shape=(
-            wide,
-            wide,
-            slim,
-            slim,
-            jax.ShapeDtypeStruct((24, 128, 8, 128), BF16),
-            jax.ShapeDtypeStruct((24, 64, 8, 128), BF16),
-        ),
-        in_specs=[resident(), in_hbm(), in_hbm()],
-        out_specs=(resident(),) * 6,
-        scratch_shapes=[pltpu.SemaphoreType.DMA((2, 24))],
-        compiler_params=pltpu.CompilerParams(vmem_limit_bytes=VMEM_LIMIT),
-        name="side_pack",
-    )(in_vmem(snap), from_hbm(modes), from_hbm(planes))
+def packed(body, rows, snap, array):
+    halo = jax.ShapeDtypeStruct((rows, 16, 128), BF16)
+    return pl.pallas_call(
+        body,
+        out_shape=(halo, halo, jax.ShapeDtypeStruct((24, array.shape[0], 8, 128), BF16)),
+        in_specs=[resident(), in_hbm()],
+        out_specs=(resident(),) * 3,
+        scratch_shapes=[pltpu.SemaphoreType.DMA((24,))],
+        compiler_params=pltpu.CompilerParams(vmem_limit_bytes=VMEM_LIMIT),
+    )(in_vmem(snap), from_hbm(array))
 
 
 def same_span(total, half, out):
@@ -401,11 +407,10 @@
     low, high, units = wall_pack(snapshots.reshape(192, 64, 128))
     y_low = shifted(high, "gy", 4, 1)
     y_high = shifted(low, "gy", 4, -1)
-    low, high, right, left, modes_in, snap_in = side_pack(
-        units, modes.reshape(128, 24, 8, 128), snapshots.reshape(64, 24, 8, 128)
-    )
+    low, high, snap_in = packed(span_pack_body, 192, units, snapshots.reshape(64, 24, 8, 128))
     z_low = shifted(high, GZ, 16, 1)
     z_high = shifted(low, GZ, 16, -1)
+    right, left, modes_in = packed(stream_pack_body, 24, units, modes.reshape(128, 24, 8, 128))
     x_low = shifted(right, "gx", 4, 1)
     x_high = shifted(left, "gx", 4, -1)
     snap_part = snap_project(modes_in, snap_in)

time: 71.6 us -> 72.7 us (1.015)
  Pallas kernels: 21.7 us -> 22.7 us
    pallas_call x1 -> x2, Pallas kernels: 4.39 us -> 5.38 us  [packed(): pl.pallas_call(body, out_shape=(halo, halo, jax.ShapeDtypeStruct((24, arr...]
  transfers between devices with their start and end apart: 15 -> 15, of which waited for: 10 -> 10; matrix products, arithmetic and copies ran while one was open for 0% -> 0% of each run, Pallas kernels for 15% -> 19%
where the time goes in v6:
time: 72.7 us; the launch traced here: 72.6 us
  waiting for transfers between devices  28.2 us (39%)
  Pallas kernels  22.7 us (31%)
  starting transfers between devices  20.8 us (29%)
  between operations  0.76 us (1%)
    ppermute x7, waiting for transfers between devices, swapped(): return lax.ppermute(value, (axis, 'gz_1'), pairs)  22.6 us
    ppermute x6, starting transfers between devices, shifted(): lax.ppermute(value, axis, [(i, (i + by) % count) for i in range(count)])  8.18 us
    ppermute x7, starting transfers between devices, swapped(): return lax.ppermute(value, (axis, 'gz_1'), pairs)  6.81 us
    pallas_call x1, Pallas kernels, feature_project(): pl.pallas_call(feature_body, out_shape=(jax.ShapeDtypeStruct((4, 1024, 12...  6.71 us
    ppermute x2, starting transfers between devices, other_core(): return lax.ppermute(value, 'gz_1', [(0, 1), (1, 0)])  5.86 us
    pallas_call x2, Pallas kernels, packed(): pl.pallas_call(body, out_shape=(halo, halo, jax.ShapeDtypeStruct((24, arr...  5.38 us
    pallas_call x1, Pallas kernels, snap_project(): pl.pallas_call(snap_project_body, out_shape=jax.ShapeDtypeStruct((64, 128...  4.27 us
    ppermute x6, waiting for transfers between devices, shifted(): lax.ppermute(value, axis, [(i, (i + by) % count) for i in range(count)])  3.92 us
  transfers between devices with their start and end apart: 15, of which 10 were waited for; matrix products, arithmetic and copies ran while one was open for 0% of the time, Pallas kernels for 19%

profile of v6, /device:TPU:1, one launch (start us, length us, event | category | flops | bytes accessed | tf_op | source)
XLA Modules:
  0.0 72.6 jit_solution(10224356941751832726)
XLA Ops:
  0.6 2.0 %wall_pack.1 = (bf16[192,16,128]{2,1,0:T(8,128)(2,1)S(1)}, bf16[192,16,128]{2,1,0:T(8,128)(2,1)S(1)}, bf16[192,64,128]{2,1,0:T(8,128)(2,1)S(1)}) custom-call(bf16[192,64,128]{2,1,0:T(8,128)(2,1)} %bitcast.5), custom_call_target="tpu_custom_call" | custom-call | tf_op jit(solution)/shard_map/wall_pack/pallas_call | solution.py:102
  2.6 2.2 %shard_map.93 = (bf16[192,16,128]{2,1,0:T(8,128)(2,1)S(1)}, bf16[192,16,128]{2,1,0:T(8,128)(2,1)S(1)}, bf16[24,64,8,128]{3,2,1,0:T(8,128)(2,1)S(1)}) custom-call(bf16[192,64,128]{2,1,0:T(8,128)(2,1)S(1)} %get-tuple-element.23.snap, bf16[64,24,8,128]{3,2,1,0:T(8,128)(2,1)} %bitcast.6), custom_call_target="tpu_custom_call" | custom-call | tf_op jit(solution)/shard_map/pallas_call | solution.py:169
  4.8 3.0 %collective-permute-start = (bf16[192,16,128]{2,1,0:T(8,128)(2,1)S(1)}, bf16[192,16,128]{2,1,0:T(8,128)(2,1)S(1)}, u32[]{:S(2)}, u32[]{:S(2)}) collective-permute-start(bf16[192,16,128]{2,1,0:T(8,128)(2,1)S(1)} %get-tuple-element.25), channel_id=1, source_target_pairs={{0,1},{1,2},{2,3},{3,4},{4,5},{5,6},{6,7},{7,8},{8,9},{9,10},{10,1... | collective-permute-start | bytes 2359304 | tf_op jit(solution)/shard_map/ppermute | solution.py:378
  7.9 0.2 collective-permute-start.1
  8.1 1.1 %collective-permute-start.4 = (bf16[192,16,128]{2,1,0:T(8,128)(2,1)S(1)}, bf16[192,16,128]{2,1,0:T(8,128)(2,1)S(1)}, u32[]{:S(2)}, u32[]{:S(2)}) collective-permute-start(bf16[192,16,128]{2,1,0:T(8,128)(2,1)S(1)} %get-tuple-element.30), channel_id=1, source_target_pairs={{0,16},{16,32},{32,48},{48,0},{1,17},{17,33},{33,49},{49,1},{2,18}... | collective-permute-start | bytes 2359304 | tf_op jit(solution)/shard_map/ppermute | solution.py:378
  9.2 1.6 %collective-permute-start.5 = (bf16[192,16,128]{2,1,0:T(8,128)(2,1)S(1)}, bf16[192,16,128]{2,1,0:T(8,128)(2,1)S(1)}, u32[]{:S(2)}, u32[]{:S(2)}) collective-permute-start(bf16[192,16,128]{2,1,0:T(8,128)(2,1)S(1)} %get-tuple-element.31), channel_id=1, source_target_pairs={{0,48},{16,0},{32,16},{48,32},{1,49},{17,1},{33,17},{49,33},{2,50}... | collective-permute-start | bytes 2359304 | tf_op jit(solution)/shard_map/ppermute | solution.py:378
  10.8 3.2 %shard_map.92 = (bf16[24,16,128]{2,1,0:T(8,128)(2,1)S(1)}, bf16[24,16,128]{2,1,0:T(8,128)(2,1)S(1)}, bf16[24,128,8,128]{3,2,1,0:T(8,128)(2,1)S(1)}) custom-call(bf16[192,64,128]{2,1,0:T(8,128)(2,1)S(1)} %get-tuple-element.23.snap, bf16[128,24,8,128]{3,2,1,0:T(8,128)(2,1)} %bitcast.7), custom_call_target="tpu_custom_call" | custom-call | tf_op jit(solution)/shard_map/pallas_call | solution.py:169
  13.9 1.1 %collective-permute-start.2 = (bf16[24,16,128]{2,1,0:T(8,128)(2,1)S(1)}, bf16[24,16,128]{2,1,0:T(8,128)(2,1)S(1)}, u32[]{:S(2)}, u32[]{:S(2)}) collective-permute-start(bf16[24,16,128]{2,1,0:T(8,128)(2,1)S(1)} %get-tuple-element.27), channel_id=1, source_target_pairs={{0,64},{64,128},{128,192},{192,0},{1,65},{65,129},{129,193},{193,1... | collective-permute-start | bytes 294920 | tf_op jit(solution)/shard_map/ppermute | solution.py:378
  15.1 3.9 %collective-permute-done.2.x_low = bf16[24,16,128]{2,1,0:T(8,128)(2,1)S(1)} collective-permute-done((bf16[24,16,128]{2,1,0:T(8,128)(2,1)S(1)}, bf16[24,16,128]{2,1,0:T(8,128)(2,1)S(1)}, u32[]{:S(2)}, u32[]{:S(2)}) %collective-permute-start.2) | collective-permute-done | bytes 98336 | tf_op jit(solution)/shard_map/ppermute | solution.py:378
  19.0 1.1 %collective-permute-start.3 = (bf16[24,16,128]{2,1,0:T(8,128)(2,1)S(1)}, bf16[24,16,128]{2,1,0:T(8,128)(2,1)S(1)}, u32[]{:S(2)}, u32[]{:S(2)}) collective-permute-start(bf16[24,16,128]{2,1,0:T(8,128)(2,1)S(1)} %get-tuple-element.28), channel_id=1, source_target_pairs={{0,192},{64,0},{128,64},{192,128},{1,193},{65,1},{129,65},{193,129... | collective-permute-start | bytes 294920 | tf_op jit(solution)/shard_map/ppermute | solution.py:378
  20.1 0.0 copy-start
  20.1 0.0 copy-start.1
  20.1 0.0 copy-start.2
  20.1 4.3 %snap_project.1.snap_part = f32[64,128]{1,0:T(8,128)S(1)} custom-call(bf16[24,128,8,128]{3,2,1,0:T(8,128)(2,1)S(1)} %get-tuple-element.24.modes_in, bf16[24,64,8,128]{3,2,1,0:T(8,128)(2,1)S(1)} %get-tuple-element.33.snap_in), custom_call_target="tpu_custom_call" | custom-call | tf_op jit(solution)/shard_map/snap_project/pallas_call | solution.py:212
  24.4 0.0 collective-permute-done.3.x_high
  24.4 0.0 collective-permute-done.z_low
  24.4 0.0 collective-permute-done.1.z_high
  24.4 0.0 copy-done
  24.4 0.0 copy-done.1
  24.4 0.0 copy-done.2
  24.4 6.7 %feature_project.1 = (f32[4,1024,128]{2,1,0:T(8,128)S(1)}, f32[192,4,8,128]{3,2,1,0:T(8,128)S(1)}) custom-call(bf16[24,128,8,128]{3,2,1,0:T(8,128)(2,1)S(1)} %get-tuple-element.24.modes_in, bf16[192,64,128]{2,1,0:T(8,128)(2,1)S(1)} %get-tuple-element.23.snap, bf16[192,16,128]{2,1,0:T(8,128)(2,1)S(1)} %collective-permute-done.z_low, ...), custom_call_target="tpu_custom_call" | custom-call | tf_op jit(solution)/shard_map/feature_project/pallas_call | solution.py:278
  31.2 0.0 collective-permute-done.4.y_low
  31.2 0.0 collective-permute-done.5.y_high
  31.2 3.4 %edge_project.1 = (f32[64,128]{1,0:T(8,128)S(1)}, f32[64,128]{1,0:T(8,128)S(1)}) custom-call(bf16[24,128,8,128]{3,2,1,0:T(8,128)(2,1)S(1)} %get-tuple-element.24.modes_in, bf16[192,64,128]{2,1,0:T(8,128)(2,1)S(1)} %get-tuple-element.23.snap, f32[192,4,8,128]{3,2,1,0:T(8,128)S(1)} %get-tuple-element.29.edges, ...), custom_call_target="tpu_custom_call" | custom-call | tf_op jit(solution)/shard_map/edge_project/pallas_call | solution.py:341
  34.6 5.5 %collective-permute-start.6 = (f32[64,128]{1,0:T(8,128)S(1)}, f32[64,128]{1,0:T(8,128)S(1)}, u32[]{:S(2)}, u32[]{:S(2)}) collective-permute-start(f32[64,128]{1,0:T(8,128)S(1)} %get-tuple-element.35), channel_id=1, source_target_pairs={{0,1},{1,0},{2,3},{3,2},{4,5},{5,4},{6,7},{7,6},{8,9},{9,8},{10,11... | collective-permute-start | bytes 98312 | tf_op jit(solution)/shard_map/ppermute | solution.py:392
  40.0 0.9 %collective-permute-done.6 = f32[64,128]{1,0:T(8,128)S(1)} collective-permute-done((f32[64,128]{1,0:T(8,128)S(1)}, f32[64,128]{1,0:T(8,128)S(1)}, u32[]{:S(2)}, u32[]{:S(2)}) %collective-permute-start.6) | collective-permute-done | bytes 32800 | tf_op jit(solution)/shard_map/ppermute | solution.py:392
  40.9 0.4 collective-permute-start.7
  41.3 2.9 %collective-permute-done.7 = f32[64,128]{1,0:T(8,128)S(1)} collective-permute-done((f32[64,128]{1,0:T(8,128)S(1)}, f32[64,128]{1,0:T(8,128)S(1)}, u32[]{:S(2)}, u32[]{:S(2)}) %collective-permute-start.7) | collective-permute-done | bytes 32800 | tf_op jit(solution)/shard_map/ppermute | solution.py:388
  44.3 1.5 %collective-permute-start.8 = (f32[64,128]{1,0:T(8,128)S(1)}, f32[64,128]{1,0:T(8,128)S(1)}, u32[]{:S(2)}, u32[]{:S(2)}) collective-permute-start(f32[64,128]{1,0:T(8,128)S(1)} %add.25), channel_id=1, source_target_pairs={{0,193},{1,192},{64,129},{65,128},{128,65},{129,64},{192,1},{193,0... | collective-permute-start | bytes 98312 | tf_op jit(solution)/shard_map/ppermute | solution.py:388
  45.7 3.1 %collective-permute-done.8 = f32[64,128]{1,0:T(8,128)S(1)} collective-permute-done((f32[64,128]{1,0:T(8,128)S(1)}, f32[64,128]{1,0:T(8,128)S(1)}, u32[]{:S(2)}, u32[]{:S(2)}) %collective-permute-start.8) | collective-permute-done | bytes 32800 | tf_op jit(solution)/shard_map/ppermute | solution.py:388
  48.8 0.3 collective-permute-start.9
  49.1 3.0 %collective-permute-done.9 = f32[64,128]{1,0:T(8,128)S(1)} collective-permute-done((f32[64,128]{1,0:T(8,128)S(1)}, f32[64,128]{1,0:T(8,128)S(1)}, u32[]{:S(2)}, u32[]{:S(2)}) %collective-permute-start.9) | collective-permute-done | bytes 32800 | tf_op jit(solution)/shard_map/ppermute | solution.py:388
  52.2 1.7 %collective-permute-start.10 = (f32[64,128]{1,0:T(8,128)S(1)}, f32[64,128]{1,0:T(8,128)S(1)}, u32[]{:S(2)}, u32[]{:S(2)}) collective-permute-start(f32[64,128]{1,0:T(8,128)S(1)} %add.27), channel_id=1, source_target_pairs={{0,49},{1,48},{16,33},{17,32},{32,17},{33,16},{48,1},{49,0},{2,51}... | collective-permute-start | bytes 98312 | tf_op jit(solution)/shard_map/ppermute | solution.py:388
  53.9 2.8 %collective-permute-done.10 = f32[64,128]{1,0:T(8,128)S(1)} collective-permute-done((f32[64,128]{1,0:T(8,128)S(1)}, f32[64,128]{1,0:T(8,128)S(1)}, u32[]{:S(2)}, u32[]{:S(2)}) %collective-permute-start.10) | collective-permute-done | bytes 32800 | tf_op jit(solution)/shard_map/ppermute | solution.py:388
  56.7 0.0 collective-permute-start.11
  56.7 3.3 %collective-permute-done.11 = f32[64,128]{1,0:T(8,128)S(1)} collective-permute-done((f32[64,128]{1,0:T(8,128)S(1)}, f32[64,128]{1,0:T(8,128)S(1)}, u32[]{:S(2)}, u32[]{:S(2)}) %collective-permute-start.11) | collective-permute-done | bytes 32800 | tf_op jit(solution)/shard_map/ppermute | solution.py:388
  60.1 0.6 collective-permute-start.12
  60.7 4.1 %collective-permute-done.12 = f32[64,128]{1,0:T(8,128)S(1)} collective-permute-done((f32[64,128]{1,0:T(8,128)S(1)}, f32[64,128]{1,0:T(8,128)S(1)}, u32[]{:S(2)}, u32[]{:S(2)}) %collective-permute-start.12) | collective-permute-done | bytes 32800 | tf_op jit(solution)/shard_map/ppermute | solution.py:388
  64.9 2.2 %collective-permute-start.13 = (f32[64,128]{1,0:T(8,128)S(1)}, f32[64,128]{1,0:T(8,128)S(1)}, u32[]{:S(2)}, u32[]{:S(2)}) collective-permute-start(f32[64,128]{1,0:T(8,128)S(1)} %add.30), channel_id=1, source_target_pairs={{0,13},{1,12},{2,15},{3,14},{4,9},{5,8},{6,11},{7,10},{8,5},{9,4},... | collective-permute-start | bytes 98312 | tf_op jit(solution)/shard_map/ppermute | solution.py:388
  67.1 3.3 %collective-permute-done.13 = f32[64,128]{1,0:T(8,128)S(1)} collective-permute-done((f32[64,128]{1,0:T(8,128)S(1)}, f32[64,128]{1,0:T(8,128)S(1)}, u32[]{:S(2)}, u32[]{:S(2)}) %collective-permute-start.13) | collective-permute-done | bytes 32800 | tf_op jit(solution)/shard_map/ppermute | solution.py:388
  70.4 0.4 collective-permute-start.14
  70.8 0.9 %collective-permute-done.14.other = f32[64,128]{1,0:T(8,128)S(1)} collective-permute-done((f32[64,128]{1,0:T(8,128)S(1)}, f32[64,128]{1,0:T(8,128)S(1)}, u32[]{:S(2)}, u32[]{:S(2)}) %collective-permute-start.14) | collective-permute-done | bytes 32800 | tf_op jit(solution)/shard_map/ppermute | solution.py:392
  71.6 1.0 %grams.1 = (f32[64,128]{1,0:T(8,128)}, f32[64,128]{1,0:T(8,128)}, f32[128,128]{1,0:T(8,128)}, f32[128,128]{1,0:T(8,128)}, f32[64,64]{1,0:T(8,128)}) custom-call(f32[64,128]{1,0:T(8,128)S(1)} %add.31.mine, f32[64,128]{1,0:T(8,128)S(1)} %collective-permute-done.14.other), custom_call_target="tpu_custom_call" | custom-call | tf_op jit(solution)/shard_map/grams/pallas_call | solution.py:368
  (8 shorter events, 0.0 us)
Async XLA Ops:
  4.8 19.5 %collective-permute-start = (bf16[192,16,128]{2,1,0:T(8,128)(2,1)S(1)}, bf16[192,16,128]{2,1,0:T(8,128)(2,1)S(1)}, u32[]{:S(2)}, u32[]{:S(2)}) collective-permute-start(bf16[192,16,128]{2,1,0:T(8,128)(2,1)S(1)} %get-tuple-element.25), channel_id=1, source_target_pairs={{0,1},{1,2},{2,3},{3,4},{4,5},{5,6},{6,7},{7,8},{8,9},{9,10},{10,1... | collective-permute-start | bytes 2359304 | tf_op jit(solution)/shard_map/ppermute | solution.py:378
  7.9 16.5 %collective-permute-start.1 = (bf16[192,16,128]{2,1,0:T(8,128)(2,1)S(1)}, bf16[192,16,128]{2,1,0:T(8,128)(2,1)S(1)}, u32[]{:S(2)}, u32[]{:S(2)}) collective-permute-start(bf16[192,16,128]{2,1,0:T(8,128)(2,1)S(1)} %get-tuple-element.26), channel_id=1, source_target_pairs={{0,15},{1,0},{2,1},{3,2},{4,3},{5,4},{6,5},{7,6},{8,7},{9,8},{10,9... | collective-permute-start | bytes 2359304 | tf_op jit(solution)/shard_map/ppermute | solution.py:378
  8.1 23.1 %collective-permute-start.4 = (bf16[192,16,128]{2,1,0:T(8,128)(2,1)S(1)}, bf16[192,16,128]{2,1,0:T(8,128)(2,1)S(1)}, u32[]{:S(2)}, u32[]{:S(2)}) collective-permute-start(bf16[192,16,128]{2,1,0:T(8,128)(2,1)S(1)} %get-tuple-element.30), channel_id=1, source_target_pairs={{0,16},{16,32},{32,48},{48,0},{1,17},{17,33},{33,49},{49,1},{2,18}... | collective-permute-start | bytes 2359304 | tf_op jit(solution)/shard_map/ppermute | solution.py:378
  9.2 22.0 %collective-permute-start.5 = (bf16[192,16,128]{2,1,0:T(8,128)(2,1)S(1)}, bf16[192,16,128]{2,1,0:T(8,128)(2,1)S(1)}, u32[]{:S(2)}, u32[]{:S(2)}) collective-permute-start(bf16[192,16,128]{2,1,0:T(8,128)(2,1)S(1)} %get-tuple-element.31), channel_id=1, source_target_pairs={{0,48},{16,0},{32,16},{48,32},{1,49},{17,1},{33,17},{49,33},{2,50}... | collective-permute-start | bytes 2359304 | tf_op jit(solution)/shard_map/ppermute | solution.py:378
  13.9 5.0 %collective-permute-start.2 = (bf16[24,16,128]{2,1,0:T(8,128)(2,1)S(1)}, bf16[24,16,128]{2,1,0:T(8,128)(2,1)S(1)}, u32[]{:S(2)}, u32[]{:S(2)}) collective-permute-start(bf16[24,16,128]{2,1,0:T(8,128)(2,1)S(1)} %get-tuple-element.27), channel_id=1, source_target_pairs={{0,64},{64,128},{128,192},{192,0},{1,65},{65,129},{129,193},{193,1... | collective-permute-start | bytes 294920 | tf_op jit(solution)/shard_map/ppermute | solution.py:378
  19.0 5.4 %collective-permute-start.3 = (bf16[24,16,128]{2,1,0:T(8,128)(2,1)S(1)}, bf16[24,16,128]{2,1,0:T(8,128)(2,1)S(1)}, u32[]{:S(2)}, u32[]{:S(2)}) collective-permute-start(bf16[24,16,128]{2,1,0:T(8,128)(2,1)S(1)} %get-tuple-element.28), channel_id=1, source_target_pairs={{0,192},{64,0},{128,64},{192,128},{1,193},{65,1},{129,65},{193,129... | collective-permute-start | bytes 294920 | tf_op jit(solution)/shard_map/ppermute | solution.py:378
  20.1 4.3 %copy-start = (bf16[8,64,128]{2,1,0:T(8,128)(2,1)S(1)}, bf16[8,64,128]{2,1,0:T(8,128)(2,1)}, u32[]{:S(2)}) copy-start(bf16[8,64,128]{2,1,0:T(8,128)(2,1)} %constant.8.clone.masks) | copy-start | bytes 393220
  20.1 4.3 %copy-start.1 = (bf16[256,256]{1,0:T(8,128)(2,1)S(1)}, bf16[256,256]{1,0:T(8,128)(2,1)}, u32[]{:S(2)}) copy-start(bf16[256,256]{1,0:T(8,128)(2,1)} %constant.7.clone.stream) | copy-start | bytes 393220
  20.1 4.3 %copy-start.2 = (bf16[128,96]{1,0:T(8,128)(2,1)S(1)}, bf16[128,96]{1,0:T(8,128)(2,1)}, u32[]{:S(2)}) copy-start(bf16[128,96]{1,0:T(8,128)(2,1)} %constant.6.clone.span) | copy-start | bytes 73732
  34.6 6.3 %collective-permute-start.6 = (f32[64,128]{1,0:T(8,128)S(1)}, f32[64,128]{1,0:T(8,128)S(1)}, u32[]{:S(2)}, u32[]{:S(2)}) collective-permute-start(f32[64,128]{1,0:T(8,128)S(1)} %get-tuple-element.35), channel_id=1, source_target_pairs={{0,1},{1,0},{2,3},{3,2},{4,5},{5,4},{6,7},{7,6},{8,9},{9,8},{10,11... | collective-permute-start | bytes 98312 | tf_op jit(solution)/shard_map/ppermute | solution.py:392
  40.9 3.3 %collective-permute-start.7 = (f32[64,128]{1,0:T(8,128)S(1)}, f32[64,128]{1,0:T(8,128)S(1)}, u32[]{:S(2)}, u32[]{:S(2)}) collective-permute-start(f32[64,128]{1,0:T(8,128)S(1)} %add.24), channel_id=1, source_target_pairs={{0,65},{1,64},{64,1},{65,0},{128,193},{129,192},{192,129},{193,128... | collective-permute-start | bytes 98312 | tf_op jit(solution)/shard_map/ppermute | solution.py:388
  44.3 4.6 %collective-permute-start.8 = (f32[64,128]{1,0:T(8,128)S(1)}, f32[64,128]{1,0:T(8,128)S(1)}, u32[]{:S(2)}, u32[]{:S(2)}) collective-permute-start(f32[64,128]{1,0:T(8,128)S(1)} %add.25), channel_id=1, source_target_pairs={{0,193},{1,192},{64,129},{65,128},{128,65},{129,64},{192,1},{193,0... | collective-permute-start | bytes 98312 | tf_op jit(solution)/shard_map/ppermute | solution.py:388
  48.8 3.3 %collective-permute-start.9 = (f32[64,128]{1,0:T(8,128)S(1)}, f32[64,128]{1,0:T(8,128)S(1)}, u32[]{:S(2)}, u32[]{:S(2)}) collective-permute-start(f32[64,128]{1,0:T(8,128)S(1)} %add.26), channel_id=1, source_target_pairs={{0,17},{1,16},{16,1},{17,0},{32,49},{33,48},{48,33},{49,32},{2,19}... | collective-permute-start | bytes 98312 | tf_op jit(solution)/shard_map/ppermute | solution.py:388
  52.2 4.6 %collective-permute-start.10 = (f32[64,128]{1,0:T(8,128)S(1)}, f32[64,128]{1,0:T(8,128)S(1)}, u32[]{:S(2)}, u32[]{:S(2)}) collective-permute-start(f32[64,128]{1,0:T(8,128)S(1)} %add.27), channel_id=1, source_target_pairs={{0,49},{1,48},{16,33},{17,32},{32,17},{33,16},{48,1},{49,0},{2,51}... | collective-permute-start | bytes 98312 | tf_op jit(solution)/shard_map/ppermute | solution.py:388
  56.7 3.3 %collective-permute-start.11 = (f32[64,128]{1,0:T(8,128)S(1)}, f32[64,128]{1,0:T(8,128)S(1)}, u32[]{:S(2)}, u32[]{:S(2)}) collective-permute-start(f32[64,128]{1,0:T(8,128)S(1)} %add.28), channel_id=1, source_target_pairs={{0,3},{1,2},{2,1},{3,0},{4,7},{5,6},{6,5},{7,4},{8,11},{9,10},{10,... | collective-permute-start | bytes 98312 | tf_op jit(solution)/shard_map/ppermute | solution.py:388
  60.1 4.8 %collective-permute-start.12 = (f32[64,128]{1,0:T(8,128)S(1)}, f32[64,128]{1,0:T(8,128)S(1)}, u32[]{:S(2)}, u32[]{:S(2)}) collective-permute-start(f32[64,128]{1,0:T(8,128)S(1)} %add.29), channel_id=1, source_target_pairs={{0,5},{1,4},{2,7},{3,6},{4,1},{5,0},{6,3},{7,2},{8,13},{9,12},{10,... | collective-permute-start | bytes 98312 | tf_op jit(solution)/shard_map/ppermute | solution.py:388
  64.9 5.5 %collective-permute-start.13 = (f32[64,128]{1,0:T(8,128)S(1)}, f32[64,128]{1,0:T(8,128)S(1)}, u32[]{:S(2)}, u32[]{:S(2)}) collective-permute-start(f32[64,128]{1,0:T(8,128)S(1)} %add.30), channel_id=1, source_target_pairs={{0,13},{1,12},{2,15},{3,14},{4,9},{5,8},{6,11},{7,10},{8,5},{9,4},... | collective-permute-start | bytes 98312 | tf_op jit(solution)/shard_map/ppermute | solution.py:388
  70.4 1.3 %collective-permute-start.14 = (f32[64,128]{1,0:T(8,128)S(1)}, f32[64,128]{1,0:T(8,128)S(1)}, u32[]{:S(2)}, u32[]{:S(2)}) collective-permute-start(f32[64,128]{1,0:T(8,128)S(1)} %add.31.mine), channel_id=1, source_target_pairs={{0,1},{1,0},{2,3},{3,2},{4,5},{5,4},{6,7},{7,6},{8,9},{9,8},{10,11... | collective-permute-start | bytes 98312 | tf_op jit(solution)/shard_map/ppermute | solution.py:392
